TPU v7x, 32 devices: a whole 2x2x4 slice. The times are simulated.
32 devices in a mesh: dp: 4 (over y, core), ctx: 4 (over z), tp: 2 (over x).
Axes of the slice: x: 2, y: 2, z: 4, core: 2. Of those that a mesh axis runs over, the one named last changes fastest.
Arguments:
- block_input: bfloat16 [8, 2048, 896], P('dp', 'ctx'), may hold values from -6 to 6
- positions: int32 [8, 2048], P('dp', 'ctx'), may hold values from 0 to 1535, as said below
- gain_attn: float32 [896], replicated, may hold values from 0.25 to 1.75
- w_qkv: bfloat16 [896, 2, 576], P(None, 'tp'), may hold values from -0.2893103 to 0.2893103, as said below
- b_qkv: float32 [2, 576], P('tp'), may hold values from -3 to 3
- w_out: bfloat16 [2, 448, 896], P('tp'), may hold values from -3 to 3
- gain_mlp: float32 [896], replicated, may hold values from 0.25 to 1.75
- w_gate: bfloat16 [896, 4864], P(None, 'tp'), may hold values from -0.1875 to 0.1875
- w_up: bfloat16 [896, 4864], P(None, 'tp'), may hold values from -0.1875 to 0.1875
- w_down: bfloat16 [4864, 896], P('tp'), may hold values from -0.625 to 0.625
- cotangent: bfloat16 [8, 2048, 896], P('dp', 'ctx'), may hold values from -6 to 6
Outputs:
- output: bfloat16 [8, 2048, 896], P('dp', 'ctx')
- grad_input: float32 [8, 2048, 896], P('dp', 'ctx')
- grad_gain_attn: float32 [896], P('dp')
- grad_qkv: float32 [896, 2, 576], P('dp', 'tp')
- grad_bias: float32 [2, 576], P('tp', 'dp')
- grad_out: float32 [2, 448, 896], P('tp', None, 'dp')
- grad_gain_mlp: float32 [896], P('dp')
- grad_gate: float32 [896, 4864], P('dp', 'tp')
- grad_up: float32 [896, 4864], P('dp', 'tp')
- grad_down: float32 [4864, 896], P('tp', 'dp')
Inputs may be any that keep to these rules, and one draw needn't show every extreme that they name: Each sequence holds two documents; the second starts at an index between 512 and 1536 drawn per sequence, in the first sequence exactly at 512; the position restarts at 0 there, and within a document positions count up by one. `w_qkv`: independent entries.
All inputs are finite; a program needn't handle non-finite values.
Results may differ from a plain program's by a relative error of at most 0.03.
The roundings to bfloat16 on the way count: a program that leaves them out, or rounds other values in their place, can miss the bound.
Values may be sent and summed in bfloat16 or wider, within the bound.
A program may use at most 256 MiB of HBM per device.

v0:
```python
import math

import jax
import jax.numpy as jnp
from jax import lax
from jax.sharding import PartitionSpec as P

HD = 64


EPS = 1e-06
THETA = 1000000.0
SCALE = 0.125
NEGATIVE = -1e30


def inverse_rms(values):
    return lax.rsqrt(jnp.mean(values * values, axis=-1, keepdims=True) + EPS)


def rotary(positions, width):
    half = width // 2
    freq = THETA ** (-(jnp.arange(half, dtype=jnp.float32) * 2.0) / width)
    angle = positions.astype(jnp.float32)[..., None] * freq
    return (jnp.cos(angle), jnp.sin(angle))


def rotate(values, cosine, sine):
    half = values.shape[-1] // 2
    first, second = (values[..., :half], values[..., half:])
    return jnp.concatenate(
        [first * cosine - second * sine, second * cosine + first * sine], axis=-1
    )


def unrotate(grads, cosine, sine):
    half = grads.shape[-1] // 2
    first, second = (grads[..., :half], grads[..., half:])
    return jnp.concatenate(
        [first * cosine + second * sine, second * cosine - first * sine], axis=-1
    )


def norm_back(grad_h, normed, scale, gain):
    upstream = grad_h * gain
    inner = jnp.mean(upstream * normed, axis=-1, keepdims=True)
    return scale * (upstream - normed * inner)


def shards(
    block_input,
    positions,
    gain_attn,
    w_qkv,
    b_qkv,
    w_out,
    gain_mlp,
    w_gate,
    w_up,
    w_down,
    cotangent,
):
    seqs, tokens, _ = block_input.shape
    heads_width = w_out.shape[1]
    head = HD
    group = heads_width // head
    rows = tokens * group
    first_token = lax.axis_index("ctx") * tokens
    seq_tokens = tokens * lax.axis_size("ctx")
    proj_qkv = w_qkv[:, 0, :]
    proj_out = w_out[0]
    inputs = block_input.astype(jnp.float32)
    scale_one = inverse_rms(inputs)
    normed_one = inputs * scale_one
    hidden_one = (normed_one * gain_attn).astype(jnp.bfloat16)
    joined = (
        jnp.einsum("std,de->ste", hidden_one, proj_qkv, preferred_element_type=jnp.float32)
        + b_qkv[0]
    )
    cosine, sine = rotary(positions, head)
    queries = rotate(
        joined[..., :heads_width].reshape(seqs, tokens, group, head),
        cosine[:, :, None, :],
        sine[:, :, None, :],
    )
    queries = queries.astype(jnp.bfloat16).reshape(seqs, rows, head)
    keys = rotate(joined[..., heads_width : heads_width + head], cosine, sine)
    key_value = jnp.concatenate([keys, joined[..., heads_width + head :]], axis=-1).astype(
        jnp.bfloat16
    )
    token_index = first_token + jnp.arange(tokens, dtype=jnp.int32)
    query_index = jnp.repeat(token_index, group)
    query_first = jnp.repeat(token_index[None, :] - positions, group, axis=1)
    query_last = first_token + tokens - 1

    def block_scores(key_block, key_start):
        scores = (
            jnp.einsum(
                "srd,skd->srk", queries, key_block[..., :head], preferred_element_type=jnp.float32
            )
            * SCALE
        )
        key_index = key_start + jnp.arange(key_block.shape[1], dtype=jnp.int32)
        allowed = (key_index[None, None, :] <= query_index[None, :, None]) & (
            key_index[None, None, :] >= query_first[:, :, None]
        )
        return (scores, allowed)

    def over_blocks(step_fn, carry, piece):
        size = math.gcd(piece.shape[1], 512)
        count = piece.shape[1] // size

        def one_block(turn, state):
            offset = turn * size
            key_block = lax.dynamic_slice_in_dim(piece, offset, size, 1)
            return lax.cond(
                offset <= query_last,
                lambda inner: step_fn(inner, key_block, offset),
                lambda inner: inner,
                state,
            )

        return lax.fori_loop(0, count, one_block, carry)

    def forward_step(state, key_block, key_start):
        top, total, accum = state
        scores, allowed = block_scores(key_block, key_start)
        new_top = jnp.maximum(top, jnp.max(jnp.where(allowed, scores, NEGATIVE), axis=-1))
        weights = jnp.where(allowed, jnp.exp(scores - new_top[..., None]), 0.0)
        factor = jnp.exp(top - new_top)
        total = total * factor + jnp.sum(weights, axis=-1)
        accum = accum * factor[..., None] + jnp.einsum(
            "srk,skd->srd",
            weights.astype(jnp.bfloat16),
            key_block[..., head:],
            preferred_element_type=jnp.float32,
        )
        return (new_top, total, accum)

    start_state = (
        jnp.full((seqs, rows), NEGATIVE, jnp.float32),
        jnp.zeros((seqs, rows), jnp.float32),
        jnp.zeros((seqs, rows, head), jnp.float32),
    )
    top, total, accum = over_blocks(
        forward_step, start_state, lax.all_gather(key_value, "ctx", axis=1, tiled=True)
    )
    log_total = top + jnp.log(total)
    attended = (accum / total[..., None]).astype(jnp.bfloat16)
    attended_flat = attended.reshape(seqs, tokens, heads_width)
    attn_part = jnp.einsum(
        "ste,ed->std", attended_flat, proj_out, preferred_element_type=jnp.float32
    )
    middle = inputs + lax.psum(attn_part, "tp")
    scale_two = inverse_rms(middle)
    normed_two = middle * scale_two
    hidden_two = (normed_two * gain_mlp).astype(jnp.bfloat16)
    gate = jnp.einsum("std,df->stf", hidden_two, w_gate, preferred_element_type=jnp.float32)
    up = jnp.einsum("std,df->stf", hidden_two, w_up, preferred_element_type=jnp.float32)
    sigma = jax.nn.sigmoid(gate)
    activated = (gate * sigma * up).astype(jnp.bfloat16)
    mlp_part = jnp.einsum("stf,fd->std", activated, w_down, preferred_element_type=jnp.float32)
    output = (middle + lax.psum(mlp_part, "tp")).astype(jnp.bfloat16)
    grad_act = jnp.einsum("std,fd->stf", cotangent, w_down, preferred_element_type=jnp.float32)
    grad_down = jnp.einsum("stf,std->fd", activated, cotangent, preferred_element_type=jnp.float32)
    grad_gate_in = (grad_act * up * sigma * (1.0 + gate * (1.0 - sigma))).astype(jnp.bfloat16)
    grad_up_in = (grad_act * gate * sigma).astype(jnp.bfloat16)
    grad_gate = jnp.einsum(
        "std,stf->df", hidden_two, grad_gate_in, preferred_element_type=jnp.float32
    )
    grad_up = jnp.einsum("std,stf->df", hidden_two, grad_up_in, preferred_element_type=jnp.float32)
    back_two = jnp.einsum("stf,df->std", grad_gate_in, w_gate, preferred_element_type=jnp.float32)
    back_two = back_two + jnp.einsum(
        "stf,df->std", grad_up_in, w_up, preferred_element_type=jnp.float32
    )
    back_two = lax.psum(back_two, "tp")
    grad_gain_mlp = jnp.sum(back_two * normed_two, axis=(0, 1))
    grad_middle = cotangent.astype(jnp.float32) + norm_back(
        back_two, normed_two, scale_two, gain_mlp
    )
    grad_middle_b = grad_middle.astype(jnp.bfloat16)
    grad_out = jnp.einsum(
        "ste,std->ed", attended_flat, grad_middle_b, preferred_element_type=jnp.float32
    )[None]
    grad_attended = jnp.einsum(
        "std,ed->ste", grad_middle_b, proj_out, preferred_element_type=jnp.float32
    )
    grad_attended = grad_attended.astype(jnp.bfloat16).reshape(seqs, rows, head)
    row_terms = jnp.einsum(
        "srd,srd->sr", grad_attended, attended, preferred_element_type=jnp.float32
    )

    def backward_step(state, key_block, key_start):
        grad_queries, grad_keys = state
        scores, allowed = block_scores(key_block, key_start)
        probs = jnp.where(allowed, jnp.exp(scores - log_total[..., None]), 0.0)
        grad_probs = jnp.einsum(
            "srd,skd->srk", grad_attended, key_block[..., head:], preferred_element_type=jnp.float32
        )
        grad_scores = (probs * (grad_probs - row_terms[..., None])).astype(jnp.bfloat16)
        grad_queries = (
            grad_queries
            + jnp.einsum(
                "srk,skd->srd",
                grad_scores,
                key_block[..., :head],
                preferred_element_type=jnp.float32,
            )
            * SCALE
        )
        grad_key = (
            jnp.einsum("srk,srd->skd", grad_scores, queries, preferred_element_type=jnp.float32)
            * SCALE
        )
        grad_value = jnp.einsum(
            "srk,srd->skd",
            probs.astype(jnp.bfloat16),
            grad_attended,
            preferred_element_type=jnp.float32,
        )
        current = lax.dynamic_slice_in_dim(grad_keys, key_start, key_block.shape[1], 1)
        grad_keys = lax.dynamic_update_slice_in_dim(
            grad_keys, current + jnp.concatenate([grad_key, grad_value], axis=-1), key_start, 1
        )
        return (grad_queries, grad_keys)

    back_state = (
        jnp.zeros((seqs, rows, head), jnp.float32),
        jnp.zeros((seqs, seq_tokens, 2 * head), jnp.float32),
    )
    grad_queries, grad_keys = over_blocks(
        backward_step, back_state, lax.all_gather(key_value, "ctx", axis=1, tiled=True)
    )
    grad_pairs = lax.psum_scatter(grad_keys, "ctx", scatter_dimension=1, tiled=True)
    grad_q = unrotate(
        grad_queries.reshape(seqs, tokens, group, head), cosine[:, :, None, :], sine[:, :, None, :]
    )
    grad_k = unrotate(grad_pairs[..., :head], cosine, sine)
    grad_joined = jnp.concatenate(
        [grad_q.reshape(seqs, tokens, heads_width), grad_k, grad_pairs[..., head:]], axis=-1
    )
    grad_bias = jnp.sum(grad_joined, axis=(0, 1))[None]
    grad_joined_b = grad_joined.astype(jnp.bfloat16)
    grad_qkv = jnp.einsum(
        "std,ste->de", hidden_one, grad_joined_b, preferred_element_type=jnp.float32
    )[:, None, :]
    back_one = jnp.einsum(
        "ste,de->std", grad_joined_b, proj_qkv, preferred_element_type=jnp.float32
    )
    back_one = lax.psum(back_one, "tp")
    grad_gain_attn = jnp.sum(back_one * normed_one, axis=(0, 1))
    grad_input = grad_middle + norm_back(back_one, normed_one, scale_one, gain_attn)
    shares = (
        lax.psum_scatter(grad_gain_attn, ("dp", "ctx"), scatter_dimension=0, tiled=True),
        lax.psum_scatter(grad_qkv, ("dp", "ctx"), scatter_dimension=0, tiled=True),
        lax.psum_scatter(grad_bias, ("dp", "ctx"), scatter_dimension=1, tiled=True),
        lax.psum_scatter(grad_out, ("dp", "ctx"), scatter_dimension=2, tiled=True),
        lax.psum_scatter(grad_gain_mlp, ("dp", "ctx"), scatter_dimension=0, tiled=True),
        lax.psum_scatter(grad_gate, ("dp", "ctx"), scatter_dimension=0, tiled=True),
        lax.psum_scatter(grad_up, ("dp", "ctx"), scatter_dimension=0, tiled=True),
        lax.psum_scatter(grad_down, ("dp", "ctx"), scatter_dimension=1, tiled=True),
    )
    reduced = (
        lax.all_gather(shares[0], "ctx", axis=0, tiled=True),
        lax.all_gather(shares[1], "ctx", axis=0, tiled=True),
        lax.all_gather(shares[2], "ctx", axis=1, tiled=True),
        lax.all_gather(shares[3], "ctx", axis=2, tiled=True),
        lax.all_gather(shares[4], "ctx", axis=0, tiled=True),
        lax.all_gather(shares[5], "ctx", axis=0, tiled=True),
        lax.all_gather(shares[6], "ctx", axis=0, tiled=True),
        lax.all_gather(shares[7], "ctx", axis=1, tiled=True),
    )
    return (
        output,
        grad_input,
        reduced[0],
        reduced[1],
        reduced[2],
        reduced[3],
        reduced[4],
        reduced[5],
        reduced[6],
        reduced[7],
    )


def solution(mesh):
    in_specs = (
        P("dp", "ctx", None),
        P("dp", "ctx"),
        P(),
        P(None, "tp", None),
        P("tp", None),
        P("tp", None, None),
        P(),
        P(None, "tp"),
        P(None, "tp"),
        P("tp", None),
        P("dp", "ctx", None),
    )
    out_specs = (
        P("dp", "ctx", None),
        P("dp", "ctx", None),
        P("dp"),
        P("dp", "tp", None),
        P("tp", "dp"),
        P("tp", None, "dp"),
        P("dp"),
        P("dp", "tp"),
        P("dp", "tp"),
        P("tp", "dp"),
    )
    return jax.shard_map(shards, mesh=mesh, in_specs=in_specs, out_specs=out_specs, check_vma=False)
```

profile of v0, /device:TPU:0, one launch (start us, length us, event | category | flops | bytes accessed | tf_op | source)
XLA Modules:
  0.0 1396.2 jit_solution(7556306745647094987)
XLA Ops:
  48.7 23.5 %while.34 = (s32[]{:T(128)}, f32[2,3584]{1,0:T(2,128)S(1)}, f32[2,3584]{1,0:T(2,128)S(1)}, f32[2,3584,64]{1,2,0:T(8,128)}, s32[]{:T(128)}, /*index=5*/bf16[2,204...) while((s32[]{:T(128)}, f32[2,3584]{1,0:T(2,128)S(1)}, ...), condition=%wide.region_6.7_spmd.clone, body=%wide.region_1.6_spmd.clone.sunk | while | flops 1004681728 | bytes 115655000 | solution.py:123
  49.1 23.1 %conditional.6 = ((f32[2,3584]{1,0:T(2,128)S(1)}, f32[2,3584]{1,0:T(2,128)S(1)}, f32[2,3584,64]{1,2,0:T(8,128)})) conditional(s32[]{:T(128)} %convert_element_type.144, (f32[2,3584]{1,0:T(2,128)S(1)}, f32[2,3584]{1,0:T(2,128)S(1)}, f32[2,3584,64]{1,2,0:T(8,128)}) %tuple.118, (s32[]{:T(128)}, s32[512]{0:T(512)S(1)}, s32[2,512]{1,0:T(2,128)S(1)}, ...), branch_computations={%region_2.0_spmd, %region_3.5_spmd} | conditional | flops 1004681728 | bytes 115654776 | solution.py:116
  83.2 11.2 fusion.44
  94.3 156.8 %all-reduce.20.cloned.1.call-done = f32[2,512,896]{2,1,0:T(8,128)} async-done(((f32[2,512,896]{2,1,0:T(8,128)}), f32[2,512,896]{2,1,0:T(8,128)}) %all-reduce.20.cloned.1.call-update) | async-done | bytes 3670032 | tf_op jit(solution)/shard_map/psum | solution.py:154
  256.0 10.8 fusion.50
  266.9 16.8 %multiply_convert_fusion.1 = (bf16[2,512,2432]{2,1,0:T(8,128)(2,1)}, bf16[2,512,2432]{2,1,0:T(8,128)(2,1)}, bf16[2,512,2432]{2,1,0:T(8,128)(2,1)}) fusion(f32[2,512,2432]{2,1,0:T(8,128)} %fusion.44, f32[2,512,2432]{2,1,0:T(8,128)} %fusion.50, bf16[2,512,896]{2,1,0:T(8,128)(2,1)S(1)} %multiply_convert_fusion.3, bf16[896,2432]{1,0:T(8,128)(2,1)} %param.26), kind=kOutput, calls=%fused_computation.47 | convolution fusion | flops 4502585344 | bytes 41058304 | tf_op jit(solution)/shard_map/std,df->stf/dot_general | solution.py:158
  301.8 96.7 %all-reduce.22.cloned.1.call-done = f32[2,512,896]{2,1,0:T(8,128)} async-done(((f32[2,512,896]{2,1,0:T(8,128)}), f32[2,512,896]{2,1,0:T(8,128)}) %all-reduce.22.cloned.1.call-update) | async-done | bytes 3670032 | tf_op jit(solution)/shard_map/psum | solution.py:176
  419.2 37.3 %while.35 = (s32[]{:T(128)}, f32[2,3584,64]{1,2,0:T(8,128)S(1)}, f32[2,2048,128]{1,2,0:T(8,128)}, s32[]{:T(128)}, bf16[2,2048,128]{1,2,0:T(8,128)(2,1)}, /*index...) while((s32[]{:T(128)}, f32[2,3584,64]{1,2,0:T(8,128)S(1)}, ...), condition=%wide.region_15.0_spmd.clone, body=%wide.region_12.15_spmd.clone.sunk | while | flops 2403271168 | bytes 96377264 | solution.py:123
  419.4 36.9 %conditional.7 = ((f32[2,3584,64]{1,2,0:T(8,128)S(1)}, f32[2,2048,128]{1,2,0:T(8,128)})) conditional(s32[]{:T(128)} %convert_element_type.145, (f32[2,3584,64]{1,2,0:T(8,128)S(1)}, f32[2,2048,128]{1,2,0:T(8,128)}) %tuple.121, (s32[]{:T(128)}, s32[512]{0:T(512)S(1)}, s32[2,512]{1,0:T(2,128)S(1)}, bf16[2,2048,128]{1,2,0:T(8,128)(2,1)}, ...), branch_computations={%region_13.13_spmd, %region_14.14_spmd} | conditional | flops 2403271168 | bytes 96377016 | solution.py:116
  457.0 11.3 convolution_bitcast_fusion.2
  468.4 11.3 convolution_bitcast_fusion.1
  480.0 11.4 convolution_bitcast_fusion
  523.9 87.1 %reduce-scatter.12.cloned.1.call-done = f32[2,512,128]{1,2,0:T(8,128)} async-done(((f32[2,2048,128]{1,2,0:T(8,128)}), f32[2,512,128]{1,2,0:T(8,128)}) %reduce-scatter.12.cloned.1.call-update) | async-done | bytes 524304 | tf_op jit(solution)/shard_map/reduce_scatter | solution.py:234
  623.9 10.7 fusion.46
  638.4 84.3 %reduce-scatter.14.cloned.1.call-done = f32[56,2432]{1,0:T(8,128)} async-done(((f32[896,2432]{1,0:T(8,128)}), f32[56,2432]{1,0:T(8,128)}) %reduce-scatter.14.cloned.1.call-update) | async-done | bytes 544784
  722.8 111.6 %reduce-scatter.16.cloned.1.call-done = f32[56,2432]{1,0:T(8,128)} async-done(((f32[896,2432]{1,0:T(8,128)}), f32[56,2432]{1,0:T(8,128)}) %reduce-scatter.16.cloned.1.call-update) | async-done | bytes 544784
  834.5 111.8 %reduce-scatter.18.cloned.1.call-done = f32[2432,56]{0,1:T(8,128)} async-done(((f32[2432,896]{0,1:T(8,128)}), f32[2432,56]{0,1:T(8,128)}) %reduce-scatter.18.cloned.1.call-update) | async-done | bytes 544784
  951.8 108.4 %all-reduce.24.cloned.1.call-done = (f32[896,1,576]{2,1,0:T(1,128)}, f32[1,448,896]{1,0,2:T(1,128)}) async-done(((f32[896,1,576]{2,1,0:T(1,128)}, f32[1,448,896]{1,0,2:T(1,128)}), (f32[896,1,576]{2,1,0:T(1,128)}, f32[1,448,896]{1,0,2:T(1,128)})) %all-reduce.24.cloned.1.call-update) | async-done | bytes 3670032
  1061.2 16.2 %all_gather.30 = f32[224,1,576]{2,1,0:T(1,128)S(1)} all-gather(f32[56,1,576]{2,1,0:T(1,128)S(1)} %constant_dynamic-slice_fusion.2), channel_id=1, replica_groups=mesh['dp'=4,'ctx'=4,'tp'=2] {'ctx'}, dimensions={0}, use_global_device_ids=true | all-gather | bytes 645120 | tf_op jit(solution)/shard_map/all_gather | solution.py:265
  1078.3 15.2 %all_gather.32 = f32[1,448,224]{1,0,2:T(1,128)} all-gather(f32[1,448,56]{1,0,2:T(1,128)S(1)} %constant_dynamic-slice_fusion), channel_id=1, replica_groups=mesh['dp'=4,'ctx'=4,'tp'=2] {'ctx'}, dimensions={2}, use_global_device_ids=true | all-gather | bytes 501760 | tf_op jit(solution)/shard_map/all_gather | solution.py:267
  1095.5 141.9 %all-reduce.26.cloned.1.call-done = (f32[2,512,896]{2,1,0:T(8,128)}, f32[2,512,896]{2,1,0:T(8,128)}) async-done(((f32[2,512,896]{2,1,0:T(8,128)}, f32[2,512,896]{2,1,0:T(8,128)}), (f32[2,512,896]{2,1,0:T(8,128)}, f32[2,512,896]{2,1,0:T(8,128)})) %all-reduce.26.cloned.1.call-update) | async-done | bytes 7340048 | tf_op jit(solution)/shard_map/psum | solution.py:163
  1240.5 64.6 %all-reduce.11 = (f32[896]{0:T(1024)S(1)}, f32[1,576]{1,0:T(1,128)S(1)}, f32[896]{0:T(1024)S(1)}) all-reduce(f32[896]{0:T(1024)S(1)} %get-tuple-element.682, f32[1,576]{1,0:T(1,128)S(1)} %broadcast_in_dim.70, f32[896]{0:T(1024)S(1)} %copy-done.29), channel_id=3, replica_groups=mesh['dp'=4,'ctx'=4,'tp'=2] {'dp','ctx'}, use_global_device_ids=true, to_apply=%region_20.21.clone | all-reduce | flops 2368 | bytes 18944
  1323.6 11.6 all-gather.9.cloned.1.call-done
  1335.2 47.2 %all-gather.11.cloned.1.call-done = f32[2432,224]{0,1:T(8,128)} async-done(((f32[2432,56]{0,1:T(8,128)}), f32[2432,224]{0,1:T(8,128)}) %all-gather.11.cloned.1.call-update) | async-done | bytes 2179088 | tf_op jit(solution)/shard_map/all_gather | solution.py:271
  (210 shorter events, 240.7 us)
Async XLA Ops:
  7.2 40.1 %all-gather.5.cloned.1.call-start = ((), (), s32[]{:S(2)}) async-start(), calls=%async_computation.4 | async-start | bytes 1310720 | tf_op jit(solution)/shard_map/all_gather | solution.py:146
  16.4 234.7 %all-reduce.20.cloned.1.call-start = ((), (), s32[]{:S(2)}) async-start(), calls=%async_computation.5 | async-start | bytes 7340032 | tf_op jit(solution)/shard_map/psum | solution.py:154
  83.1 168.1 %copy-start.7 = (bf16[2,512,896]{2,1,0:T(8,128)(2,1)S(1)}, bf16[2,512,896]{2,1,0:T(8,128)(2,1)}, u32[]{:S(2)}) copy-start(bf16[2,512,896]{2,1,0:T(8,128)(2,1)} %param.19) | copy-start | bytes 5505028
  83.1 315.4 %all-reduce.22.cloned.1.call-start = ((), (), s32[]{:S(2)}) async-start(), calls=%async_computation.6 | async-start | bytes 7340032 | tf_op jit(solution)/shard_map/psum | solution.py:176
  94.3 161.2 %copy-start.23 = (f32[896]{0:T(1024)S(1)}, f32[896]{0:T(1024)}, u32[]{:S(2)}) copy-start(f32[896]{0:T(1024)} %param.25) | copy-start | bytes 10756
  256.0 27.6 %slice-start = ((s8[4358144]{0:T(1024)(128)(4,1)}), s8[4194304]{0:T(1024)(128)(4,1)S(1)}, s32[]{:S(2)}) async-start(s8[4358144]{0:T(1024)(128)(4,1)} %bitcast.113), calls=%async_computation.16 | async-start | bytes 8388608
  301.0 102.3 %copy-start.20 = (bf16[2,512,896]{2,1,0:T(8,128)(2,1)S(1)}, bf16[2,512,896]{2,1,0:T(8,128)(2,1)}, u32[]{:S(2)}) copy-start(bf16[2,512,896]{2,1,0:T(8,128)(2,1)} %param.29) | copy-start | bytes 5505028
  301.1 309.9 %reduce-scatter.12.cloned.1.call-start = ((), (), s32[]{:S(2)}) async-start(), calls=%async_computation.7 | async-start | bytes 2621440 | tf_op jit(solution)/shard_map/reduce_scatter | solution.py:234
  456.5 266.2 %reduce-scatter.14.cloned.1.call-start = ((), (), s32[]{:S(2)}) async-start(), calls=%async_computation.11 | async-start | bytes 9261056
  468.4 366.0 %reduce-scatter.16.cloned.1.call-start = ((), (), s32[]{:S(2)}) async-start(), calls=%async_computation.12 | async-start | bytes 9261056
  479.8 466.5 %reduce-scatter.18.cloned.1.call-start = ((), (), s32[]{:S(2)}) async-start(), calls=%async_computation.13 | async-start | bytes 9261056
  491.4 568.8 %all-reduce.24.cloned.1.call-start = ((), (), s32[]{:S(2)}) async-start(), calls=%async_computation.14 | async-start | bytes 8257536
  518.3 93.7 %copy-start.25 = (f32[2,512]{1,0:T(2,128)S(1)}, f32[2,512]{1,0:T(2,128)}, u32[]{:S(2)}) copy-start(f32[2,512]{1,0:T(2,128)} %copy-done.24) | copy-start | bytes 12292
  518.3 93.7 %copy-start.33 = (f32[32]{0:T(128)S(1)}, f32[32]{0:T(128)}, u32[]{:S(2)}) copy-start(f32[32]{0:T(128)} %copy-done.32) | copy-start | bytes 388
  518.3 95.2 %copy-start.8 = (bf16[2,512,896]{2,1,0:T(8,128)(2,1)S(1)}, bf16[2,512,896]{2,1,0:T(8,128)(2,1)}, u32[]{:S(2)}) copy-start(bf16[2,512,896]{2,1,0:T(8,128)(2,1)} %param.19) | copy-start | bytes 5505028
  518.3 95.2 %copy-start.27 = (f32[2,512]{1,0:T(2,128)S(1)}, f32[2,512]{1,0:T(2,128)}, u32[]{:S(2)}) copy-start(f32[2,512]{1,0:T(2,128)} %copy-done.26) | copy-start | bytes 12292
  518.3 95.3 %copy-start.30 = (f32[896]{0:T(1024)S(1)}, f32[896]{0:T(1024)}, u32[]{:S(2)}) copy-start(f32[896]{0:T(1024)} %param.21) | copy-start | bytes 10756
  623.7 613.7 %all-reduce.26.cloned.1.call-start = ((), (), s32[]{:S(2)}) async-start(), calls=%async_computation.15 | async-start | bytes 14680064 | tf_op jit(solution)/shard_map/psum | solution.py:163
  638.3 308.0 %copy-start.35 = (u32[32]{0:T(128)S(1)}, u32[32]{0:T(128)}, u32[]{:S(2)}) copy-start(u32[32]{0:T(128)} %constant.148) | copy-start | bytes 388
  638.3 309.9 %copy-start.34 = (u32[32]{0:T(128)S(1)}, u32[32]{0:T(128)}, u32[]{:S(2)}) copy-start(u32[32]{0:T(128)} %constant.167) | copy-start | bytes 388
  638.4 685.2 %all-gather.7.cloned.1.call-start = ((), (), s32[]{:S(2)}) async-start(), calls=%async_computation.8 | async-start | bytes 2723840 | tf_op jit(solution)/shard_map/all_gather | solution.py:269
  722.7 612.4 %all-gather.9.cloned.1.call-start = ((), (), s32[]{:S(2)}) async-start(), calls=%async_computation.9 | async-start | bytes 2723840 | tf_op jit(solution)/shard_map/all_gather | solution.py:270
  834.4 547.9 %all-gather.11.cloned.1.call-start = ((), (), s32[]{:S(2)}) async-start(), calls=%async_computation.10 | async-start | bytes 2723840 | tf_op jit(solution)/shard_map/all_gather | solution.py:271
  1077.4 163.0 %copy-start.29 = (f32[896]{0:T(1024)S(1)}, f32[896]{0:T(1024)}, u32[]{:S(2)}) copy-start(f32[896]{0:T(1024)} %get-tuple-element.680) | copy-start | bytes 10756
  (27 other events, 152.0 us)
Sparse Core Ops, SparseCore 0:
  16.6 30.6 all-gather.4
  83.2 167.9 all-reduce.19
  301.2 97.2 all-reduce.21
  456.7 154.2 reduce-scatter.11
  614.8 107.8 reduce-scatter.13
  726.6 107.7 reduce-scatter.15
  838.4 107.8 reduce-scatter.17
  950.5 109.6 all-reduce.23
  1062.7 174.5 all-reduce.25
  1238.8 48.8 all-gather.6
  1289.2 45.9 all-gather.8
  1336.6 45.7 all-gather.10
where the time goes:
time: 1400 us
  waiting for transfers between devices  959 us (68%)
  matrix products  169 us (12%)
  blocking collectives  106 us (8%)
  local copies, waits for them, and re-layouts  74.4 us (5%)
  other arithmetic  68.5 us (5%)
  between operations  17.6 us (1%)
    unnamed x16, waiting for transfers between devices  416 us
    psum x1, waiting for transfers between devices, shards(): middle = inputs + lax.psum(attn_part, 'tp')  157 us
    psum x1, waiting for transfers between devices, shards(): output = (middle + lax.psum(mlp_part, 'tp')).astype(jnp.bfloat16)  142 us
    psum x1, waiting for transfers between devices, shards(): back_two = lax.psum(back_two, 'tp')  96.7 us
    reduce_scatter x1, waiting for transfers between devices, shards(): lax.psum_scatter(grad_keys, 'ctx', scatter_dimension=1, tiled=True)  87.1 us
    unnamed x2, blocking collectives  74.1 us
    all_gather x1, waiting for transfers between devices, shards(): lax.all_gather(shares[7], 'ctx', axis=1, tiled=True)  47.2 us
    unnamed x90, local copies, waits for them, and re-layouts  34.2 us
  transfers between devices with their start and end apart: 12, of which 11 were waited for; matrix products, arithmetic and copies ran while one was open for 11% of the time, Pallas kernels for 0%

commit v1 on v0

--- a/solution.py
+++ b/solution.py
@@ -45,6 +45,78 @@
     upstream = grad_h * gain
     inner = jnp.mean(upstream * normed, axis=-1, keepdims=True)
     return scale * (upstream - normed * inner)
+
+
+def to_bf16(values):
+    return values.astype(jnp.bfloat16)
+
+
+def tp_other(values):
+    return lax.ppermute(values, "tp", [(0, 1), (1, 0)])
+
+
+def tp_sum(values):
+    mine = to_bf16(values)
+    return mine.astype(jnp.float32) + tp_other(mine).astype(jnp.float32)
+
+
+def core_other(values):
+    pairs = [(i, i ^ 1) for i in range(lax.axis_size("dp"))]
+    return lax.ppermute(values, "dp", pairs)
+
+
+def earlier(values, shift):
+    n = lax.axis_size("ctx")
+    return lax.ppermute(values, "ctx", [(i, i + shift) for i in range(n - shift)])
+
+
+def later(values, shift):
+    n = lax.axis_size("ctx")
+    return lax.ppermute(values, "ctx", [(i + shift, i) for i in range(n - shift)])
+
+
+def line_sum(part):
+    n = lax.axis_size("ctx")
+    half = n // 2
+    me = lax.axis_index("ctx")
+    for step in range(half - 1):
+        pairs = [(step, step + 1), (n - 1 - step, n - 2 - step)]
+        part = part + lax.ppermute(to_bf16(part), "ctx", pairs).astype(jnp.float32)
+    mine = to_bf16(part)
+    moved = lax.ppermute(mine, "ctx", [(half - 1, half), (half, half - 1)])
+    total = to_bf16(mine.astype(jnp.float32) + moved.astype(jnp.float32))
+    for step in reversed(range(half - 1)):
+        pairs = [(step + 1, step), (n - 2 - step, n - 1 - step)]
+        moved = lax.ppermute(total, "ctx", pairs)
+        total = jnp.where((me == step) | (me == n - 1 - step), moved, total)
+    return total.astype(jnp.float32)
+
+
+def quarter_grads(make, wide):
+    n_dp = lax.axis_size("dp")
+    rows = n_dp // 2
+    me = lax.axis_index("dp")
+    row, core = me // 2, me % 2
+    split = wide.reshape(wide.shape[0], rows, 2, wide.shape[1] // n_dp)
+    mine = lax.dynamic_index_in_dim(split, core, 2, keepdims=False)
+    theirs = core_other(lax.dynamic_index_in_dim(split, 1 - core, 2, keepdims=False))
+    both = jnp.concatenate([mine, theirs], axis=0)
+
+    def columns(which):
+        return lax.dynamic_index_in_dim(both, which, 1, keepdims=False)
+
+    total = None
+    for shift in range(1, rows):
+        part = to_bf16(make(columns((row + shift) % rows)))
+        pairs = [(r * 2 + c, ((r + shift) % rows) * 2 + c) for r in range(rows) for c in range(2)]
+        moved = lax.ppermute(part, "dp", pairs).astype(jnp.float32)
+        total = moved if total is None else total + moved
+    own = make(columns(row))
+    return own if total is None else own + total
+
+
+def both_cores(values):
+    return jnp.concatenate([values, core_other(values)], axis=0)
 
 
 def shards(
@@ -69,6 +141,8 @@
     seq_tokens = tokens * lax.axis_size("ctx")
     proj_qkv = w_qkv[:, 0, :]
     proj_out = w_out[0]
+    other_qkv = tp_other(proj_qkv)
+    other_out = tp_other(proj_out)
     inputs = block_input.astype(jnp.float32)
     scale_one = inverse_rms(inputs)
     normed_one = inputs * scale_one
@@ -88,6 +162,12 @@
     key_value = jnp.concatenate([keys, joined[..., heads_width + head :]], axis=-1).astype(
         jnp.bfloat16
     )
+    gathered = jnp.zeros((seqs, seq_tokens, 2 * head), jnp.bfloat16)
+    gathered = lax.dynamic_update_slice_in_dim(gathered, key_value, first_token, 1)
+    n_ctx = lax.axis_size("ctx")
+    for shift in range(1, n_ctx):
+        place = (lax.axis_index("ctx") - shift) % n_ctx * tokens
+        gathered = lax.dynamic_update_slice_in_dim(gathered, earlier(key_value, shift), place, 1)
     token_index = first_token + jnp.arange(tokens, dtype=jnp.int32)
     query_index = jnp.repeat(token_index, group)
     query_first = jnp.repeat(token_index[None, :] - positions, group, axis=1)
@@ -143,15 +223,18 @@
         jnp.zeros((seqs, rows, head), jnp.float32),
     )
     top, total, accum = over_blocks(
-        forward_step, start_state, lax.all_gather(key_value, "ctx", axis=1, tiled=True)
+        forward_step, start_state, gathered
     )
     log_total = top + jnp.log(total)
     attended = (accum / total[..., None]).astype(jnp.bfloat16)
     attended_flat = attended.reshape(seqs, tokens, heads_width)
-    attn_part = jnp.einsum(
+    attn_mine = jnp.einsum(
         "ste,ed->std", attended_flat, proj_out, preferred_element_type=jnp.float32
     )
-    middle = inputs + lax.psum(attn_part, "tp")
+    attn_other = jnp.einsum(
+        "ste,ed->std", tp_other(attended_flat), other_out, preferred_element_type=jnp.float32
+    )
+    middle = inputs + (attn_mine + attn_other)
     scale_two = inverse_rms(middle)
     normed_two = middle * scale_two
     hidden_two = (normed_two * gain_mlp).astype(jnp.bfloat16)
@@ -160,28 +243,46 @@
     sigma = jax.nn.sigmoid(gate)
     activated = (gate * sigma * up).astype(jnp.bfloat16)
     mlp_part = jnp.einsum("stf,fd->std", activated, w_down, preferred_element_type=jnp.float32)
-    output = (middle + lax.psum(mlp_part, "tp")).astype(jnp.bfloat16)
+    output = (middle + tp_sum(mlp_part)).astype(jnp.bfloat16)
     grad_act = jnp.einsum("std,fd->stf", cotangent, w_down, preferred_element_type=jnp.float32)
-    grad_down = jnp.einsum("stf,std->fd", activated, cotangent, preferred_element_type=jnp.float32)
     grad_gate_in = (grad_act * up * sigma * (1.0 + gate * (1.0 - sigma))).astype(jnp.bfloat16)
     grad_up_in = (grad_act * gate * sigma).astype(jnp.bfloat16)
-    grad_gate = jnp.einsum(
-        "std,stf->df", hidden_two, grad_gate_in, preferred_element_type=jnp.float32
-    )
-    grad_up = jnp.einsum("std,stf->df", hidden_two, grad_up_in, preferred_element_type=jnp.float32)
+    flat = seqs * tokens
+    acts = both_cores(activated.reshape(flat, -1))
+    gates = both_cores(grad_gate_in.reshape(flat, -1))
+    ups = both_cores(grad_up_in.reshape(flat, -1))
+    grad_down = quarter_grads(
+        lambda cols: jnp.einsum("tf,td->fd", acts, cols, preferred_element_type=jnp.float32),
+        cotangent.reshape(flat, -1),
+    )
+    hidden_flat = hidden_two.reshape(flat, -1)
+    grad_gate = quarter_grads(
+        lambda cols: jnp.einsum("td,tf->df", cols, gates, preferred_element_type=jnp.float32),
+        hidden_flat,
+    )
+    grad_up = quarter_grads(
+        lambda cols: jnp.einsum("td,tf->df", cols, ups, preferred_element_type=jnp.float32),
+        hidden_flat,
+    )
+    grad_down = line_sum(grad_down)
+    grad_gate = line_sum(grad_gate)
+    grad_up = line_sum(grad_up)
     back_two = jnp.einsum("stf,df->std", grad_gate_in, w_gate, preferred_element_type=jnp.float32)
     back_two = back_two + jnp.einsum(
         "stf,df->std", grad_up_in, w_up, preferred_element_type=jnp.float32
     )
-    back_two = lax.psum(back_two, "tp")
+    back_two = tp_sum(back_two)
     grad_gain_mlp = jnp.sum(back_two * normed_two, axis=(0, 1))
     grad_middle = cotangent.astype(jnp.float32) + norm_back(
         back_two, normed_two, scale_two, gain_mlp
     )
     grad_middle_b = grad_middle.astype(jnp.bfloat16)
-    grad_out = jnp.einsum(
-        "ste,std->ed", attended_flat, grad_middle_b, preferred_element_type=jnp.float32
-    )[None]
+    att_both = both_cores(attended_flat.reshape(flat, -1))
+    grad_out = quarter_grads(
+        lambda cols: jnp.einsum("te,td->ed", att_both, cols, preferred_element_type=jnp.float32),
+        grad_middle_b.reshape(flat, -1),
+    )
+    grad_out = line_sum(grad_out)[None]
     grad_attended = jnp.einsum(
         "std,ed->ste", grad_middle_b, proj_out, preferred_element_type=jnp.float32
     )
@@ -229,9 +330,13 @@
         jnp.zeros((seqs, seq_tokens, 2 * head), jnp.float32),
     )
     grad_queries, grad_keys = over_blocks(
-        backward_step, back_state, lax.all_gather(key_value, "ctx", axis=1, tiled=True)
-    )
-    grad_pairs = lax.psum_scatter(grad_keys, "ctx", scatter_dimension=1, tiled=True)
+        backward_step, back_state, gathered
+    )
+    grad_pairs = lax.dynamic_slice_in_dim(grad_keys, first_token, tokens, 1)
+    for shift in range(1, n_ctx):
+        place = (lax.axis_index("ctx") - shift) % n_ctx * tokens
+        sent = to_bf16(lax.dynamic_slice_in_dim(grad_keys, place, tokens, 1))
+        grad_pairs = grad_pairs + later(sent, shift).astype(jnp.float32)
     grad_q = unrotate(
         grad_queries.reshape(seqs, tokens, group, head), cosine[:, :, None, :], sine[:, :, None, :]
     )
@@ -241,46 +346,38 @@
     )
     grad_bias = jnp.sum(grad_joined, axis=(0, 1))[None]
     grad_joined_b = grad_joined.astype(jnp.bfloat16)
-    grad_qkv = jnp.einsum(
-        "std,ste->de", hidden_one, grad_joined_b, preferred_element_type=jnp.float32
-    )[:, None, :]
-    back_one = jnp.einsum(
+    joined_both = both_cores(grad_joined_b.reshape(flat, -1))
+    grad_qkv = quarter_grads(
+        lambda cols: jnp.einsum("td,te->de", cols, joined_both, preferred_element_type=jnp.float32),
+        hidden_one.reshape(flat, -1),
+    )
+    grad_qkv = line_sum(grad_qkv)[:, None, :]
+    back_mine = jnp.einsum(
         "ste,de->std", grad_joined_b, proj_qkv, preferred_element_type=jnp.float32
     )
-    back_one = lax.psum(back_one, "tp")
+    back_other = jnp.einsum(
+        "ste,de->std", tp_other(grad_joined_b), other_qkv, preferred_element_type=jnp.float32
+    )
+    back_one = back_mine + back_other
     grad_gain_attn = jnp.sum(back_one * normed_one, axis=(0, 1))
     grad_input = grad_middle + norm_back(back_one, normed_one, scale_one, gain_attn)
-    shares = (
-        lax.psum_scatter(grad_gain_attn, ("dp", "ctx"), scatter_dimension=0, tiled=True),
-        lax.psum_scatter(grad_qkv, ("dp", "ctx"), scatter_dimension=0, tiled=True),
-        lax.psum_scatter(grad_bias, ("dp", "ctx"), scatter_dimension=1, tiled=True),
-        lax.psum_scatter(grad_out, ("dp", "ctx"), scatter_dimension=2, tiled=True),
-        lax.psum_scatter(grad_gain_mlp, ("dp", "ctx"), scatter_dimension=0, tiled=True),
-        lax.psum_scatter(grad_gate, ("dp", "ctx"), scatter_dimension=0, tiled=True),
-        lax.psum_scatter(grad_up, ("dp", "ctx"), scatter_dimension=0, tiled=True),
-        lax.psum_scatter(grad_down, ("dp", "ctx"), scatter_dimension=1, tiled=True),
-    )
-    reduced = (
-        lax.all_gather(shares[0], "ctx", axis=0, tiled=True),
-        lax.all_gather(shares[1], "ctx", axis=0, tiled=True),
-        lax.all_gather(shares[2], "ctx", axis=1, tiled=True),
-        lax.all_gather(shares[3], "ctx", axis=2, tiled=True),
-        lax.all_gather(shares[4], "ctx", axis=0, tiled=True),
-        lax.all_gather(shares[5], "ctx", axis=0, tiled=True),
-        lax.all_gather(shares[6], "ctx", axis=0, tiled=True),
-        lax.all_gather(shares[7], "ctx", axis=1, tiled=True),
-    )
+    small = lax.psum((grad_gain_attn, grad_bias[0], grad_gain_mlp), ("dp", "ctx"))
+    n_dp = lax.axis_size("dp")
+    small = [
+        lax.dynamic_slice_in_dim(v, lax.axis_index("dp") * (v.shape[0] // n_dp), v.shape[0] // n_dp)
+        for v in small
+    ]
     return (
         output,
         grad_input,
-        reduced[0],
-        reduced[1],
-        reduced[2],
-        reduced[3],
-        reduced[4],
-        reduced[5],
-        reduced[6],
-        reduced[7],
+        small[0],
+        grad_qkv,
+        small[1][None],
+        grad_out,
+        small[2],
+        grad_gate,
+        grad_up,
+        grad_down,
     )
 
 

time: 1400 us -> 914 us (0.65)
  waiting for transfers between devices: 959 us -> 383 us
  local copies, waits for them, and re-layouts: 74.4 us -> 189 us
  blocking collectives: 106 us -> 61 us
  starting transfers between devices: 1.28 us -> 45.6 us
  between operations: 17.6 us -> 2.26 us
  other arithmetic: 68.5 us -> 53.5 us
    unnamed x16 -> x0, waiting for transfers between devices: 416 us -> none
    psum x3 -> x0, waiting for transfers between devices: 395 us -> none  [the longest x1 157 us: shards(): middle = inputs + lax.psum(attn_part, 'tp')]
    ppermute x0 -> x41, waiting for transfers between devices: none -> 383 us  [the longest x3 184 us: later(): lax.ppermute(values, 'ctx', [(i + shift, i) for i in range(n - shift)])]
    reduce_scatter x1 -> x0, waiting for transfers between devices: 87.1 us -> none  [shards(): lax.psum_scatter(grad_keys, 'ctx', scatter_dimension=1, tiled=True)]
    unnamed x2 -> x0, blocking collectives: 74.1 us -> none
    psum x0 -> x1, blocking collectives: none -> 61 us  [shards(): lax.psum((grad_gain_attn, grad_bias[0], grad_gain_mlp), ('dp', 'ctx'))]
    all_gather x4 -> x0, waiting for transfers between devices: 59.9 us -> none  [the longest x1 47.2 us: shards(): lax.all_gather(shares[7], 'ctx', axis=1, tiled=True)]
    another operation x2 -> x11, local copies, waits for them, and re-layouts: 1.59 us -> 50.3 us  [the longest x4 34.7 us: quarter_grads(): split = wide.reshape(wide.shape[0], rows, 2, wide.shape[1] // n_dp)]
  transfers between devices with their start and end apart: 12 -> 41, of which waited for: 11 -> 14; matrix products, arithmetic and copies ran while one was open for 11% -> 44% of each run, Pallas kernels for 0% -> 0%
where the time goes in v1:
time: 914 us; the launch traced here: 908 us
  waiting for transfers between devices  383 us (42%)
  local copies, waits for them, and re-layouts  189 us (21%)
  matrix products  174 us (19%)
  blocking collectives  61 us (7%)
  other arithmetic  53.5 us (6%)
  starting transfers between devices  45.6 us (5%)
    ppermute x3, waiting for transfers between devices, later(): lax.ppermute(values, 'ctx', [(i + shift, i) for i in range(n - shift)])  184 us
    unnamed x129, local copies, waits for them, and re-layouts  70.2 us
    ppermute x5, waiting for transfers between devices, line_sum(): moved = lax.ppermute(total, 'ctx', pairs)  67.4 us
    psum x1, blocking collectives, shards(): lax.psum((grad_gain_attn, grad_bias[0], grad_gain_mlp), ('dp', 'ctx'))  61 us
    ppermute x6, waiting for transfers between devices, tp_other(): return lax.ppermute(values, 'tp', [(0, 1), (1, 0)])  58.1 us
    ppermute x5, waiting for transfers between devices, quarter_grads(): moved = lax.ppermute(part, 'dp', pairs).astype(jnp.float32)  52.2 us
    another operation x4, local copies, waits for them, and re-layouts, quarter_grads(): split = wide.reshape(wide.shape[0], rows, 2, wide.shape[1] // n_dp)  34.7 us
    dynamic_slice x3, local copies, waits for them, and re-layouts, quarter_grads(): lax.dynamic_index_in_dim(split, 1 - core, 2, keepdims=False)  23.1 us
  transfers between devices with their start and end apart: 41, of which 14 were waited for; matrix products, arithmetic and copies ran while one was open for 44% of the time, Pallas kernels for 0%

profile of v1, /device:TPU:0, one launch (start us, length us, event | category | flops | bytes accessed | tf_op | source)
XLA Modules:
  0.0 908.3 jit_solution(10584803297683141531)
XLA Ops:
  67.3 22.9 %while.34 = (s32[]{:T(128)}, f32[2,3584]{1,0:T(2,128)S(1)}, f32[2,3584]{1,0:T(2,128)S(1)}, f32[2,3584,64]{1,2,0:T(8,128)}, s32[]{:T(128)}, /*index=5*/bf16[2,204...) while((s32[]{:T(128)}, f32[2,3584]{1,0:T(2,128)S(1)}, ...), condition=%wide.region_6.7_spmd.clone, body=%wide.region_1.6_spmd.clone.sunk | while | flops 1004681728 | bytes 115655000 | solution.py:203
  67.5 22.7 %conditional.6 = ((f32[2,3584]{1,0:T(2,128)S(1)}, f32[2,3584]{1,0:T(2,128)S(1)}, f32[2,3584,64]{1,2,0:T(8,128)})) conditional(s32[]{:T(128)} %convert_element_type.440, (f32[2,3584]{1,0:T(2,128)S(1)}, f32[2,3584]{1,0:T(2,128)S(1)}, f32[2,3584,64]{1,2,0:T(8,128)}) %tuple.139, (s32[]{:T(128)}, s32[512]{0:T(512)S(1)}, s32[2,512]{1,0:T(2,128)S(1)}, ...), branch_computations={%region_2.2_spmd, %region_3.5_spmd} | conditional | flops 1004681728 | bytes 115654776 | solution.py:196
  101.1 10.5 %fusion.50 = f32[2,512,2432]{2,1,0:T(8,128)} fusion(bf16[2,512,896]{2,1,0:T(8,128)(2,1)S(1)} %copy-done.10, bf16[2432,896]{1,0:T(8,128)(2,1)} %param.28), kind=kOutput, calls=%fused_computation.66 | convolution fusion | flops 4462739456 | bytes 16154624 | tf_op jit(solution)/shard_map/std,fd->stf/dot_general | solution.py:247
  148.1 17.1 %multiply_convert_fusion.1 = (bf16[2,512,2432]{2,1,0:T(8,128)(2,1)}, bf16[2,512,2432]{2,1,0:T(8,128)(2,1)}, bf16[2,512,2432]{2,1,0:T(8,128)(2,1)}) fusion(f32[2,512,2432]{2,1,0:T(8,128)} %fusion.50, f32[2,512,2432]{2,1,0:T(8,128)} %fusion.56, bf16[2,512,896]{2,1,0:T(8,128)(2,1)S(1)} %multiply_convert_fusion.3, bf16[896,2432]{1,0:T(8,128)(2,1)} %param.26), kind=kOutput, calls=%fused_computation.50 | convolution fusion | flops 4502585344 | bytes 41058304 | tf_op jit(solution)/shard_map/std,df->stf/dot_general | solution.py:241
  172.7 9.7 %add_convert_fusion = bf16[2,512,896]{2,1,0:T(8,128)(2,1)} fusion(f32[2,512,896]{2,1,0:T(8,128)S(1)} %fusion.54, bf16[2,512,2432]{2,1,0:T(8,128)(2,1)} %get-tuple-element.765, bf16[896,2432]{1,0:T(8,128)(2,1)} %param.26), kind=kOutput, calls=%fused_computation.95 | convolution fusion | flops 4464574464 | bytes 14843904 | tf_op jit(solution)/shard_map/stf,df->std/dot_general | solution.py:270
  192.1 9.9 %fusion.78 = bf16[2,512,896]{2,1,0:T(8,128)(2,1)} fusion(bf16[2,512,2432]{2,1,0:T(8,128)(2,1)} %get-tuple-element.766, bf16[2432,896]{1,0:T(8,128)(2,1)} %param.28), kind=kOutput, calls=%fused_computation.130 | convolution fusion | flops 4463656960 | bytes 11173888 | tf_op jit(solution)/shard_map/stf,fd->std/dot_general | solution.py:245
  202.0 21.1 %collective-permute-done.6 = bf16[2,512,896]{2,1,0:T(8,128)(2,1)} collective-permute-done((bf16[2,512,896]{2,1,0:T(8,128)(2,1)}, bf16[2,512,896]{2,1,0:T(8,128)(2,1)}, u32[]{:S(2)}, u32[]{:S(2)}) %collective-permute-start.6) | collective-permute-done | bytes 1835040 | tf_op jit(solution)/shard_map/ppermute | solution.py:55
  255.1 11.2 %constant_dynamic-slice_fusion = (bf16[1024,2,1,224]{3,2,1,0:T(2,128)(2,1)}, bf16[1024,2,1,224]{3,2,1,0:T(2,128)(2,1)}, bf16[1024,2,1,224]{3,2,1,0:T(2,128)(2,1)}, bf16[1024,2,1,224]{3,2,1,0:T(2,128)(2,1)}) fusion(bf16[1024,2,2,224]{3,2,1,0:T(2,128)(2,1)S(1)} %reshape.205, s32[]{:T(128)S(6)} %select_n.195, s32[]{:T(128)S(6)} %select_n.194, ...), kind=kLoop, calls=%fused_computation.212 | loop fusion | bytes 7340040 | tf_op jit(solution)/shard_map/jit(dynamic_index_in_dim)/dynamic_slice | solution.py:102
  275.7 36.9 %while.35 = (s32[]{:T(128)}, f32[2,3584,64]{1,2,0:T(8,128)S(1)}, f32[2,2048,128]{1,2,0:T(8,128)}, s32[]{:T(128)}, bf16[2,2048,128]{1,2,0:T(8,128)(2,1)}, /*index...) while((s32[]{:T(128)}, f32[2,3584,64]{1,2,0:T(8,128)S(1)}, ...), condition=%wide.region_12.13_spmd.clone, body=%wide.region_9.12_spmd.clone.sunk | while | flops 2403271168 | bytes 92707216 | solution.py:203
  276.2 36.4 %conditional.7 = ((f32[2,3584,64]{1,2,0:T(8,128)S(1)}, f32[2,2048,128]{1,2,0:T(8,128)})) conditional(s32[]{:T(128)} %convert_element_type.441, (f32[2,3584,64]{1,2,0:T(8,128)S(1)}, f32[2,2048,128]{1,2,0:T(8,128)}) %tuple.142, (s32[]{:T(128)}, s32[512]{0:T(512)S(1)}, s32[2,512]{1,0:T(2,128)S(1)}, bf16[2,2048,128]{1,2,0:T(8,128)(2,1)}, ...), branch_computations={%region_10.10_spmd, %region_11.11_spmd} | conditional | flops 2403271168 | bytes 92706968 | solution.py:196
  287.5 10.5 %fusion.25 = bf16[2,3584,512]{1,2,0:T(8,128)(2,1)S(1)} fusion(f32[2,512,3584]{2,1,0:T(8,128)} %fusion.33, bf16[2,3584,64]{1,2,0:T(8,128)(2,1)} %get-tuple-element.514, f32[2,3584]{1,0:T(2,128)S(1)} %get-tuple-element.515, f32[2,3584]{1,0:T(2,128)S(1)} %get-tuple-element.513, s32[2,3584]{1,0:T(2,128)S(1)} %ge.43, s32[512]{0:T(512)S(1)} %iota_add_fusion.1, ...), kind=kOutput, calls=%fused_computation.26 | convolution fusion | flops 499122176 | bytes 24991752 | tf_op jit(solution)/shard_map/while/body/eval_jaxpr/cond/branch_1_fun/srd,skd->srk/dot_general | solution.py:298
  316.5 11.1 %fusion.159 = (f32[2,512,7,32]{3,0,2,1:T(2,128)}, f32[2,512,7,32]{3,0,2,1:T(2,128)}) fusion(f32[2,512,7,64]{3,0,2,1:T(2,128)} %bitcast.162), kind=kLoop, calls=%fused_computation.247 | loop fusion | bytes 3670016 | tf_op jit(solution)/shard_map/slice | solution.py:38
  348.4 55.2 %collective-permute-done.7 = bf16[2,512,128]{1,2,0:T(8,128)(2,1)S(1)} collective-permute-done((bf16[2,512,128]{1,2,0:T(8,128)(2,1)S(1)}, bf16[2,512,128]{1,2,0:T(8,128)(2,1)S(1)}, u32[]{:S(2)}, u32[]{:S(2)}) %collective-permute-start.7) | collective-permute-done | bytes 262176 | tf_op jit(solution)/shard_map/ppermute | solution.py:75
  403.6 64.6 %collective-permute-done.8 = bf16[2,512,128]{1,2,0:T(8,128)(2,1)S(1)} collective-permute-done((bf16[2,512,128]{1,2,0:T(8,128)(2,1)S(1)}, bf16[2,512,128]{1,2,0:T(8,128)(2,1)S(1)}, u32[]{:S(2)}, u32[]{:S(2)}) %collective-permute-start.8) | collective-permute-done | bytes 262176 | tf_op jit(solution)/shard_map/ppermute | solution.py:75
  468.2 63.9 %collective-permute-done.9 = bf16[2,512,128]{1,2,0:T(8,128)(2,1)S(1)} collective-permute-done((bf16[2,512,128]{1,2,0:T(8,128)(2,1)S(1)}, bf16[2,512,128]{1,2,0:T(8,128)(2,1)S(1)}, u32[]{:S(2)}, u32[]{:S(2)}) %collective-permute-start.9) | collective-permute-done | bytes 262176 | tf_op jit(solution)/shard_map/ppermute | solution.py:75
  616.0 28.8 %collective-permute-done.5 = bf16[2,512,896]{2,1,0:T(8,128)(2,1)S(1)} collective-permute-done((bf16[2,512,896]{2,1,0:T(8,128)(2,1)S(1)}, bf16[2,512,896]{2,1,0:T(8,128)(2,1)S(1)}, u32[]{:S(2)}, u32[]{:S(2)}) %collective-permute-start.5) | collective-permute-done | bytes 1835040 | tf_op jit(solution)/shard_map/ppermute | solution.py:55
  652.2 61.0 %all-reduce = (f32[896]{0:T(1024)}, f32[576]{0:T(1024)}, f32[896]{0:T(1024)}) all-reduce(f32[896]{0:T(1024)} %get-tuple-element.712, f32[576]{0:T(1024)} %fusion.83, f32[896]{0:T(1024)} %get-tuple-element.710), channel_id=1, replica_groups=mesh['dp'=4,'ctx'=4,'tp'=2] {'dp','ctx'}, use_global_device_ids=true, to_apply=%region_15.16 | all-reduce | flops 2368 | bytes 18944 | tf_op jit(solution)/shard_map/psum | solution.py:364
  742.6 11.5 %collective-permute-done.37 = bf16[2432,224]{0,1:T(8,128)(2,1)S(1)} collective-permute-done((bf16[2432,224]{0,1:T(8,128)(2,1)S(1)}, bf16[2432,224]{0,1:T(8,128)(2,1)S(1)}, u32[]{:S(2)}, u32[]{:S(2)}) %collective-permute-start.37) | collective-permute-done | bytes 1089568 | tf_op jit(solution)/shard_map/ppermute | solution.py:112
  760.8 16.6 %collective-permute-done.31 = bf16[224,2432]{1,0:T(8,128)(2,1)S(1)} collective-permute-done((bf16[224,2432]{1,0:T(8,128)(2,1)S(1)}, bf16[224,2432]{1,0:T(8,128)(2,1)S(1)}, u32[]{:S(2)}, u32[]{:S(2)}) %collective-permute-start.31) | collective-permute-done | bytes 1089568 | tf_op jit(solution)/shard_map/ppermute | solution.py:112
  784.1 16.2 %collective-permute-done.26 = bf16[224,2432]{1,0:T(8,128)(2,1)S(1)} collective-permute-done((bf16[224,2432]{1,0:T(8,128)(2,1)S(1)}, bf16[224,2432]{1,0:T(8,128)(2,1)S(1)}, u32[]{:S(2)}, u32[]{:S(2)}) %collective-permute-start.26) | collective-permute-done | bytes 1089568 | tf_op jit(solution)/shard_map/ppermute | solution.py:112
  809.2 21.2 %collective-permute-done.27 = bf16[224,2432]{1,0:T(8,128)(2,1)S(1)} collective-permute-done((bf16[224,2432]{1,0:T(8,128)(2,1)S(1)}, bf16[224,2432]{1,0:T(8,128)(2,1)S(1)}, u32[]{:S(2)}, u32[]{:S(2)}) %collective-permute-start.27) | collective-permute-done | bytes 1089568 | tf_op jit(solution)/shard_map/ppermute | solution.py:84
  836.2 25.3 %collective-permute-done.40 = bf16[2432,224]{0,1:T(8,128)(2,1)S(1)} collective-permute-done((bf16[2432,224]{0,1:T(8,128)(2,1)S(1)}, bf16[2432,224]{0,1:T(8,128)(2,1)S(1)}, u32[]{:S(2)}, u32[]{:S(2)}) %collective-permute-start.40) | collective-permute-done | bytes 1089568 | tf_op jit(solution)/shard_map/ppermute | solution.py:90
  863.0 21.9 %collective-permute-done.34 = bf16[224,2432]{1,0:T(8,128)(2,1)S(1)} collective-permute-done((bf16[224,2432]{1,0:T(8,128)(2,1)S(1)}, bf16[224,2432]{1,0:T(8,128)(2,1)S(1)}, u32[]{:S(2)}, u32[]{:S(2)}) %collective-permute-start.34) | collective-permute-done | bytes 1089568 | tf_op jit(solution)/shard_map/ppermute | solution.py:90
  886.3 20.2 %collective-permute-done.29 = bf16[224,2432]{1,0:T(8,128)(2,1)S(1)} collective-permute-done((bf16[224,2432]{1,0:T(8,128)(2,1)S(1)}, bf16[224,2432]{1,0:T(8,128)(2,1)S(1)}, u32[]{:S(2)}, u32[]{:S(2)}) %collective-permute-start.29) | collective-permute-done | bytes 1089568 | tf_op jit(solution)/shard_map/ppermute | solution.py:90
  (337 shorter events, 397.5 us)
Async XLA Ops:
  11.1 50.8 %collective-permute-start = (bf16[2,512,128]{1,2,0:T(8,128)(2,1)}, bf16[2,512,128]{1,2,0:T(8,128)(2,1)}, u32[]{:S(2)}, u32[]{:S(2)}) collective-permute-start(bf16[2,512,128]{1,2,0:T(8,128)(2,1)} %get-tuple-element.791), channel_id=1, source_target_pairs={{0,2},{2,4},{4,6},{1,3},{3,5},{5,7},{8,10},{10,12},{12,14},{9,11},... | collective-permute-start | bytes 786440 | tf_op jit(solution)/shard_map/ppermute | solution.py:70
  16.8 47.4 %collective-permute-start.1 = (bf16[2,512,128]{1,2,0:T(8,128)(2,1)}, bf16[2,512,128]{1,2,0:T(8,128)(2,1)S(1)}, u32[]{:S(2)}, u32[]{:S(2)}) collective-permute-start(bf16[2,512,128]{1,2,0:T(8,128)(2,1)} %get-tuple-element.791), channel_id=1, source_target_pairs={{0,4},{2,6},{1,5},{3,7},{8,12},{10,14},{9,13},{11,15},{16,20},{18,... | collective-permute-start | bytes 786440 | tf_op jit(solution)/shard_map/ppermute | solution.py:70
  20.6 44.4 %collective-permute-start.2 = (bf16[2,512,128]{1,2,0:T(8,128)(2,1)}, bf16[2,512,128]{1,2,0:T(8,128)(2,1)S(1)}, u32[]{:S(2)}, u32[]{:S(2)}) collective-permute-start(bf16[2,512,128]{1,2,0:T(8,128)(2,1)} %get-tuple-element.791), channel_id=1, source_target_pairs={{0,6},{1,7},{8,14},{9,15},{16,22},{17,23},{24,30},{25,31}} | collective-permute-start | bytes 786440 | tf_op jit(solution)/shard_map/ppermute | solution.py:70
  22.5 112.2 %collective-permute-start.4 = (bf16[448,896]{1,0:T(8,128)(2,1)}, bf16[448,896]{1,0:T(8,128)(2,1)}, u32[]{:S(2)}, u32[]{:S(2)}) collective-permute-start(bf16[448,896]{1,0:T(8,128)(2,1)} %bitcast.8), channel_id=1, source_target_pairs={{0,1},{1,0},{2,3},{3,2},{4,5},{5,4},{6,7},{7,6},{8,9},{9,8},{10,11... | collective-permute-start | bytes 2408456 | tf_op jit(solution)/shard_map/ppermute | solution.py:55
  44.5 533.3 %collective-permute-start.12 = (bf16[1024,2,224]{0,2,1:T(8,128)(2,1)}, bf16[1024,2,224]{0,2,1:T(8,128)(2,1)}, u32[]{:S(2)}, u32[]{:S(2)}) collective-permute-start(bf16[1024,2,224]{0,2,1:T(8,128)(2,1)} %bitcast.18), channel_id=1, source_target_pairs={{0,8},{8,0},{16,24},{24,16},{1,9},{9,1},{17,25},{25,17},{2,10},{10... | collective-permute-start | bytes 2752520 | tf_op jit(solution)/shard_map/ppermute | solution.py:65
  61.9 523.0 %collective-permute-start.11 = (bf16[896,576]{0,1:T(8,128)(2,1)}, bf16[896,576]{0,1:T(8,128)(2,1)}, u32[]{:S(2)}, u32[]{:S(2)}) collective-permute-start(bf16[896,576]{0,1:T(8,128)(2,1)} %bitcast.198), channel_id=1, source_target_pairs={{0,1},{1,0},{2,3},{3,2},{4,5},{5,4},{6,7},{7,6},{8,9},{9,8},{10,11... | collective-permute-start | bytes 3096584 | tf_op jit(solution)/shard_map/ppermute | solution.py:55
  182.4 40.7 %collective-permute-start.6 = (bf16[2,512,896]{2,1,0:T(8,128)(2,1)}, bf16[2,512,896]{2,1,0:T(8,128)(2,1)}, u32[]{:S(2)}, u32[]{:S(2)}) collective-permute-start(bf16[2,512,896]{2,1,0:T(8,128)(2,1)} %add_convert_fusion), channel_id=1, source_target_pairs={{0,1},{1,0},{2,3},{3,2},{4,5},{5,4},{6,7},{7,6},{8,9},{9,8},{10,11... | collective-permute-start | bytes 5505032 | tf_op jit(solution)/shard_map/ppermute | solution.py:55
  339.5 64.1 %collective-permute-start.7 = (bf16[2,512,128]{1,2,0:T(8,128)(2,1)S(1)}, bf16[2,512,128]{1,2,0:T(8,128)(2,1)S(1)}, u32[]{:S(2)}, u32[]{:S(2)}) collective-permute-start(bf16[2,512,128]{1,2,0:T(8,128)(2,1)S(1)} %get-tuple-element.784), channel_id=1, source_target_pairs={{2,0},{4,2},{6,4},{3,1},{5,3},{7,5},{10,8},{12,10},{14,12},{11,9},... | collective-permute-start | bytes 786440 | tf_op jit(solution)/shard_map/ppermute | solution.py:75
  340.8 127.5 %collective-permute-start.8 = (bf16[2,512,128]{1,2,0:T(8,128)(2,1)S(1)}, bf16[2,512,128]{1,2,0:T(8,128)(2,1)S(1)}, u32[]{:S(2)}, u32[]{:S(2)}) collective-permute-start(bf16[2,512,128]{1,2,0:T(8,128)(2,1)S(1)} %get-tuple-element.785), channel_id=1, source_target_pairs={{4,0},{6,2},{5,1},{7,3},{12,8},{14,10},{13,9},{15,11},{20,16},{22,... | collective-permute-start | bytes 786440 | tf_op jit(solution)/shard_map/ppermute | solution.py:75
  342.1 190.1 %collective-permute-start.9 = (bf16[2,512,128]{1,2,0:T(8,128)(2,1)S(1)}, bf16[2,512,128]{1,2,0:T(8,128)(2,1)S(1)}, u32[]{:S(2)}, u32[]{:S(2)}) collective-permute-start(bf16[2,512,128]{1,2,0:T(8,128)(2,1)S(1)} %get-tuple-element.786), channel_id=1, source_target_pairs={{6,0},{7,1},{14,8},{15,9},{22,16},{23,17},{30,24},{31,25}} | collective-permute-start | bytes 786440 | tf_op jit(solution)/shard_map/ppermute | solution.py:75
  403.6 147.3 %collective-permute-start.18 = (bf16[1024,448]{0,1:T(8,128)(2,1)}, bf16[1024,448]{0,1:T(8,128)(2,1)}, u32[]{:S(2)}, u32[]{:S(2)}) collective-permute-start(bf16[1024,448]{0,1:T(8,128)(2,1)} %copy.108), channel_id=1, source_target_pairs={{0,8},{8,0},{16,24},{24,16},{1,9},{9,1},{17,25},{25,17},{2,10},{10... | collective-permute-start | bytes 2752520 | tf_op jit(solution)/shard_map/ppermute | solution.py:65
  468.2 89.3 %collective-permute-start.19 = (bf16[1024,2,224]{0,2,1:T(8,128)(2,1)}, bf16[1024,2,224]{0,2,1:T(8,128)(2,1)}, u32[]{:S(2)}, u32[]{:S(2)}) collective-permute-start(bf16[1024,2,224]{0,2,1:T(8,128)(2,1)} %bitcast.24), channel_id=1, source_target_pairs={{0,8},{8,0},{16,24},{24,16},{1,9},{9,1},{17,25},{25,17},{2,10},{10... | collective-permute-start | bytes 2752520 | tf_op jit(solution)/shard_map/ppermute | solution.py:65
  535.6 42.8 %collective-permute-start.13 = (bf16[1024,576]{0,1:T(8,128)(2,1)}, bf16[1024,576]{0,1:T(8,128)(2,1)}, u32[]{:S(2)}, u32[]{:S(2)}) collective-permute-start(bf16[1024,576]{0,1:T(8,128)(2,1)} %constant_dynamic-update-slice_fusion), channel_id=1, source_target_pairs={{0,8},{8,0},{16,24},{24,16},{1,9},{9,1},{17,25},{25,17},{2,10},{10... | collective-permute-start | bytes 3538952 | tf_op jit(solution)/shard_map/ppermute | solution.py:65
  550.9 169.5 %collective-permute-start.35 = (bf16[1024,2432]{1,0:T(8,128)(2,1)}, bf16[1024,2432]{1,0:T(8,128)(2,1)}, u32[]{:S(2)}, u32[]{:S(2)}) collective-permute-start(bf16[1024,2432]{1,0:T(8,128)(2,1)} %bitcast.191), channel_id=1, source_target_pairs={{0,8},{8,0},{16,24},{24,16},{1,9},{9,1},{17,25},{25,17},{2,10},{10... | collective-permute-start | bytes 14942216 | tf_op jit(solution)/shard_map/ppermute | solution.py:65
  574.4 154.4 %collective-permute-start.30 = (bf16[1024,2432]{1,0:T(8,128)(2,1)}, bf16[1024,2432]{1,0:T(8,128)(2,1)}, u32[]{:S(2)}, u32[]{:S(2)}) collective-permute-start(bf16[1024,2432]{1,0:T(8,128)(2,1)} %bitcast.186), channel_id=1, source_target_pairs={{0,8},{8,0},{16,24},{24,16},{1,9},{9,1},{17,25},{25,17},{2,10},{10... | collective-permute-start | bytes 14942216 | tf_op jit(solution)/shard_map/ppermute | solution.py:65
  584.9 149.5 %collective-permute-start.25 = (bf16[1024,2432]{1,0:T(8,128)(2,1)}, bf16[1024,2432]{1,0:T(8,128)(2,1)}, u32[]{:S(2)}, u32[]{:S(2)}) collective-permute-start(bf16[1024,2432]{1,0:T(8,128)(2,1)} %bitcast.31), channel_id=1, source_target_pairs={{0,8},{8,0},{16,24},{24,16},{1,9},{9,1},{17,25},{25,17},{2,10},{10... | collective-permute-start | bytes 14942216 | tf_op jit(solution)/shard_map/ppermute | solution.py:65
  594.2 50.6 %collective-permute-start.5 = (bf16[2,512,896]{2,1,0:T(8,128)(2,1)S(1)}, bf16[2,512,896]{2,1,0:T(8,128)(2,1)S(1)}, u32[]{:S(2)}, u32[]{:S(2)}) collective-permute-start(bf16[2,512,896]{2,1,0:T(8,128)(2,1)S(1)} %copy-done.20), channel_id=1, source_target_pairs={{0,1},{1,0},{2,3},{3,2},{4,5},{5,4},{6,7},{7,6},{8,9},{9,8},{10,11... | collective-permute-start | bytes 5505032 | tf_op jit(solution)/shard_map/ppermute | solution.py:55
  644.8 75.6 %collective-permute-start.36 = (bf16[1024,2,224]{0,2,1:T(8,128)(2,1)S(1)}, bf16[1024,2,224]{0,2,1:T(8,128)(2,1)}, u32[]{:S(2)}, u32[]{:S(2)}) collective-permute-start(bf16[1024,2,224]{0,2,1:T(8,128)(2,1)S(1)} %bitcast.179), channel_id=1, source_target_pairs={{0,8},{8,0},{16,24},{24,16},{1,9},{9,1},{17,25},{25,17},{2,10},{10... | collective-permute-start | bytes 2752520 | tf_op jit(solution)/shard_map/ppermute | solution.py:65
  644.8 72.3 %collective-permute-start.17 = (bf16[224,576]{1,0:T(8,128)(2,1)S(1)}, bf16[224,576]{1,0:T(8,128)(2,1)S(1)}, u32[]{:S(2)}, u32[]{:S(2)}) collective-permute-start(bf16[224,576]{1,0:T(8,128)(2,1)S(1)} %add_convert_fusion.9), channel_id=1, source_target_pairs={{2,0},{4,6},{3,1},{5,7},{10,8},{12,14},{11,9},{13,15},{18,16},{20,... | collective-permute-start | bytes 774152 | tf_op jit(solution)/shard_map/ppermute | solution.py:90
  734.0 43.5 %collective-permute-start.31 = (bf16[224,2432]{1,0:T(8,128)(2,1)S(1)}, bf16[224,2432]{1,0:T(8,128)(2,1)S(1)}, u32[]{:S(2)}, u32[]{:S(2)}) collective-permute-start(bf16[224,2432]{1,0:T(8,128)(2,1)S(1)} %fusion.66), channel_id=1, source_target_pairs={{0,16},{8,24},{16,0},{24,8},{1,17},{9,25},{17,1},{25,9},{2,18},{10... | collective-permute-start | bytes 3268616 | tf_op jit(solution)/shard_map/ppermute | solution.py:112
  740.9 59.4 %collective-permute-start.26 = (bf16[224,2432]{1,0:T(8,128)(2,1)S(1)}, bf16[224,2432]{1,0:T(8,128)(2,1)S(1)}, u32[]{:S(2)}, u32[]{:S(2)}) collective-permute-start(bf16[224,2432]{1,0:T(8,128)(2,1)S(1)} %fusion.65), channel_id=1, source_target_pairs={{0,16},{8,24},{16,0},{24,8},{1,17},{9,25},{17,1},{25,9},{2,18},{10... | collective-permute-start | bytes 3268616 | tf_op jit(solution)/shard_map/ppermute | solution.py:112
  759.4 47.7 %collective-permute-start.38 = (bf16[2432,224]{0,1:T(8,128)(2,1)S(1)}, bf16[2432,224]{0,1:T(8,128)(2,1)S(1)}, u32[]{:S(2)}, u32[]{:S(2)}) collective-permute-start(bf16[2432,224]{0,1:T(8,128)(2,1)S(1)} %get-tuple-element.810), channel_id=1, source_target_pairs={{0,2},{6,4},{1,3},{7,5},{8,10},{14,12},{9,11},{15,13},{16,18},{22,... | collective-permute-start | bytes 3268616 | tf_op jit(solution)/shard_map/ppermute | solution.py:84
  833.3 51.6 %collective-permute-start.34 = (bf16[224,2432]{1,0:T(8,128)(2,1)S(1)}, bf16[224,2432]{1,0:T(8,128)(2,1)S(1)}, u32[]{:S(2)}, u32[]{:S(2)}) collective-permute-start(bf16[224,2432]{1,0:T(8,128)(2,1)S(1)} %add_convert_fusion.4), channel_id=1, source_target_pairs={{2,0},{4,6},{3,1},{5,7},{10,8},{12,14},{11,9},{13,15},{18,16},{20,... | collective-permute-start | bytes 3268616 | tf_op jit(solution)/shard_map/ppermute | solution.py:90
  834.9 71.7 %collective-permute-start.29 = (bf16[224,2432]{1,0:T(8,128)(2,1)S(1)}, bf16[224,2432]{1,0:T(8,128)(2,1)S(1)}, u32[]{:S(2)}, u32[]{:S(2)}) collective-permute-start(bf16[224,2432]{1,0:T(8,128)(2,1)S(1)} %add_convert_fusion.6), channel_id=1, source_target_pairs={{2,0},{4,6},{3,1},{5,7},{10,8},{12,14},{11,9},{13,15},{18,16},{20,... | collective-permute-start | bytes 3268616 | tf_op jit(solution)/shard_map/ppermute | solution.py:90
  (76 other events, 1757.0 us)

commit v2 on v1

v2 whole, which is shorter than its diff:
```python
import jax
import jax.numpy as jnp
from jax import lax
from jax.experimental import pallas as pl
from jax.experimental.pallas import tpu as pltpu
from jax.sharding import PartitionSpec as P

EPS = 1e-06
THETA = 1000000.0
SCALE = 0.125
NEGATIVE = -1e30
HD=64
F32=jnp.float32
BF=jnp.bfloat16

def dot(a, b):
    return jnp.dot(a, b, preferred_element_type=jnp.float32)

def dot_nt(a, b):
    return lax.dot_general(a, b, (((1,), (1,)), ((), ())), preferred_element_type=jnp.float32)

def turn(rows, cosine, sine):
    half = rows.shape[0] // 2
    first, second = rows[:half], rows[half:]
    return jnp.concatenate([first * cosine - second * sine, second * cosine + first * sine], axis=0)

def turn_back(rows, cosine, sine):
    return turn(rows, cosine, -sine)

def project_kernel(x_ref, gain_ref, w_ref, b_ref, cos_ref, sin_ref, hidden_ref, q_ref, kv_ref):
    x = x_ref[0].astype(F32)
    scale = lax.rsqrt(jnp.mean(x * x, axis=-1, keepdims=True) + EPS)
    hidden = (x * scale * gain_ref[...]).astype(BF)
    hidden_ref[0] = hidden
    joined = dot(hidden, w_ref[...]) + b_ref[...]
    turned = joined.T
    cosine, sine = cos_ref[0], sin_ref[0]
    width = q_ref.shape[1]
    for start in range(0, width, HD):
        q_ref[0, start:start + HD, :] = (turn(turned[start:start + HD], cosine, sine) * SCALE).astype(BF)
    keys = turn(turned[width:width + HD], cosine, sine)
    pair = jnp.concatenate([keys, turned[width + HD:]], axis=0)
    kv_ref[0] = pair.T.astype(BF)

def project(x, gain, w, b, cosine, sine, width):
    seqs, tokens, model = x.shape
    half = cosine.shape[1]
    whole = lambda a: pl.BlockSpec(a.shape, lambda s: (0,) * a.ndim)
    per = lambda r, c: pl.BlockSpec((1, r, c), lambda s: (s, 0, 0))
    return pl.pallas_call(
        project_kernel, grid=(seqs,),
        in_specs=[per(tokens, model), whole(gain), whole(w), whole(b), per(half, tokens), per(half, tokens)],
        out_specs=[per(tokens, model), per(width, tokens), per(tokens, 2 * HD)],
        out_shape=[jax.ShapeDtypeStruct((seqs, tokens, model), BF), jax.ShapeDtypeStruct((seqs, width, tokens), BF),
                   jax.ShapeDtypeStruct((seqs, tokens, 2 * HD), BF)],
        cost_estimate=pl.CostEstimate(flops=2 * seqs * tokens * model * w.shape[1], transcendentals=0, bytes_accessed=8 * seqs * tokens * model),
        name="project")(x, gain, w, b, cosine, sine)

def allowed_of(first_ref, place, s, tokens):
    key = lax.broadcasted_iota(jnp.int32, (tokens, tokens), 0) + (place - s * tokens)
    query = lax.broadcasted_iota(jnp.int32, (tokens, tokens), 1) + place
    return (key <= query) & (key >= first_ref[0])

def attend_kernel(info_ref, q_ref, kv_ref, first_ref, out_ref, lse_ref, top_ref, total_ref, acc_ref):
    seq = pl.program_id(0)
    tokens = q_ref.shape[2]
    heads = q_ref.shape[1] // HD
    place = info_ref[0]
    count, last_first = info_ref[1 + 2 * seq], info_ref[2 + 2 * seq]
    top_ref[...] = jnp.full_like(top_ref, NEGATIVE)
    total_ref[...] = jnp.zeros_like(total_ref)
    acc_ref[...] = jnp.zeros_like(acc_ref)

    def block(s, masked):
        pair = kv_ref[s, 0]
        keys = pair[:, :HD]
        values = pair.T[HD:]
        ok = allowed_of(first_ref, place, s, tokens) if masked else None
        for h in range(heads):
            rows = slice(h * HD, (h + 1) * HD)
            scores = dot(keys, q_ref[0, rows, :])
            if masked:
                scores = jnp.where(ok, scores, NEGATIVE)
            old = top_ref[h:h + 1, :]
            new = jnp.maximum(old, jnp.max(scores, axis=0, keepdims=True))
            weights = jnp.exp(scores - new)
            factor = jnp.exp(old - new)
            top_ref[h:h + 1, :] = new
            total_ref[h:h + 1, :] = total_ref[h:h + 1, :] * factor + jnp.sum(weights, axis=0, keepdims=True)
            acc_ref[rows, :] = acc_ref[rows, :] * factor + dot(values, weights.astype(BF))

    block(0, True)

    @pl.loop(1, count)
    def _(s):
        masked = last_first > place - s * tokens

        @pl.when(masked)
        def _():
            block(s, True)

        @pl.when(jnp.logical_not(masked))
        def _():
            block(s, False)

    lse_ref[0] = top_ref[...] + jnp.log(total_ref[...])
    for h in range(heads):
        rows = slice(h * HD, (h + 1) * HD)
        acc_ref[rows, :] = acc_ref[rows, :] / total_ref[h:h + 1, :]
    out_ref[0] = acc_ref[...].T.astype(BF)

def attend(info, q, kv, first):
    seqs, width, tokens = q.shape
    n = kv.shape[0]
    heads = width // HD
    pad = -(-heads // 8) * 8
    per = lambda r, c: pl.BlockSpec((1, r, c), lambda s, i: (s, 0, 0))
    return pl.pallas_call(
        attend_kernel,
        grid_spec=pltpu.PrefetchScalarGridSpec(
            num_scalar_prefetch=1, grid=(seqs,),
            in_specs=[per(width, tokens), pl.BlockSpec((n, 1, tokens, 2 * HD), lambda s, i: (0, s, 0, 0)), per(1, tokens)],
            out_specs=[per(tokens, width), per(pad, tokens)],
            scratch_shapes=[pltpu.VMEM((pad, tokens), F32), pltpu.VMEM((pad, tokens), F32), pltpu.VMEM((width, tokens), F32)]),
        out_shape=[jax.ShapeDtypeStruct((seqs, tokens, width), BF), jax.ShapeDtypeStruct((seqs, pad, tokens), F32)],
        cost_estimate=pl.CostEstimate(flops=8 * seqs * tokens * tokens * width * 2, transcendentals=seqs * heads * tokens * tokens * 2, bytes_accessed=8 * seqs * tokens * width),
        name="attend")(info, q, kv, first)

def attend_back_kernel(info_ref, grad_ref, w_ref, att_ref, q_ref, kv_ref, lse_ref, first_ref, cos_ref, sin_ref,
                       gq_ref, own_ref, sent_ref, bias_ref, gt_ref, qn_ref, gn_ref, term_ref, gacc_ref):
    seq = pl.program_id(0)
    tokens = q_ref.shape[2]
    heads = q_ref.shape[1] // HD
    place = info_ref[0]
    count, last_first = info_ref[1 + 2 * seq], info_ref[2 + 2 * seq]
    gt_ref[...] = dot_nt(w_ref[...], grad_ref[0]).astype(BF)
    att = att_ref[0].astype(F32).T
    for h in range(heads):
        rows = slice(h * HD, (h + 1) * HD)
        grad = gt_ref[rows, :].astype(F32)
        term_ref[h:h + 1, :] = jnp.sum(grad * att[rows], axis=0, keepdims=True)
        gn_ref[h] = grad.T.astype(BF)
        qn_ref[h] = q_ref[0, rows, :].astype(F32).T.astype(BF)
    gacc_ref[...] = jnp.zeros_like(gacc_ref)

    def block(s, masked):
        pair = kv_ref[s, 0]
        keys, values = pair[:, :HD], pair[:, HD:]
        keys_t = pair.T[:HD]
        ok = allowed_of(first_ref, place, s, tokens) if masked else None
        grad_key = jnp.zeros((tokens, HD), F32)
        grad_value = jnp.zeros((tokens, HD), F32)
        for h in range(heads):
            rows = slice(h * HD, (h + 1) * HD)
            scores = dot(keys, q_ref[0, rows, :])
            probs = jnp.exp(scores - lse_ref[0, h:h + 1, :])
            if masked:
                probs = jnp.where(ok, probs, 0.0)
            grad_probs = dot(values, gt_ref[rows, :])
            grad_scores = (probs * (grad_probs - term_ref[h:h + 1, :])).astype(BF)
            grad_value = grad_value + dot(probs.astype(BF), gn_ref[h])
            grad_key = grad_key + dot(grad_scores, qn_ref[h])
            gacc_ref[rows, :] = gacc_ref[rows, :] + dot(keys_t, grad_scores)
        return jnp.concatenate([grad_key, grad_value], axis=1)

    own_ref[0] = block(0, True)

    @pl.loop(1, sent_ref.shape[0] + 1)
    def _(s):
        masked = last_first > place - s * tokens

        @pl.when(s >= count)
        def _():
            sent_ref[s - 1, 0] = jnp.zeros((tokens, 2 * HD), BF)

        @pl.when((s < count) & masked)
        def _():
            sent_ref[s - 1, 0] = block(s, True).astype(BF)

        @pl.when((s < count) & jnp.logical_not(masked))
        def _():
            sent_ref[s - 1, 0] = block(s, False).astype(BF)

    cosine, sine = cos_ref[0], sin_ref[0]
    for h in range(heads):
        rows = slice(h * HD, (h + 1) * HD)
        gacc_ref[rows, :] = turn_back(gacc_ref[rows, :] * SCALE, cosine, sine)
    out = gacc_ref[...].T
    gq_ref[0] = out.astype(BF)
    bias_ref[0] = jnp.sum(out, axis=0, keepdims=True)

def attend_back(info, grad, w, att, q, kv, lse, first, cosine, sine):
    seqs, width, tokens = q.shape
    model = grad.shape[-1]
    n = kv.shape[0]
    heads = width // HD
    pad = lse.shape[1]
    half = cosine.shape[1]
    per = lambda r, c: pl.BlockSpec((1, r, c), lambda s, i: (s, 0, 0))
    blocks = lambda k: pl.BlockSpec((k, 1, tokens, 2 * HD), lambda s, i: (0, s, 0, 0))
    return pl.pallas_call(
        attend_back_kernel,
        grid_spec=pltpu.PrefetchScalarGridSpec(
            num_scalar_prefetch=1, grid=(seqs,),
            in_specs=[per(tokens, model), pl.BlockSpec(w.shape, lambda s, i: (0, 0)), per(tokens, width), per(width, tokens),
                      blocks(n), per(pad, tokens), per(1, tokens), per(half, tokens), per(half, tokens)],
            out_specs=[per(tokens, width), per(tokens, 2 * HD), blocks(n - 1), per(1, width)],
            scratch_shapes=[pltpu.VMEM((width, tokens), BF), pltpu.VMEM((heads, tokens, HD), BF), pltpu.VMEM((heads, tokens, HD), BF),
                            pltpu.VMEM((pad, tokens), F32), pltpu.VMEM((width, tokens), F32)]),
        out_shape=[jax.ShapeDtypeStruct((seqs, tokens, width), BF), jax.ShapeDtypeStruct((seqs, tokens, 2 * HD), F32),
                   jax.ShapeDtypeStruct((n - 1, seqs, tokens, 2 * HD), BF), jax.ShapeDtypeStruct((seqs, 1, width), F32)],
        cost_estimate=pl.CostEstimate(flops=20 * seqs * tokens * tokens * width * 2, transcendentals=seqs * heads * tokens * tokens * 2, bytes_accessed=16 * seqs * tokens * width),
        name="attend_back")(info, grad, w, att, q, kv, lse, first, cosine, sine)


def to_bf16(values):
    return values.astype(jnp.bfloat16)


def tp_other(values):
    return lax.ppermute(values, "tp", [(0, 1), (1, 0)])


def tp_sum(values):
    mine = to_bf16(values)
    return mine.astype(jnp.float32) + tp_other(mine).astype(jnp.float32)


def core_other(values):
    pairs = [(i, i ^ 1) for i in range(lax.axis_size("dp"))]
    return lax.ppermute(values, "dp", pairs)


def earlier(values, shift):
    n = lax.axis_size("ctx")
    return lax.ppermute(values, "ctx", [(i, i + shift) for i in range(n - shift)])


def later(values, shift):
    n = lax.axis_size("ctx")
    return lax.ppermute(values, "ctx", [(i + shift, i) for i in range(n - shift)])


def line_sum(part):
    n = lax.axis_size("ctx")
    half = n // 2
    me = lax.axis_index("ctx")
    for step in range(half - 1):
        pairs = [(step, step + 1), (n - 1 - step, n - 2 - step)]
        part = part + lax.ppermute(to_bf16(part), "ctx", pairs).astype(jnp.float32)
    mine = to_bf16(part)
    moved = lax.ppermute(mine, "ctx", [(half - 1, half), (half, half - 1)])
    total = to_bf16(mine.astype(jnp.float32) + moved.astype(jnp.float32))
    for step in reversed(range(half - 1)):
        pairs = [(step + 1, step), (n - 2 - step, n - 1 - step)]
        moved = lax.ppermute(total, "ctx", pairs)
        total = jnp.where((me == step) | (me == n - 1 - step), moved, total)
    return total.astype(jnp.float32)


def quarter_grads(make, wide):
    n_dp = lax.axis_size("dp")
    rows = n_dp // 2
    me = lax.axis_index("dp")
    row, core = me // 2, me % 2
    split = wide.reshape(wide.shape[0], rows, 2, wide.shape[1] // n_dp)
    mine = lax.dynamic_index_in_dim(split, core, 2, keepdims=False)
    theirs = core_other(lax.dynamic_index_in_dim(split, 1 - core, 2, keepdims=False))
    both = jnp.concatenate([mine, theirs], axis=0)

    def columns(which):
        return lax.dynamic_index_in_dim(both, which, 1, keepdims=False)

    total = None
    for shift in range(1, rows):
        part = to_bf16(make(columns((row + shift) % rows)))
        pairs = [(r * 2 + c, ((r + shift) % rows) * 2 + c) for r in range(rows) for c in range(2)]
        moved = lax.ppermute(part, "dp", pairs).astype(jnp.float32)
        total = moved if total is None else total + moved
    own = make(columns(row))
    return own if total is None else own + total


def both_cores(values):
    return jnp.concatenate([values, core_other(values)], axis=0)


def inverse_rms(values):
    return lax.rsqrt(jnp.mean(values * values, axis=-1, keepdims=True) + EPS)


def norm_back(grad_h, normed, scale, gain):
    upstream = grad_h * gain
    inner = jnp.mean(upstream * normed, axis=-1, keepdims=True)
    return scale * (upstream - normed * inner)


def shards(
    block_input,
    positions,
    gain_attn,
    w_qkv,
    b_qkv,
    w_out,
    gain_mlp,
    w_gate,
    w_up,
    w_down,
    cotangent,
):
    seqs, tokens, _ = block_input.shape
    flat = seqs * tokens
    heads_width = w_out.shape[1]
    n_ctx = lax.axis_size("ctx")
    me = lax.axis_index("ctx")
    first_token = me * tokens
    proj_qkv = w_qkv[:, 0, :]
    proj_out = w_out[0]
    other_qkv = tp_other(proj_qkv)
    other_out = tp_other(proj_out)
    half = HD // 2
    freq = THETA ** (-(jnp.arange(half, dtype=jnp.float32) * 2.0) / HD)
    angle = positions.astype(jnp.float32)[:, None, :] * freq[None, :, None]
    cosine, sine = jnp.cos(angle), jnp.sin(angle)
    token_index = first_token + jnp.arange(tokens, dtype=jnp.int32)
    query_first = token_index[None, :] - positions
    counts = me - query_first[:, 0] // tokens + 1
    info = jnp.concatenate(
        [first_token[None], jnp.stack([counts, query_first[:, -1]], axis=1).reshape(-1)]
    ).astype(jnp.int32)
    query_first = query_first[:, None, :]

    hidden_one, queries, key_value = project(
        block_input, gain_attn[None, :], proj_qkv, b_qkv, cosine, sine, heads_width
    )
    pairs = jnp.stack([key_value] + [earlier(key_value, shift) for shift in range(1, n_ctx)])
    grad_act = jnp.einsum("std,fd->stf", cotangent, w_down, preferred_element_type=jnp.float32)
    attended, lse = attend(info, queries, pairs, query_first)
    inputs = block_input.astype(jnp.float32)
    attn_mine = jnp.einsum(
        "ste,ed->std", attended, proj_out, preferred_element_type=jnp.float32
    )
    attn_other = jnp.einsum(
        "ste,ed->std", tp_other(attended), other_out, preferred_element_type=jnp.float32
    )
    middle = inputs + (attn_mine + attn_other)
    scale_two = inverse_rms(middle)
    normed_two = middle * scale_two
    hidden_two = (normed_two * gain_mlp).astype(jnp.bfloat16)
    gate = jnp.einsum("std,df->stf", hidden_two, w_gate, preferred_element_type=jnp.float32)
    up = jnp.einsum("std,df->stf", hidden_two, w_up, preferred_element_type=jnp.float32)
    sigma = jax.nn.sigmoid(gate)
    activated = (gate * sigma * up).astype(jnp.bfloat16)
    mlp_part = jnp.einsum("stf,fd->std", activated, w_down, preferred_element_type=jnp.float32)
    output = (middle + tp_sum(mlp_part)).astype(jnp.bfloat16)
    grad_gate_in = (grad_act * up * sigma * (1.0 + gate * (1.0 - sigma))).astype(jnp.bfloat16)
    grad_up_in = (grad_act * gate * sigma).astype(jnp.bfloat16)
    acts = both_cores(activated.reshape(flat, -1))
    gates = both_cores(grad_gate_in.reshape(flat, -1))
    ups = both_cores(grad_up_in.reshape(flat, -1))
    grad_down = quarter_grads(
        lambda cols: jnp.einsum("tf,td->fd", acts, cols, preferred_element_type=jnp.float32),
        cotangent.reshape(flat, -1),
    )
    hidden_flat = hidden_two.reshape(flat, -1)
    grad_gate = quarter_grads(
        lambda cols: jnp.einsum("td,tf->df", cols, gates, preferred_element_type=jnp.float32),
        hidden_flat,
    )
    grad_up = quarter_grads(
        lambda cols: jnp.einsum("td,tf->df", cols, ups, preferred_element_type=jnp.float32),
        hidden_flat,
    )
    grad_down = line_sum(grad_down)
    grad_gate = line_sum(grad_gate)
    grad_up = line_sum(grad_up)
    back_two = jnp.einsum("stf,df->std", grad_gate_in, w_gate, preferred_element_type=jnp.float32)
    back_two = back_two + jnp.einsum(
        "stf,df->std", grad_up_in, w_up, preferred_element_type=jnp.float32
    )
    back_two = tp_sum(back_two)
    grad_gain_mlp = jnp.sum(back_two * normed_two, axis=(0, 1))
    grad_middle = cotangent.astype(jnp.float32) + norm_back(
        back_two, normed_two, scale_two, gain_mlp
    )
    grad_middle_b = grad_middle.astype(jnp.bfloat16)
    att_both = both_cores(attended.reshape(flat, -1))
    grad_out = quarter_grads(
        lambda cols: jnp.einsum("te,td->ed", att_both, cols, preferred_element_type=jnp.float32),
        grad_middle_b.reshape(flat, -1),
    )
    grad_out = line_sum(grad_out)[None]

    grad_q, grad_own, grad_sent, bias_q = attend_back(
        info, grad_middle_b, proj_out, attended, queries, pairs, lse, query_first, cosine, sine
    )
    grad_pairs = grad_own
    for shift in range(1, n_ctx):
        grad_pairs = grad_pairs + later(grad_sent[shift - 1], shift).astype(jnp.float32)
    cos_rows, sin_rows = jnp.swapaxes(cosine, 1, 2), jnp.swapaxes(sine, 1, 2)
    one, two = grad_pairs[..., :half], grad_pairs[..., half:HD]
    grad_kv = jnp.concatenate(
        [one * cos_rows + two * sin_rows, two * cos_rows - one * sin_rows, grad_pairs[..., HD:]],
        axis=-1,
    )
    grad_bias = jnp.concatenate([jnp.sum(bias_q, axis=(0, 1)), jnp.sum(grad_kv, axis=(0, 1))])
    grad_joined_b = jnp.concatenate([grad_q, to_bf16(grad_kv)], axis=-1)
    joined_both = both_cores(grad_joined_b.reshape(flat, -1))
    grad_qkv = quarter_grads(
        lambda cols: jnp.einsum("td,te->de", cols, joined_both, preferred_element_type=jnp.float32),
        hidden_one.reshape(flat, -1),
    )
    grad_qkv = line_sum(grad_qkv)[:, None, :]
    back_mine = jnp.einsum(
        "ste,de->std", grad_joined_b, proj_qkv, preferred_element_type=jnp.float32
    )
    back_other = jnp.einsum(
        "ste,de->std", tp_other(grad_joined_b), other_qkv, preferred_element_type=jnp.float32
    )
    back_one = back_mine + back_other
    scale_one = inverse_rms(inputs)
    normed_one = inputs * scale_one
    grad_gain_attn = jnp.sum(back_one * normed_one, axis=(0, 1))
    grad_input = grad_middle + norm_back(back_one, normed_one, scale_one, gain_attn)
    small = lax.psum((grad_gain_attn, grad_bias, grad_gain_mlp), ("dp", "ctx"))
    n_dp = lax.axis_size("dp")
    small = [
        lax.dynamic_slice_in_dim(v, lax.axis_index("dp") * (v.shape[0] // n_dp), v.shape[0] // n_dp)
        for v in small
    ]
    return (
        output,
        grad_input,
        small[0],
        grad_qkv,
        small[1][None],
        grad_out,
        small[2],
        grad_gate,
        grad_up,
        grad_down,
    )


def solution(mesh):
    in_specs = (
        P("dp", "ctx", None),
        P("dp", "ctx"),
        P(),
        P(None, "tp", None),
        P("tp", None),
        P("tp", None, None),
        P(),
        P(None, "tp"),
        P(None, "tp"),
        P("tp", None),
        P("dp", "ctx", None),
    )
    out_specs = (
        P("dp", "ctx", None),
        P("dp", "ctx", None),
        P("dp"),
        P("dp", "tp", None),
        P("tp", "dp"),
        P("tp", None, "dp"),
        P("dp"),
        P("dp", "tp"),
        P("dp", "tp"),
        P("tp", "dp"),
    )
    return jax.shard_map(shards, mesh=mesh, in_specs=in_specs, out_specs=out_specs, check_vma=False)
```

time: 914 us -> 658 us (0.72)
  waiting for transfers between devices: 383 us -> 214 us
  local copies, waits for them, and re-layouts: 189 us -> 118 us
  matrix products: 174 us -> 122 us
  Pallas kernels: 0 us -> 33.2 us
  other arithmetic: 53.5 us -> 31.5 us
  blocking collectives: 61 us -> 78.1 us
  starting transfers between devices: 45.6 us -> 58.1 us
    ppermute x3, waiting for transfers between devices: 184 us -> 28 us  [later(): lax.ppermute(values, 'ctx', [(i + shift, i) for i in range(n - shift)])]
    dot_general x11 -> x2, matrix products: 59.2 us -> 5.68 us  [the longest x1 3.15 us: shards(): jnp.einsum('ste,ed->std', tp_other(attended), other_out, preferred_elemen...]
    pallas_call x0 -> x3, Pallas kernels: none -> 33.2 us  [the longest x1 16.9 us: attend_back(): pl.pallas_call(attend_back_kernel, grid_spec=pltpu.PrefetchScalarGridSpec...]
    ppermute x6, waiting for transfers between devices: 58.1 us -> 32.8 us  [tp_other(): return lax.ppermute(values, 'tp', [(0, 1), (1, 0)])]
    unnamed x129 -> x122, local copies, waits for them, and re-layouts: 70.2 us -> 50.9 us
    psum x1, blocking collectives: 61 us -> 78.1 us  [shards(): small = lax.psum((grad_gain_attn, grad_bias, grad_gain_mlp), ('dp', 'ctx'))]
    another operation x7 -> x0, local copies, waits for them, and re-layouts: 15.6 us -> none
    slice x5 -> x1, local copies, waits for them, and re-layouts: 12.7 us -> 0.2 us  [shards(): grad_pairs[..., HD:]]
  transfers between devices with their start and end apart: 41 -> 41, of which waited for: 14 -> 18; matrix products, arithmetic and copies ran while one was open for 44% -> 33% of each run, Pallas kernels for 0% -> 4%
where the time goes in v2:
time: 658 us
  waiting for transfers between devices  214 us (33%)
  matrix products  122 us (19%)
  local copies, waits for them, and re-layouts  118 us (18%)
  blocking collectives  78.1 us (12%)
  starting transfers between devices  58.1 us (9%)
  Pallas kernels  33.2 us (5%)
  other arithmetic  31.5 us (5%)
    psum x1, blocking collectives, shards(): small = lax.psum((grad_gain_attn, grad_bias, grad_gain_mlp), ('dp', 'ctx'))  78.1 us
    ppermute x5, waiting for transfers between devices, line_sum(): moved = lax.ppermute(total, 'ctx', pairs)  67.4 us
    ppermute x5, waiting for transfers between devices, quarter_grads(): moved = lax.ppermute(part, 'dp', pairs).astype(jnp.float32)  52.8 us
    unnamed x122, local copies, waits for them, and re-layouts  50.9 us
    ppermute x6, waiting for transfers between devices, tp_other(): return lax.ppermute(values, 'tp', [(0, 1), (1, 0)])  32.8 us
    another operation x4, local copies, waits for them, and re-layouts, quarter_grads(): split = wide.reshape(wide.shape[0], rows, 2, wide.shape[1] // n_dp)  28.9 us
    ppermute x3, waiting for transfers between devices, later(): lax.ppermute(values, 'ctx', [(i + shift, i) for i in range(n - shift)])  28 us
    dynamic_slice x3, local copies, waits for them, and re-layouts, quarter_grads(): lax.dynamic_index_in_dim(split, 1 - core, 2, keepdims=False)  24.8 us
  transfers between devices with their start and end apart: 41, of which 18 were waited for; matrix products, arithmetic and copies ran while one was open for 33% of the time, Pallas kernels for 4%

profile of v2, /device:TPU:0, one launch (start us, length us, event | category | flops | bytes accessed | tf_op | source)
XLA Modules:
  0.0 657.7 jit_solution(1542672067636819659)
XLA Ops:
  37.6 11.3 %attend.1 = (bf16[2,512,448]{2,1,0:T(8,128)(2,1)}, f32[2,8,512]{2,1,0:T(8,128)}) custom-call(s32[5]{0:T(128)} %pad_add_fusion.1.info_ref, bf16[2,448,512]{2,1,0:T(8,128)(2,1)} %get-tuple-element.19.q_ref, bf16[4,2,512,128]{3,2,1,0:T(8,128)(2,1)} %pad_maximum_fusion.32.kv_ref, s32[2,1,512]{2,1,0:T(1,128)} %broadcast_in_dim.36.first_ref), custom_call_target="tpu_custom_call" | custom-call | flops 3758096384 | bytes 3670016 | tf_op jit(solution)/shard_map/attend/pallas_call | solution.py:118
  52.6 10.5 %fusion.9 = f32[2,512,2432]{2,1,0:T(8,128)} fusion(bf16[2,512,896]{2,1,0:T(8,128)(2,1)S(1)} %copy-done.6, bf16[2432,896]{1,0:T(8,128)(2,1)} %param.20), kind=kOutput, calls=%fused_computation.19 | convolution fusion | flops 4462739456 | bytes 16154624 | tf_op jit(solution)/shard_map/std,fd->stf/dot_general | solution.py:337
  63.1 8.4 %reshape.91 = bf16[1024,2,2,224]{3,2,1,0:T(2,128)(2,1)S(1)} reshape(bf16[2,512,896]{2,1,0:T(8,128)(2,1)} %get-tuple-element.26) | data formatting | bytes 3670016 | tf_op jit(solution)/shard_map/reshape;reshape | solution.py:266
  79.5 7.9 %fusion.15 = f32[2,512,2432]{2,1,0:T(8,128)} fusion(bf16[2,512,896]{2,1,0:T(8,128)(2,1)S(1)} %multiply_convert_fusion.3, bf16[896,2432]{1,0:T(8,128)(2,1)S(1)} %bitcast.155), kind=kOutput, calls=%fused_computation.25 | convolution fusion | flops 4462739456 | bytes 16154624 | tf_op jit(solution)/shard_map/std,df->stf/dot_general | solution.py:351
  87.5 17.2 %multiply_convert_fusion.1 = (bf16[2,512,2432]{2,1,0:T(8,128)(2,1)}, bf16[2,512,2432]{2,1,0:T(8,128)(2,1)}, bf16[2,512,2432]{2,1,0:T(8,128)(2,1)}) fusion(f32[2,512,2432]{2,1,0:T(8,128)} %fusion.9, f32[2,512,2432]{2,1,0:T(8,128)} %fusion.15, bf16[2,512,896]{2,1,0:T(8,128)(2,1)S(1)} %multiply_convert_fusion.3, bf16[896,2432]{1,0:T(8,128)(2,1)} %param.18), kind=kOutput, calls=%fused_computation.4 | convolution fusion | flops 4502585344 | bytes 41058304 | tf_op jit(solution)/shard_map/std,df->stf/dot_general | solution.py:350
  112.3 8.9 %add_convert_fusion = bf16[2,512,896]{2,1,0:T(8,128)(2,1)} fusion(f32[2,512,896]{2,1,0:T(8,128)S(1)} %fusion.13, bf16[2,512,2432]{2,1,0:T(8,128)(2,1)S(1)} %copy-done.45, bf16[896,2432]{1,0:T(8,128)(2,1)} %param.18), kind=kOutput, calls=%fused_computation.47 | convolution fusion | flops 4464574464 | bytes 14843904 | tf_op jit(solution)/shard_map/stf,df->std/dot_general | solution.py:377
  145.3 8.3 %reshape.93 = bf16[1024,2,2,224]{3,2,1,0:T(2,128)(2,1)S(1)} reshape(bf16[2,512,896]{2,1,0:T(8,128)(2,1)} %copy-done.13) | data formatting | bytes 3670016 | tf_op jit(solution)/shard_map/reshape;reshape | solution.py:266
  153.6 9.7 %fusion.36 = bf16[2,512,896]{2,1,0:T(8,128)(2,1)} fusion(bf16[2,512,2432]{2,1,0:T(8,128)(2,1)} %get-tuple-element.76, bf16[2432,896]{1,0:T(8,128)(2,1)} %param.20), kind=kOutput, calls=%fused_computation.77 | convolution fusion | flops 4463656960 | bytes 11173888 | tf_op jit(solution)/shard_map/stf,fd->std/dot_general | solution.py:354
  171.4 9.0 %reshape.92 = bf16[1024,2,2,224]{3,2,1,0:T(2,128)(2,1)} reshape(bf16[2,512,896]{2,1,0:T(8,128)(2,1)} %fusion.99.grad_ref) | data formatting | bytes 3670016 | tf_op jit(solution)/shard_map/reshape;reshape | solution.py:266
  180.4 16.9 %attend_back.1 = (bf16[2,512,448]{2,1,0:T(8,128)(2,1)}, f32[2,512,128]{2,1,0:T(8,128)}, bf16[3,2,512,128]{3,2,1,0:T(8,128)(2,1)}, f32[2,1,448]{2,1,0:T(1,128)}) custom-call(s32[5]{0:T(128)} %pad_add_fusion.1.info_ref, bf16[2,512,896]{2,1,0:T(8,128)(2,1)} %fusion.99.grad_ref, bf16[448,896]{1,0:T(8,128)(2,1)} %bitcast.6.w_ref, ...), custom_call_target="tpu_custom_call" | custom-call | flops 9395240960 | bytes 7340032 | tf_op jit(solution)/shard_map/attend_back/pallas_call | solution.py:201
  203.2 12.2 %constant_dynamic-slice_fusion = (bf16[1024,2,1,224]{3,2,1,0:T(2,128)(2,1)}, bf16[1024,2,1,224]{3,2,1,0:T(2,128)(2,1)}, bf16[1024,2,1,224]{3,2,1,0:T(2,128)(2,1)}, bf16[1024,2,1,224]{3,2,1,0:T(2,128)(2,1)}) fusion(bf16[1024,2,2,224]{3,2,1,0:T(2,128)(2,1)} %reshape.94, s32[]{:T(128)S(6)} %select_n.119, s32[]{:T(128)S(6)} %select_n.118, ...), kind=kLoop, calls=%fused_computation.134 | loop fusion | bytes 7340040 | tf_op jit(solution)/shard_map/jit(dynamic_index_in_dim)/dynamic_slice | solution.py:268
  221.2 17.0 %collective-permute-done.9 = bf16[2,512,128]{2,1,0:T(8,128)(2,1)S(1)} collective-permute-done((bf16[2,512,128]{2,1,0:T(8,128)(2,1)}, bf16[2,512,128]{2,1,0:T(8,128)(2,1)S(1)}, u32[]{:S(2)}, u32[]{:S(2)}) %collective-permute-start.9) | collective-permute-done | bytes 262176 | tf_op jit(solution)/shard_map/ppermute | solution.py:241
  238.2 11.1 %collective-permute-done.8 = bf16[2,512,128]{2,1,0:T(8,128)(2,1)S(1)} collective-permute-done((bf16[2,512,128]{2,1,0:T(8,128)(2,1)}, bf16[2,512,128]{2,1,0:T(8,128)(2,1)S(1)}, u32[]{:S(2)}, u32[]{:S(2)}) %collective-permute-start.8) | collective-permute-done | bytes 262176 | tf_op jit(solution)/shard_map/ppermute | solution.py:241
  328.1 10.3 %collective-permute-done.10 = bf16[2,512,576]{1,2,0:T(8,128)(2,1)S(1)} collective-permute-done((bf16[2,512,576]{1,2,0:T(8,128)(2,1)S(1)}, bf16[2,512,576]{1,2,0:T(8,128)(2,1)S(1)}, u32[]{:S(2)}, u32[]{:S(2)}) %collective-permute-start.10) | collective-permute-done | bytes 1179680 | tf_op jit(solution)/shard_map/ppermute | solution.py:221
  354.3 22.5 %collective-permute-done.5 = bf16[2,512,896]{2,1,0:T(8,128)(2,1)S(1)} collective-permute-done((bf16[2,512,896]{2,1,0:T(8,128)(2,1)S(1)}, bf16[2,512,896]{2,1,0:T(8,128)(2,1)S(1)}, u32[]{:S(2)}, u32[]{:S(2)}) %collective-permute-start.5) | collective-permute-done | bytes 1835040 | tf_op jit(solution)/shard_map/ppermute | solution.py:221
  384.3 78.1 %all-reduce = (f32[896]{0:T(1024)}, f32[576]{0:T(1024)}, f32[896]{0:T(1024)}) all-reduce(f32[896]{0:T(1024)} %get-tuple-element.70, f32[576]{0:T(1024)} %pad_maximum_fusion.34, f32[896]{0:T(1024)} %get-tuple-element.68), channel_id=1, replica_groups=mesh['dp'=4,'ctx'=4,'tp'=2] {'dp','ctx'}, use_global_device_ids=true, to_apply=%region_5.6 | all-reduce | flops 2368 | bytes 18944 | tf_op jit(solution)/shard_map/psum | solution.py:425
  476.4 7.7 %fusion.25 = bf16[224,2432]{1,0:T(8,128)(2,1)} fusion(bf16[1024,2432]{1,0:T(8,128)(2,1)} %collective-permute-done.30, bf16[1024,2432]{1,0:T(8,128)(2,1)} %bitcast.145, s32[]{:T(128)S(6)} %select_n.123, bf16[1024,2,224]{0,2,1:T(8,128)(2,1)S(1)} %bitcast.124, bf16[1024,2,224]{0,2,1:T(8,128)(2,1)} %collective-permute-done.24), kind=kOutput, calls=%fused_computation.35 | convolution fusion | flops 2253672448 | bytes 12886020 | tf_op jit(solution)/shard_map/td,tf->df/dot_general | solution.py:371
  492.3 11.1 %collective-permute-done.26 = bf16[224,2432]{1,0:T(8,128)(2,1)} collective-permute-done((bf16[224,2432]{1,0:T(8,128)(2,1)S(1)}, bf16[224,2432]{1,0:T(8,128)(2,1)}, u32[]{:S(2)}, u32[]{:S(2)}) %collective-permute-start.26) | collective-permute-done | bytes 1089568 | tf_op jit(solution)/shard_map/ppermute | solution.py:278
  510.2 16.5 %collective-permute-done.31 = bf16[224,2432]{1,0:T(8,128)(2,1)S(1)} collective-permute-done((bf16[224,2432]{1,0:T(8,128)(2,1)}, bf16[224,2432]{1,0:T(8,128)(2,1)S(1)}, u32[]{:S(2)}, u32[]{:S(2)}) %collective-permute-start.31) | collective-permute-done | bytes 1089568 | tf_op jit(solution)/shard_map/ppermute | solution.py:278
  533.4 16.1 %collective-permute-done.37 = bf16[2432,224]{0,1:T(8,128)(2,1)S(1)} collective-permute-done((bf16[2432,224]{0,1:T(8,128)(2,1)S(1)}, bf16[2432,224]{0,1:T(8,128)(2,1)S(1)}, u32[]{:S(2)}, u32[]{:S(2)}) %collective-permute-start.37) | collective-permute-done | bytes 1089568 | tf_op jit(solution)/shard_map/ppermute | solution.py:278
  558.4 21.4 %collective-permute-done.38 = bf16[2432,224]{0,1:T(8,128)(2,1)S(1)} collective-permute-done((bf16[2432,224]{0,1:T(8,128)(2,1)S(1)}, bf16[2432,224]{0,1:T(8,128)(2,1)S(1)}, u32[]{:S(2)}, u32[]{:S(2)}) %collective-permute-start.38) | collective-permute-done | bytes 1089568 | tf_op jit(solution)/shard_map/ppermute | solution.py:250
  585.5 25.3 %collective-permute-done.29 = bf16[224,2432]{1,0:T(8,128)(2,1)S(1)} collective-permute-done((bf16[224,2432]{1,0:T(8,128)(2,1)S(1)}, bf16[224,2432]{1,0:T(8,128)(2,1)S(1)}, u32[]{:S(2)}, u32[]{:S(2)}) %collective-permute-start.29) | collective-permute-done | bytes 1089568 | tf_op jit(solution)/shard_map/ppermute | solution.py:256
  612.3 21.9 %collective-permute-done.34 = bf16[224,2432]{1,0:T(8,128)(2,1)S(1)} collective-permute-done((bf16[224,2432]{1,0:T(8,128)(2,1)S(1)}, bf16[224,2432]{1,0:T(8,128)(2,1)S(1)}, u32[]{:S(2)}, u32[]{:S(2)}) %collective-permute-start.34) | collective-permute-done | bytes 1089568 | tf_op jit(solution)/shard_map/ppermute | solution.py:256
  635.7 20.2 %collective-permute-done.40 = bf16[2432,224]{0,1:T(8,128)(2,1)S(1)} collective-permute-done((bf16[2432,224]{0,1:T(8,128)(2,1)S(1)}, bf16[2432,224]{0,1:T(8,128)(2,1)S(1)}, u32[]{:S(2)}, u32[]{:S(2)}) %collective-permute-start.40) | collective-permute-done | bytes 1089568 | tf_op jit(solution)/shard_map/ppermute | solution.py:256
  (266 shorter events, 256.3 us)
Async XLA Ops:
  22.3 51.7 %collective-permute-start.4 = (bf16[448,896]{1,0:T(8,128)(2,1)}, bf16[448,896]{1,0:T(8,128)(2,1)}, u32[]{:S(2)}, u32[]{:S(2)}) collective-permute-start(bf16[448,896]{1,0:T(8,128)(2,1)} %bitcast.6.w_ref), channel_id=1, source_target_pairs={{0,1},{1,0},{2,3},{3,2},{4,5},{5,4},{6,7},{7,6},{8,9},{9,8},{10,11... | collective-permute-start | bytes 2408456 | tf_op jit(solution)/shard_map/ppermute | solution.py:221
  121.2 42.2 %collective-permute-start.6 = (bf16[2,512,896]{2,1,0:T(8,128)(2,1)}, bf16[2,512,896]{2,1,0:T(8,128)(2,1)}, u32[]{:S(2)}, u32[]{:S(2)}) collective-permute-start(bf16[2,512,896]{2,1,0:T(8,128)(2,1)} %add_convert_fusion), channel_id=1, source_target_pairs={{0,1},{1,0},{2,3},{3,2},{4,5},{5,4},{6,7},{7,6},{8,9},{9,8},{10,11... | collective-permute-start | bytes 5505032 | tf_op jit(solution)/shard_map/ppermute | solution.py:221
  134.0 157.2 %collective-permute-start.12 = (bf16[1024,2,224]{0,2,1:T(8,128)(2,1)}, bf16[1024,2,224]{0,2,1:T(8,128)(2,1)}, u32[]{:S(2)}, u32[]{:S(2)}) collective-permute-start(bf16[1024,2,224]{0,2,1:T(8,128)(2,1)} %bitcast.129), channel_id=1, source_target_pairs={{0,8},{8,0},{16,24},{24,16},{1,9},{9,1},{17,25},{25,17},{2,10},{10... | collective-permute-start | bytes 2752520 | tf_op jit(solution)/shard_map/ppermute | solution.py:231
  144.8 142.3 %collective-permute-start.18 = (bf16[1024,448]{0,1:T(8,128)(2,1)}, bf16[1024,448]{0,1:T(8,128)(2,1)}, u32[]{:S(2)}, u32[]{:S(2)}) collective-permute-start(bf16[1024,448]{0,1:T(8,128)(2,1)} %copy.65), channel_id=1, source_target_pairs={{0,8},{8,0},{16,24},{24,16},{1,9},{9,1},{17,25},{25,17},{2,10},{10... | collective-permute-start | bytes 2752520 | tf_op jit(solution)/shard_map/ppermute | solution.py:231
  199.3 38.9 %collective-permute-start.9 = (bf16[2,512,128]{2,1,0:T(8,128)(2,1)}, bf16[2,512,128]{2,1,0:T(8,128)(2,1)S(1)}, u32[]{:S(2)}, u32[]{:S(2)}) collective-permute-start(bf16[2,512,128]{2,1,0:T(8,128)(2,1)} %get-tuple-element.89), channel_id=1, source_target_pairs={{6,0},{7,1},{14,8},{15,9},{22,16},{23,17},{30,24},{31,25}} | collective-permute-start | bytes 786440 | tf_op jit(solution)/shard_map/ppermute | solution.py:241
  200.6 48.7 %collective-permute-start.8 = (bf16[2,512,128]{2,1,0:T(8,128)(2,1)}, bf16[2,512,128]{2,1,0:T(8,128)(2,1)S(1)}, u32[]{:S(2)}, u32[]{:S(2)}) collective-permute-start(bf16[2,512,128]{2,1,0:T(8,128)(2,1)} %get-tuple-element.90), channel_id=1, source_target_pairs={{4,0},{6,2},{5,1},{7,3},{12,8},{14,10},{13,9},{15,11},{20,16},{22,... | collective-permute-start | bytes 786440 | tf_op jit(solution)/shard_map/ppermute | solution.py:241
  201.9 47.4 %collective-permute-start.7 = (bf16[2,512,128]{2,1,0:T(8,128)(2,1)}, bf16[2,512,128]{2,1,0:T(8,128)(2,1)S(1)}, u32[]{:S(2)}, u32[]{:S(2)}) collective-permute-start(bf16[2,512,128]{2,1,0:T(8,128)(2,1)} %get-tuple-element.88), channel_id=1, source_target_pairs={{2,0},{4,2},{6,4},{3,1},{5,3},{7,5},{10,8},{12,10},{14,12},{11,9},... | collective-permute-start | bytes 786440 | tf_op jit(solution)/shard_map/ppermute | solution.py:241
  238.2 231.3 %collective-permute-start.25 = (bf16[1024,2432]{1,0:T(8,128)(2,1)}, bf16[1024,2432]{1,0:T(8,128)(2,1)}, u32[]{:S(2)}, u32[]{:S(2)}) collective-permute-start(bf16[1024,2432]{1,0:T(8,128)(2,1)} %bitcast.149), channel_id=1, source_target_pairs={{0,8},{8,0},{16,24},{24,16},{1,9},{9,1},{17,25},{25,17},{2,10},{10... | collective-permute-start | bytes 14942216 | tf_op jit(solution)/shard_map/ppermute | solution.py:231
  249.3 38.6 %collective-permute-start.19 = (bf16[1024,2,224]{0,2,1:T(8,128)(2,1)}, bf16[1024,2,224]{0,2,1:T(8,128)(2,1)}, u32[]{:S(2)}, u32[]{:S(2)}) collective-permute-start(bf16[1024,2,224]{0,2,1:T(8,128)(2,1)} %bitcast.27), channel_id=1, source_target_pairs={{0,8},{8,0},{16,24},{24,16},{1,9},{9,1},{17,25},{25,17},{2,10},{10... | collective-permute-start | bytes 2752520 | tf_op jit(solution)/shard_map/ppermute | solution.py:231
  255.2 49.7 %collective-permute-start.13 = (bf16[1024,576]{0,1:T(8,128)(2,1)}, bf16[1024,576]{0,1:T(8,128)(2,1)}, u32[]{:S(2)}, u32[]{:S(2)}) collective-permute-start(bf16[1024,576]{0,1:T(8,128)(2,1)} %copy.63), channel_id=1, source_target_pairs={{0,8},{8,0},{16,24},{24,16},{1,9},{9,1},{17,25},{25,17},{2,10},{10... | collective-permute-start | bytes 3538952 | tf_op jit(solution)/shard_map/ppermute | solution.py:231
  287.1 26.7 %collective-permute-start.11 = (bf16[896,576]{0,1:T(8,128)(2,1)}, bf16[896,576]{0,1:T(8,128)(2,1)}, u32[]{:S(2)}, u32[]{:S(2)}) collective-permute-start(bf16[896,576]{0,1:T(8,128)(2,1)} %bitcast.120), channel_id=1, source_target_pairs={{0,1},{1,0},{2,3},{3,2},{4,5},{5,4},{6,7},{7,6},{8,9},{9,8},{10,11... | collective-permute-start | bytes 3096584 | tf_op jit(solution)/shard_map/ppermute | solution.py:221
  287.9 188.5 %collective-permute-start.30 = (bf16[1024,2432]{1,0:T(8,128)(2,1)}, bf16[1024,2432]{1,0:T(8,128)(2,1)}, u32[]{:S(2)}, u32[]{:S(2)}) collective-permute-start(bf16[1024,2432]{1,0:T(8,128)(2,1)} %bitcast.144), channel_id=1, source_target_pairs={{0,8},{8,0},{16,24},{24,16},{1,9},{9,1},{17,25},{25,17},{2,10},{10... | collective-permute-start | bytes 14942216 | tf_op jit(solution)/shard_map/ppermute | solution.py:231
  302.0 36.4 %collective-permute-start.10 = (bf16[2,512,576]{1,2,0:T(8,128)(2,1)S(1)}, bf16[2,512,576]{1,2,0:T(8,128)(2,1)S(1)}, u32[]{:S(2)}, u32[]{:S(2)}) collective-permute-start(bf16[2,512,576]{1,2,0:T(8,128)(2,1)S(1)} %copy.59), channel_id=1, source_target_pairs={{0,1},{1,0},{2,3},{3,2},{4,5},{5,4},{6,7},{7,6},{8,9},{9,8},{10,11... | collective-permute-start | bytes 3538952 | tf_op jit(solution)/shard_map/ppermute | solution.py:221
  313.8 172.3 %collective-permute-start.35 = (bf16[1024,2432]{1,0:T(8,128)(2,1)}, bf16[1024,2432]{1,0:T(8,128)(2,1)}, u32[]{:S(2)}, u32[]{:S(2)}) collective-permute-start(bf16[1024,2432]{1,0:T(8,128)(2,1)} %bitcast.139), channel_id=1, source_target_pairs={{0,8},{8,0},{16,24},{24,16},{1,9},{9,1},{17,25},{25,17},{2,10},{10... | collective-permute-start | bytes 14942216 | tf_op jit(solution)/shard_map/ppermute | solution.py:231
  324.2 52.6 %collective-permute-start.5 = (bf16[2,512,896]{2,1,0:T(8,128)(2,1)S(1)}, bf16[2,512,896]{2,1,0:T(8,128)(2,1)S(1)}, u32[]{:S(2)}, u32[]{:S(2)}) collective-permute-start(bf16[2,512,896]{2,1,0:T(8,128)(2,1)S(1)} %copy-done.20), channel_id=1, source_target_pairs={{0,1},{1,0},{2,3},{3,2},{4,5},{5,4},{6,7},{7,6},{8,9},{9,8},{10,11... | collective-permute-start | bytes 5505032 | tf_op jit(solution)/shard_map/ppermute | solution.py:221
  376.8 92.7 %collective-permute-start.24 = (bf16[1024,2,224]{0,2,1:T(8,128)(2,1)S(1)}, bf16[1024,2,224]{0,2,1:T(8,128)(2,1)}, u32[]{:S(2)}, u32[]{:S(2)}) collective-permute-start(bf16[1024,2,224]{0,2,1:T(8,128)(2,1)S(1)} %bitcast.131), channel_id=1, source_target_pairs={{0,8},{8,0},{16,24},{24,16},{1,9},{9,1},{17,25},{25,17},{2,10},{10... | collective-permute-start | bytes 2752520 | tf_op jit(solution)/shard_map/ppermute | solution.py:231
  376.8 91.2 %collective-permute-start.17 = (bf16[224,576]{1,0:T(8,128)(2,1)S(1)}, bf16[224,576]{1,0:T(8,128)(2,1)S(1)}, u32[]{:S(2)}, u32[]{:S(2)}) collective-permute-start(bf16[224,576]{1,0:T(8,128)(2,1)S(1)} %add_convert_fusion.8), channel_id=1, source_target_pairs={{2,0},{4,6},{3,1},{5,7},{10,8},{12,14},{11,9},{13,15},{18,16},{20,... | collective-permute-start | bytes 774152 | tf_op jit(solution)/shard_map/ppermute | solution.py:256
  476.3 27.1 %collective-permute-start.26 = (bf16[224,2432]{1,0:T(8,128)(2,1)S(1)}, bf16[224,2432]{1,0:T(8,128)(2,1)}, u32[]{:S(2)}, u32[]{:S(2)}) collective-permute-start(bf16[224,2432]{1,0:T(8,128)(2,1)S(1)} %fusion.24), channel_id=1, source_target_pairs={{0,16},{8,24},{16,0},{24,8},{1,17},{9,25},{17,1},{25,9},{2,18},{10... | collective-permute-start | bytes 3268616 | tf_op jit(solution)/shard_map/ppermute | solution.py:278
  484.1 42.5 %collective-permute-start.31 = (bf16[224,2432]{1,0:T(8,128)(2,1)}, bf16[224,2432]{1,0:T(8,128)(2,1)S(1)}, u32[]{:S(2)}, u32[]{:S(2)}) collective-permute-start(bf16[224,2432]{1,0:T(8,128)(2,1)} %fusion.25), channel_id=1, source_target_pairs={{0,16},{8,24},{16,0},{24,8},{1,17},{9,25},{17,1},{25,9},{2,18},{10... | collective-permute-start | bytes 3268616 | tf_op jit(solution)/shard_map/ppermute | solution.py:278
  492.2 57.3 %collective-permute-start.37 = (bf16[2432,224]{0,1:T(8,128)(2,1)S(1)}, bf16[2432,224]{0,1:T(8,128)(2,1)S(1)}, u32[]{:S(2)}, u32[]{:S(2)}) collective-permute-start(bf16[2432,224]{0,1:T(8,128)(2,1)S(1)} %fusion.26), channel_id=1, source_target_pairs={{0,16},{8,24},{16,0},{24,8},{1,17},{9,25},{17,1},{25,9},{2,18},{10... | collective-permute-start | bytes 3268616 | tf_op jit(solution)/shard_map/ppermute | solution.py:278
  508.8 47.6 %collective-permute-start.27 = (bf16[224,2432]{1,0:T(8,128)(2,1)S(1)}, bf16[224,2432]{1,0:T(8,128)(2,1)S(1)}, u32[]{:S(2)}, u32[]{:S(2)}) collective-permute-start(bf16[224,2432]{1,0:T(8,128)(2,1)S(1)} %get-tuple-element.106), channel_id=1, source_target_pairs={{0,2},{6,4},{1,3},{7,5},{8,10},{14,12},{9,11},{15,13},{16,18},{22,... | collective-permute-start | bytes 3268616 | tf_op jit(solution)/shard_map/ppermute | solution.py:250
  581.0 29.8 %collective-permute-start.29 = (bf16[224,2432]{1,0:T(8,128)(2,1)S(1)}, bf16[224,2432]{1,0:T(8,128)(2,1)S(1)}, u32[]{:S(2)}, u32[]{:S(2)}) collective-permute-start(bf16[224,2432]{1,0:T(8,128)(2,1)S(1)} %add_convert_fusion.6), channel_id=1, source_target_pairs={{2,0},{4,6},{3,1},{5,7},{10,8},{12,14},{11,9},{13,15},{18,16},{20,... | collective-permute-start | bytes 3268616 | tf_op jit(solution)/shard_map/ppermute | solution.py:256
  582.6 51.6 %collective-permute-start.34 = (bf16[224,2432]{1,0:T(8,128)(2,1)S(1)}, bf16[224,2432]{1,0:T(8,128)(2,1)S(1)}, u32[]{:S(2)}, u32[]{:S(2)}) collective-permute-start(bf16[224,2432]{1,0:T(8,128)(2,1)S(1)} %add_convert_fusion.4), channel_id=1, source_target_pairs={{2,0},{4,6},{3,1},{5,7},{10,8},{12,14},{11,9},{13,15},{18,16},{20,... | collective-permute-start | bytes 3268616 | tf_op jit(solution)/shard_map/ppermute | solution.py:256
  584.2 71.6 %collective-permute-start.40 = (bf16[2432,224]{0,1:T(8,128)(2,1)S(1)}, bf16[2432,224]{0,1:T(8,128)(2,1)S(1)}, u32[]{:S(2)}, u32[]{:S(2)}) collective-permute-start(bf16[2432,224]{0,1:T(8,128)(2,1)S(1)} %add_convert_fusion.2), channel_id=1, source_target_pairs={{2,0},{4,6},{3,1},{5,7},{10,8},{12,14},{11,9},{13,15},{18,16},{20,... | collective-permute-start | bytes 3268616 | tf_op jit(solution)/shard_map/ppermute | solution.py:256
  (73 other events, 1424.8 us)

commit v3 on v2

v3 whole, which is shorter than its diff:
```python
import functools

import jax
import jax.numpy as jnp
from jax import lax
from jax.experimental import pallas as pl
from jax.experimental.pallas import tpu as pltpu
from jax.sharding import PartitionSpec as P

EPS = 1e-06
THETA = 1000000.0
SCALE = 0.125
NEGATIVE = -1e30
HD = 64
F32 = jnp.float32
BF = jnp.bfloat16
VMEM_LIMIT = 60 * 2**20


def shape_of(shape, dtype):
    return jax.ShapeDtypeStruct(shape, dtype)


def dot(a, b):
    return jnp.dot(a, b, preferred_element_type=F32)


def dot_nt(a, b):
    return lax.dot_general(a, b, (((1,), (1,)), ((), ())), preferred_element_type=F32)


def turn(rows, cosine, sine):
    half = rows.shape[0] // 2
    first, second = rows[:half], rows[half:]
    return jnp.concatenate([first * cosine - second * sine, second * cosine + first * sine], axis=0)


def inverse_rms(values):
    return lax.rsqrt(jnp.mean(values * values, axis=-1, keepdims=True) + EPS)


def norm_back(back, normed, scale, gain):
    upstream = back * gain
    inner = jnp.mean(upstream * normed, axis=-1, keepdims=True)
    return scale * (upstream - normed * inner)


def whole(a):
    return pl.BlockSpec(a.shape, lambda *_: (0,) * a.ndim)


def row_of(a, seq):
    return pl.BlockSpec((1,) + a.shape[1:], lambda *_: (seq,) + (0,) * (a.ndim - 1))


def full(*shape):
    return pl.BlockSpec(shape, lambda *_: (0,) * len(shape))


def params():
    return pltpu.CompilerParams(vmem_limit_bytes=VMEM_LIMIT)


def project_kernel(x_ref, gain_ref, w_ref, b_ref, cos_ref, sin_ref, hidden_ref, q_ref, kv_ref):
    x = x_ref[0].astype(F32)
    hidden = x * inverse_rms(x) * gain_ref[...]
    hidden_ref[0] = hidden.T.astype(BF)
    turned = (dot(hidden.astype(BF), w_ref[...]) + b_ref[...]).T
    cosine, sine = cos_ref[0], sin_ref[0]
    width = q_ref.shape[1]
    for start in range(0, width, HD):
        rows = slice(start, start + HD)
        q_ref[0, rows, :] = (turn(turned[rows], cosine, sine) * SCALE).astype(BF)
    keys = turn(turned[width : width + HD], cosine, sine)
    kv_ref[0] = jnp.concatenate([keys, turned[width + HD :]], axis=0).T.astype(BF)


def project(x, gain, w, b, cosine, sine, width):
    seqs, tokens, model = x.shape
    per = lambda r, c: pl.BlockSpec((1, r, c), lambda s: (s, 0, 0))
    half = cosine.shape[1]
    return pl.pallas_call(
        project_kernel,
        grid=(seqs,),
        in_specs=[
            per(tokens, model),
            whole(gain),
            whole(w),
            whole(b),
            per(half, tokens),
            per(half, tokens),
        ],
        out_specs=[per(model, tokens), per(width, tokens), per(tokens, 2 * HD)],
        out_shape=[
            shape_of((seqs, model, tokens), BF),
            shape_of((seqs, width, tokens), BF),
            shape_of((seqs, tokens, 2 * HD), BF),
        ],
        cost_estimate=pl.CostEstimate(
            flops=2 * seqs * tokens * model * w.shape[1],
            transcendentals=0,
            bytes_accessed=8 * seqs * tokens * model,
        ),
        compiler_params=params(),
        name="project",
    )(x, gain, w, b, cosine, sine)


def allowed_of(first_ref, place, back, tokens):
    shape = (tokens, tokens)
    key = lax.broadcasted_iota(jnp.int32, shape, 0) + (place - back * tokens)
    query = lax.broadcasted_iota(jnp.int32, shape, 1) + place
    return (key <= query) & (key >= first_ref[0])


def attend_kernel(n, seq, info_ref, q_ref, first_ref, *refs):
    pair_refs, (out_ref, lse_ref, pairs_ref, top_ref, total_ref, acc_ref) = refs[:n], refs[n:]
    tokens = q_ref.shape[2]
    heads = q_ref.shape[1] // HD
    place = info_ref[0]
    count, last_first = info_ref[1 + 2 * seq], info_ref[2 + 2 * seq]
    for s in range(n):
        pairs_ref[s] = pair_refs[s][0]
    top_ref[...] = jnp.full_like(top_ref, NEGATIVE)
    total_ref[...] = jnp.zeros_like(total_ref)
    acc_ref[...] = jnp.zeros_like(acc_ref)

    def block(back, masked):
        pair = pairs_ref[back]
        keys = pair[:, :HD]
        values = pair.T[HD:]
        ok = allowed_of(first_ref, place, back, tokens) if masked else None
        for h in range(heads):
            rows = slice(h * HD, (h + 1) * HD)
            scores = dot(keys, q_ref[0, rows, :])
            if masked:
                scores = jnp.where(ok, scores, NEGATIVE)
            old = top_ref[h : h + 1, :]
            new = jnp.maximum(old, jnp.max(scores, axis=0, keepdims=True))
            weights = jnp.exp(scores - new)
            factor = jnp.exp(old - new)
            top_ref[h : h + 1, :] = new
            total_ref[h : h + 1, :] = total_ref[h : h + 1, :] * factor + jnp.sum(
                weights, axis=0, keepdims=True
            )
            acc_ref[rows, :] = acc_ref[rows, :] * factor + dot(values, weights.astype(BF))

    block(0, True)

    @pl.loop(1, count)
    def _(back):
        masked = last_first > place - back * tokens

        @pl.when(masked)
        def _():
            block(back, True)

        @pl.when(jnp.logical_not(masked))
        def _():
            block(back, False)

    lse_ref[...] = top_ref[...] + jnp.log(total_ref[...])
    for h in range(heads):
        rows = slice(h * HD, (h + 1) * HD)
        acc_ref[rows, :] = acc_ref[rows, :] / total_ref[h : h + 1, :]
    out_ref[...] = acc_ref[...].T.astype(BF)


def attend(seq, info, q, pairs, first):
    _, width, tokens = q.shape
    n = len(pairs)
    heads = width // HD
    pad = -(-heads // 8) * 8
    return pl.pallas_call(
        functools.partial(attend_kernel, n, seq),
        grid_spec=pltpu.PrefetchScalarGridSpec(
            num_scalar_prefetch=1,
            grid=(1,),
            in_specs=[row_of(q, seq), row_of(first, seq)] + [row_of(p, seq) for p in pairs],
            out_specs=[full(tokens, width), full(pad, tokens)],
            scratch_shapes=[
                pltpu.VMEM((n, tokens, 2 * HD), BF),
                pltpu.VMEM((pad, tokens), F32),
                pltpu.VMEM((pad, tokens), F32),
                pltpu.VMEM((width, tokens), F32),
            ],
        ),
        out_shape=[shape_of((tokens, width), BF), shape_of((pad, tokens), F32)],
        cost_estimate=pl.CostEstimate(
            flops=8 * tokens * tokens * width,
            transcendentals=2 * heads * tokens * tokens,
            bytes_accessed=16 * tokens * width,
        ),
        compiler_params=params(),
        name="attend",
    )(info, q, first, *pairs)


def attend_back_kernel(
    n,
    seq,
    info_ref,
    mine_ref,
    other_ref,
    middle_ref,
    cot_ref,
    gain_ref,
    w_ref,
    att_ref,
    q_ref,
    lse_ref,
    first_ref,
    cos_ref,
    sin_ref,
    *refs,
):
    pair_refs, refs = refs[:n], refs[n:]
    gmid_ref, gmid_t_ref, gain_out_ref, gq_ref, bias_ref, own_ref = refs[:6]
    sent_refs, refs = refs[6 : 6 + n - 1], refs[6 + n - 1 :]
    pairs_ref, sent_ref, gt_ref, qn_ref, gn_ref, term_ref, gacc_ref = refs
    tokens = q_ref.shape[2]
    heads = q_ref.shape[1] // HD
    place = info_ref[0]
    count, last_first = info_ref[1 + 2 * seq], info_ref[2 + 2 * seq]
    for s in range(n):
        pairs_ref[s] = pair_refs[s][0]

    middle = middle_ref[...]
    scale = inverse_rms(middle)
    normed = middle * scale
    back = mine_ref[...].astype(F32) + other_ref[...].astype(F32)
    gain_out_ref[...] = jnp.sum(back * normed, axis=0, keepdims=True)
    gmid = cot_ref[0].astype(F32) + norm_back(back, normed, scale, gain_ref[...])
    gmid_ref[...] = gmid
    gmid_t = gmid.T.astype(BF)
    gmid_t_ref[...] = gmid_t
    gt_ref[...] = dot(w_ref[...], gmid_t).astype(BF)
    att = att_ref[...].astype(F32).T
    for h in range(heads):
        rows = slice(h * HD, (h + 1) * HD)
        grad = gt_ref[rows, :].astype(F32)
        term_ref[h : h + 1, :] = jnp.sum(grad * att[rows], axis=0, keepdims=True)
        gn_ref[h] = grad.T.astype(BF)
        qn_ref[h] = q_ref[0, rows, :].astype(F32).T.astype(BF)
    gacc_ref[...] = jnp.zeros_like(gacc_ref)

    def block(back, masked):
        pair = pairs_ref[back]
        keys, values = pair[:, :HD], pair[:, HD:]
        keys_t = pair.T[:HD]
        ok = allowed_of(first_ref, place, back, tokens) if masked else None
        grad_key = jnp.zeros((tokens, HD), F32)
        grad_value = jnp.zeros((tokens, HD), F32)
        for h in range(heads):
            rows = slice(h * HD, (h + 1) * HD)
            scores = dot(keys, q_ref[0, rows, :])
            probs = jnp.exp(scores - lse_ref[h : h + 1, :])
            if masked:
                probs = jnp.where(ok, probs, 0.0)
            grad_probs = dot(values, gt_ref[rows, :])
            grad_scores = (probs * (grad_probs - term_ref[h : h + 1, :])).astype(BF)
            grad_value = grad_value + dot(probs.astype(BF), gn_ref[h])
            grad_key = grad_key + dot(grad_scores, qn_ref[h])
            gacc_ref[rows, :] = gacc_ref[rows, :] + dot(keys_t, grad_scores)
        return jnp.concatenate([grad_key, grad_value], axis=1)

    own_ref[...] = block(0, True)

    @pl.loop(1, n)
    def _(back):
        masked = last_first > place - back * tokens

        @pl.when(back >= count)
        def _():
            sent_ref[back - 1] = jnp.zeros((tokens, 2 * HD), BF)

        @pl.when((back < count) & masked)
        def _():
            sent_ref[back - 1] = block(back, True).astype(BF)

        @pl.when((back < count) & jnp.logical_not(masked))
        def _():
            sent_ref[back - 1] = block(back, False).astype(BF)

    for s in range(n - 1):
        sent_refs[s][...] = sent_ref[s]
    cosine, sine = cos_ref[0], sin_ref[0]
    for h in range(heads):
        rows = slice(h * HD, (h + 1) * HD)
        gacc_ref[rows, :] = turn(gacc_ref[rows, :] * SCALE, cosine, -sine)
    out = gacc_ref[...].T
    gq_ref[...] = out.astype(BF)
    bias_ref[...] = jnp.sum(out, axis=0, keepdims=True)


def attend_back(seq, info, mine, other, middle, cot, gain, w, att, q, lse, first, cosine, sine, pairs):
    _, width, tokens = q.shape
    model = w.shape[1]
    n = len(pairs)
    heads = width // HD
    pad = lse.shape[0]
    pair = (tokens, 2 * HD)
    return pl.pallas_call(
        functools.partial(attend_back_kernel, n, seq),
        grid_spec=pltpu.PrefetchScalarGridSpec(
            num_scalar_prefetch=1,
            grid=(1,),
            in_specs=[
                whole(mine),
                whole(other),
                whole(middle),
                row_of(cot, seq),
                whole(gain),
                whole(w),
                whole(att),
                row_of(q, seq),
                whole(lse),
                row_of(first, seq),
                row_of(cosine, seq),
                row_of(sine, seq),
            ]
            + [row_of(p, seq) for p in pairs],
            out_specs=[
                full(tokens, model),
                full(model, tokens),
                full(1, model),
                full(tokens, width),
                full(1, width),
                full(*pair),
            ]
            + [full(*pair)] * (n - 1),
            scratch_shapes=[
                pltpu.VMEM((n,) + pair, BF),
                pltpu.VMEM((n - 1,) + pair, BF),
                pltpu.VMEM((width, tokens), BF),
                pltpu.VMEM((heads, tokens, HD), BF),
                pltpu.VMEM((heads, tokens, HD), BF),
                pltpu.VMEM((pad, tokens), F32),
                pltpu.VMEM((width, tokens), F32),
            ],
        ),
        out_shape=[
            shape_of((tokens, model), F32),
            shape_of((model, tokens), BF),
            shape_of((1, model), F32),
            shape_of((tokens, width), BF),
            shape_of((1, width), F32),
            shape_of(pair, F32),
        ]
        + [shape_of(pair, BF)] * (n - 1),
        cost_estimate=pl.CostEstimate(
            flops=24 * tokens * tokens * width,
            transcendentals=2 * heads * tokens * tokens,
            bytes_accessed=16 * tokens * model,
        ),
        compiler_params=params(),
        name="attend_back",
    )(info, mine, other, middle, cot, gain, w, att, q, lse, first, cosine, sine, *pairs)


def mlp_kernel(
    total,
    x_ref,
    mine_ref,
    other_ref,
    wo_ref,
    wx_ref,
    gain_ref,
    cot_ref,
    gate_ref,
    up_ref,
    down_ref,
    middle_ref,
    hid_t_ref,
    act_ref,
    gg_ref,
    gu_ref,
    part_ref,
    back_ref,
    hidden_ref,
    acc_ref,
    bacc_ref,
):
    j = pl.program_id(0)

    @pl.when(j == 0)
    def _():
        middle = x_ref[0].astype(F32) + (
            dot(mine_ref[...], wo_ref[...]) + dot(other_ref[...], wx_ref[...])
        )
        middle_ref[...] = middle
        hidden = middle * inverse_rms(middle) * gain_ref[...]
        hidden_ref[...] = hidden.astype(BF)
        hid_t_ref[...] = hidden.T.astype(BF)
        acc_ref[...] = jnp.zeros_like(acc_ref)
        bacc_ref[...] = jnp.zeros_like(bacc_ref)

    tile = gate_ref.shape[1]
    wg, wu, wd = gate_ref[...], up_ref[...], down_ref[...]
    if total % tile:
        left = total - j * tile
        cols = lax.broadcasted_iota(jnp.int32, wg.shape, 1) < left
        wg, wu = jnp.where(cols, wg, jnp.zeros_like(wg)), jnp.where(cols, wu, jnp.zeros_like(wu))
        rows = lax.broadcasted_iota(jnp.int32, wd.shape, 0) < left
        wd = jnp.where(rows, wd, jnp.zeros_like(wd))
    hidden = hidden_ref[...]
    gate = dot(hidden, wg)
    up = dot(hidden, wu)
    grad_act = dot_nt(cot_ref[0], wd)
    sigma = 1.0 / (1.0 + jnp.exp(-gate))
    silu = gate * sigma
    act = (silu * up).astype(BF)
    gg = (grad_act * up * sigma * (1.0 + gate * (1.0 - sigma))).astype(BF)
    gu = (grad_act * silu).astype(BF)
    act_ref[...] = act
    gg_ref[...] = gg
    gu_ref[...] = gu
    acc_ref[...] += dot(act, wd)
    bacc_ref[...] += dot_nt(gg, wg) + dot_nt(gu, wu)

    @pl.when(j == pl.num_programs(0) - 1)
    def _():
        part_ref[...] = acc_ref[...].astype(BF)
        back_ref[...] = bacc_ref[...].astype(BF)


def mlp(seq, x, mine, other, wo, wx, gain, cot, wg, wu, wd, tile=512):
    _, tokens, model = x.shape
    ff = wg.shape[1]
    cols = pl.BlockSpec((tokens, tile), lambda j: (0, j))
    columns = pl.BlockSpec((model, tile), lambda j: (0, j))
    return pl.pallas_call(
        functools.partial(mlp_kernel, ff),
        grid=(pl.cdiv(ff, tile),),
        in_specs=[
            row_of(x, seq),
            whole(mine),
            whole(other),
            whole(wo),
            whole(wx),
            whole(gain),
            row_of(cot, seq),
            columns,
            columns,
            pl.BlockSpec((tile, model), lambda j: (j, 0)),
        ],
        out_specs=[full(tokens, model), full(model, tokens)]
        + [cols] * 3
        + [full(tokens, model)] * 2,
        out_shape=[shape_of((tokens, model), F32), shape_of((model, tokens), BF)]
        + [shape_of((tokens, ff), BF)] * 3
        + [shape_of((tokens, model), BF)] * 2,
        scratch_shapes=[
            pltpu.VMEM((tokens, model), BF),
            pltpu.VMEM((tokens, model), F32),
            pltpu.VMEM((tokens, model), F32),
        ],
        cost_estimate=pl.CostEstimate(
            flops=12 * tokens * model * ff,
            transcendentals=tokens * ff,
            bytes_accessed=6 * model * ff + 6 * tokens * ff,
        ),
        compiler_params=params(),
        name="mlp",
    )(x, mine, other, wo, wx, gain, cot, wg, wu, wd)


def weight_kernel(count, shares, places_ref, *refs):
    lefts, rights, outs = refs[: 2 * count], refs[2 * count : 4 * count], refs[4 * count :]
    for share in range(shares):
        total = None
        for k in range(2 * count):
            place = places_ref[share if k < count else shares + share]
            part = dot(lefts[k][place], rights[k][...])
            total = part if total is None else total + part
        outs[share][...] = total.astype(outs[share].dtype)


def weight_grad(places, lefts, rights, tile):
    count = len(lefts) // 2
    shares = places.shape[0] // 2
    _, rows, tokens = lefts[0].shape
    ff = rights[0].shape[1]
    tile = min(tile, ff)
    cols = pl.BlockSpec((tokens, tile), lambda j, p: (0, j))
    out = pl.BlockSpec((rows, tile), lambda j, p: (0, j))
    return pl.pallas_call(
        functools.partial(weight_kernel, count, shares),
        grid_spec=pltpu.PrefetchScalarGridSpec(
            num_scalar_prefetch=1,
            grid=(pl.cdiv(ff, tile),),
            in_specs=[whole(a) for a in lefts] + [cols] * len(rights),
            out_specs=[out] * shares,
        ),
        out_shape=[shape_of((rows, ff), F32)] + [shape_of((rows, ff), BF)] * (shares - 1),
        cost_estimate=pl.CostEstimate(
            flops=4 * count * shares * rows * tokens * ff,
            transcendentals=0,
            bytes_accessed=4 * count * tokens * ff + 6 * rows * ff,
        ),
        compiler_params=params(),
        name="weight_grad",
    )(places, *lefts, *rights)


def pair_back_kernel(own_ref, cos_ref, sin_ref, *refs):
    moved, out_ref, bias_ref = refs[:-2], refs[-2], refs[-1]
    total = own_ref[...]
    for ref in moved:
        total = total + ref[...].astype(F32)
    turned = total.T
    keys = turn(turned[:HD], cos_ref[0], -sin_ref[0])
    total = jnp.concatenate([keys, turned[HD:]], axis=0).T
    out_ref[...] = total.astype(BF)
    bias_ref[...] = jnp.sum(total, axis=0, keepdims=True)


def pair_back(seq, own, moved, cosine, sine):
    return pl.pallas_call(
        pair_back_kernel,
        grid=(1,),
        in_specs=[whole(own), row_of(cosine, seq), row_of(sine, seq)] + [whole(m) for m in moved],
        out_specs=[full(*own.shape), full(1, own.shape[1])],
        out_shape=[shape_of(own.shape, BF), shape_of((1, own.shape[1]), F32)],
        compiler_params=params(),
        name="pair_back",
    )(own, cosine, sine, *moved)


def input_back_kernel(
    gq_ref, gqx_ref, gkv_ref, gkvx_ref, w_ref, wx_ref, x_ref, gain_ref, gmid_ref, *refs
):
    out_ref, gain_out_ref = refs[-2:]
    width = gq_ref.shape[1]

    def back_of(q_ref, kv_ref, weights):
        return dot_nt(q_ref[...], weights[:, :width]) + dot_nt(kv_ref[...], weights[:, width:])

    back = back_of(gq_ref, gkv_ref, w_ref[...]) + back_of(gqx_ref, gkvx_ref, wx_ref[...])
    x = x_ref[0].astype(F32)
    scale = inverse_rms(x)
    normed = x * scale
    gain_out_ref[...] = jnp.sum(back * normed, axis=0, keepdims=True)
    out_ref[0] = gmid_ref[...] + norm_back(back, normed, scale, gain_ref[...])


def input_back(seq, gq, gqx, gkv, gkvx, w, wx, x, gain, gmid, so_far):
    seqs, tokens, model = x.shape
    operands = [gq, gqx, gkv, gkvx, w, wx, x, gain, gmid]
    specs = [whole(a) for a in operands]
    specs[6] = row_of(x, seq)
    aliases = {}
    if so_far is not None:
        aliases = {len(operands): 0}
        operands.append(so_far)
        specs.append(pl.BlockSpec(memory_space=pl.ANY))
    return pl.pallas_call(
        input_back_kernel,
        grid=(1,),
        in_specs=specs,
        out_specs=[row_of(x, seq), full(1, model)],
        out_shape=[shape_of(x.shape, F32), shape_of((1, model), F32)],
        input_output_aliases=aliases,
        cost_estimate=pl.CostEstimate(
            flops=4 * tokens * model * w.shape[1],
            transcendentals=0,
            bytes_accessed=14 * tokens * model,
        ),
        compiler_params=params(),
        name="input_back",
    )(*operands)


def tp_other(values):
    return lax.ppermute(values, "tp", [(0, 1), (1, 0)])


def core_other(values):
    return lax.ppermute(values, "dp", [(i, i ^ 1) for i in range(lax.axis_size("dp"))])


def row_back(values, shift):
    rows = lax.axis_size("dp") // 2
    pairs = [(r * 2 + c, (r + shift) % rows * 2 + c) for r in range(rows) for c in range(2)]
    return lax.ppermute(values, "dp", pairs)


def earlier(values, shift):
    n = lax.axis_size("ctx")
    return lax.ppermute(values, "ctx", [(i, i + shift) for i in range(n - shift)])


def later(values, shift):
    n = lax.axis_size("ctx")
    return lax.ppermute(values, "ctx", [(i + shift, i) for i in range(n - shift)])


def tree_sum(terms):
    if len(terms) == 1:
        return terms[0]
    if len(terms) % 2:
        return terms[0] + tree_sum(terms[1:])
    return tree_sum(terms[0::2]) + tree_sum(terms[1::2])


def ring_sum(part):
    n = lax.axis_size("ctx")
    mine = part.astype(BF)
    terms = [mine]
    for shift in range(1, n):
        terms.append(lax.ppermute(mine, "ctx", [(i, (i + shift) % n) for i in range(n)]))
    return tree_sum([t.astype(F32) for t in terms])


def line_sum(part):
    n = lax.axis_size("ctx")
    half = n // 2
    me = lax.axis_index("ctx")
    for step in range(half - 1):
        pairs = [(step, step + 1), (n - 1 - step, n - 2 - step)]
        part = part + lax.ppermute(part.astype(BF), "ctx", pairs).astype(F32)
    mine = part.astype(BF)
    moved = lax.ppermute(mine, "ctx", [(half - 1, half), (half, half - 1)])
    total = (mine.astype(F32) + moved.astype(F32)).astype(BF)
    for step in reversed(range(half - 1)):
        pairs = [(step + 1, step), (n - 2 - step, n - 1 - step)]
        moved = lax.ppermute(total, "ctx", pairs)
        total = jnp.where((me == step) | (me == n - 1 - step), moved, total)
    return total.astype(F32)


def shards(
    block_input,
    positions,
    gain_attn,
    w_qkv,
    b_qkv,
    w_out,
    gain_mlp,
    w_gate,
    w_up,
    w_down,
    cotangent,
):
    seqs, tokens, model = block_input.shape
    heads_width = w_out.shape[1]
    n_ctx, n_dp = lax.axis_size("ctx"), lax.axis_size("dp")
    n_row = n_dp // 2
    me, my_dp = lax.axis_index("ctx"), lax.axis_index("dp")
    row, core = my_dp // 2, my_dp % 2
    first_token = me * tokens
    every = range(seqs)
    share = model // n_dp
    proj_qkv, proj_out = w_qkv[:, 0, :], w_out[0]
    other_out = tp_other(proj_out)
    other_qkv = tp_other(proj_qkv)
    gain_one, gain_two = gain_attn[None, :], gain_mlp[None, :]

    half = HD // 2
    freq = THETA ** (-(jnp.arange(half, dtype=F32) * 2.0) / HD)
    angle = positions.astype(F32)[:, None, :] * freq[None, :, None]
    cosine, sine = jnp.cos(angle), jnp.sin(angle)
    query_first = (first_token + jnp.arange(tokens, dtype=jnp.int32))[None, :] - positions
    counts = me - query_first[:, 0] // tokens + 1
    info = jnp.concatenate(
        [first_token[None], jnp.stack([counts, query_first[:, -1]], axis=1).reshape(-1)]
    ).astype(jnp.int32)
    query_first = query_first[:, None, :]
    rows_from = (row + jnp.arange(n_row, dtype=jnp.int32)) % n_row
    places = jnp.concatenate([rows_from * 2 + core, rows_from]).astype(jnp.int32)

    def for_other_core(turned):
        split = turned.reshape(n_row, 2, share, turned.shape[1])
        return core_other(lax.dynamic_index_in_dim(split, 1 - core, 1, keepdims=False))

    def blocks(turned):
        return turned.reshape(n_dp, share, turned.shape[1])

    def gradient(lefts, lefts_other, rights, rights_other, tile=512):
        own, *sent = weight_grad(places, lefts + lefts_other, rights + rights_other, tile)
        return own, sent

    def over_rows(own, sent):
        for shift in range(1, n_row):
            own = own + row_back(sent[shift - 1], shift).astype(F32)
        return own

    hidden_t, queries, key_value = project(
        block_input, gain_one, proj_qkv, b_qkv, cosine, sine, heads_width
    )
    pairs = [key_value] + [earlier(key_value, shift) for shift in range(1, n_ctx)]
    cot_t = jnp.swapaxes(cotangent, 1, 2)
    cot_other = [for_other_core(cot_t[i]) for i in every]
    hidden_other = [for_other_core(hidden_t[i]) for i in every]

    attended, lse = zip(*[attend(i, info, queries, pairs, query_first) for i in every])
    att_moved = [tp_other(a) for a in attended]
    middle, hid_t, acts, gates, ups, part, back = zip(
        *[
            mlp(
                i,
                block_input,
                attended[i],
                att_moved[i],
                proj_out,
                other_out,
                gain_two,
                cotangent,
                w_gate,
                w_up,
                w_down,
            )
            for i in every
        ]
    )
    back_moved = [tp_other(b) for b in back]
    part_moved = [tp_other(p) for p in part]
    output = jnp.stack(
        [
            (middle[i] + (part[i].astype(F32) + part_moved[i].astype(F32))).astype(BF)
            for i in every
        ]
    )
    hid_other = [for_other_core(h) for h in hid_t]
    hid_blocks = [blocks(h) for h in hid_t]
    acts_other, gates_other, ups_other = (
        [core_other(a) for a in group] for group in (acts, gates, ups)
    )
    down = gradient([blocks(cot_t[i]) for i in every], cot_other, list(acts), acts_other)
    gate = gradient(hid_blocks, hid_other, list(gates), gates_other)
    up = gradient(hid_blocks, hid_other, list(ups), ups_other)
    back_moved, down, gate, up = lax.optimization_barrier((back_moved, down, gate, up))
    down, gate, up = over_rows(*down), over_rows(*gate), over_rows(*up)
    grad_down, grad_gate, grad_up = line_sum(down).T, line_sum(gate), line_sum(up)

    results = [
        attend_back(
            i,
            info,
            back[i],
            back_moved[i],
            middle[i],
            cotangent,
            gain_two,
            proj_out,
            attended[i],
            queries,
            lse[i],
            query_first,
            cosine,
            sine,
            pairs,
        )
        for i in every
    ]
    grad_mid, grad_mid_t, gain_mlp_parts, grad_q, bias_q, grad_own = zip(*[r[:6] for r in results])
    grad_q_moved = [tp_other(g) for g in grad_q]
    pair_results = [
        pair_back(
            i,
            grad_own[i],
            [later(results[i][5 + shift], shift) for shift in range(1, n_ctx)],
            cosine,
            sine,
        )
        for i in every
    ]
    grad_kv, bias_kv = zip(*pair_results)
    grad_kv_moved = [tp_other(g) for g in grad_kv]

    mid_blocks = [blocks(g) for g in grad_mid_t]
    mid_other = [for_other_core(g) for g in grad_mid_t]
    hidden_blocks = [blocks(hidden_t[i]) for i in every]
    grad_out = over_rows(
        *gradient(mid_blocks, mid_other, list(attended), [core_other(a) for a in attended])
    )
    grad_out = ring_sum(grad_out).T[None]
    qkv_q = over_rows(
        *gradient(hidden_blocks, hidden_other, list(grad_q), [core_other(g) for g in grad_q])
    )
    qkv_kv = over_rows(
        *gradient(hidden_blocks, hidden_other, list(grad_kv), [core_other(g) for g in grad_kv])
    )
    grad_qkv = jnp.concatenate([ring_sum(qkv_q), ring_sum(qkv_kv)], axis=1)[:, None, :]

    grad_input, gain_attn_parts = None, []
    for i in every:
        grad_input, gain_part = input_back(
            i,
            grad_q[i],
            grad_q_moved[i],
            grad_kv[i],
            grad_kv_moved[i],
            proj_qkv,
            other_qkv,
            block_input,
            gain_one,
            grad_mid[i],
            grad_input,
        )
        gain_attn_parts.append(gain_part)

    def small_sum(values):
        values = values + core_other(values)
        values = tree_sum([values] + [row_back(values, shift) for shift in range(1, n_row)])
        ring = [
            lax.ppermute(values, "ctx", [(i, (i + shift) % n_ctx) for i in range(n_ctx)])
            for shift in range(1, n_ctx)
        ]
        return tree_sum([values] + ring)[0]

    small = small_sum(
        jnp.concatenate(
            [sum(gain_attn_parts), sum(gain_mlp_parts), sum(bias_q), sum(bias_kv)], axis=1
        )
    )

    def my_part(values):
        size = values.shape[0] // n_dp
        return lax.dynamic_slice_in_dim(values, my_dp * size, size)

    return (
        output,
        grad_input,
        my_part(small[:model]),
        grad_qkv,
        my_part(small[2 * model :])[None],
        grad_out,
        my_part(small[model : 2 * model]),
        grad_gate,
        grad_up,
        grad_down,
    )


def solution(mesh):
    in_specs = (
        P("dp", "ctx", None),
        P("dp", "ctx"),
        P(),
        P(None, "tp", None),
        P("tp", None),
        P("tp", None, None),
        P(),
        P(None, "tp"),
        P(None, "tp"),
        P("tp", None),
        P("dp", "ctx", None),
    )
    out_specs = (
        P("dp", "ctx", None),
        P("dp", "ctx", None),
        P("dp"),
        P("dp", "tp", None),
        P("tp", "dp"),
        P("tp", None, "dp"),
        P("dp"),
        P("dp", "tp"),
        P("dp", "tp"),
        P("tp", "dp"),
    )
    return jax.shard_map(shards, mesh=mesh, in_specs=in_specs, out_specs=out_specs, check_vma=False)
```

time: 658 us -> 569 us (0.86); the launches traced: 658 us -> 560 us
  Pallas kernels: 33.2 us -> 170 us
  matrix products: 122 us -> 0 us
  local copies, waits for them, and re-layouts: 118 us -> 27.2 us
  blocking collectives: 78.1 us -> 0 us
  waiting for transfers between devices: 214 us -> 262 us
  starting transfers between devices: 58.1 us -> 78.7 us
  other arithmetic: 31.5 us -> 20.7 us
    pallas_call x2 -> x16, Pallas kernels: 28.1 us -> 165 us  [the longest x2 52.9 us: mlp(): pl.pallas_call(functools.partial(mlp_kernel, ff), grid=(pl.cdiv(ff, tile)...]
    dot_general x20 -> x0, matrix products: 122 us -> none  [the longest x1 17.2 us: shards(): jnp.einsum('std,df->stf', hidden_two, w_gate, preferred_element_type=jnp....]
    psum x1 -> x0, blocking collectives: 78.1 us -> none  [shards(): small = lax.psum((grad_gain_attn, grad_bias, grad_gain_mlp), ('dp', 'ctx'))]
    ppermute x19 -> x43, waiting for transfers between devices: 75.5 us -> 139 us  [the longest x7 54.6 us: row_back(): return lax.ppermute(values, 'dp', pairs)]
    unnamed x122 -> x98, local copies, waits for them, and re-layouts: 50.9 us -> 10.5 us
    another operation x4 -> x0, local copies, waits for them, and re-layouts: 28.9 us -> none  [quarter_grads(): split = wide.reshape(wide.shape[0], rows, 2, wide.shape[1] // n_dp)]
    dynamic_slice x6 -> x3, local copies, waits for them, and re-layouts: 28.8 us -> 1.91 us  [my_part(): return lax.dynamic_slice_in_dim(values, my_dp * size, size)]
    ppermute x19 -> x43, starting transfers between devices: 26.8 us -> 38.9 us  [the longest x9 15.2 us: ring_sum(): lax.ppermute(mine, 'ctx', [(i, (i + shift) % n) for i in range(n)])]
  transfers between devices with their start and end apart: 41 -> 70, of which waited for: 18 -> 22; matrix products, arithmetic and copies ran while one was open for 33% -> 7% of each run, Pallas kernels for 4% -> 29%
where the time goes in v3:
time: 569 us; the launch traced here: 560 us
  waiting for transfers between devices  262 us (46%)
  Pallas kernels  170 us (30%)
  starting transfers between devices  78.7 us (14%)
  local copies, waits for them, and re-layouts  27.2 us (5%)
  other arithmetic  20.7 us (4%)
    ppermute x3, waiting for transfers between devices, line_sum(): moved = lax.ppermute(total, 'ctx', pairs)  68.3 us
    ppermute x7, waiting for transfers between devices, row_back(): return lax.ppermute(values, 'dp', pairs)  54.6 us
    pallas_call x2, Pallas kernels, mlp(): pl.pallas_call(functools.partial(mlp_kernel, ff), grid=(pl.cdiv(ff, tile)...  52.9 us
    ppermute x3, waiting for transfers between devices, line_sum(): part = part + lax.ppermute(part.astype(BF), 'ctx', pairs).astype(F32)  50.8 us
    pallas_call x6, Pallas kernels, weight_grad(): pl.pallas_call(functools.partial(weight_kernel, count, shares), grid_spec...  46 us
    ppermute x9, waiting for transfers between devices, ring_sum(): lax.ppermute(mine, 'ctx', [(i, (i + shift) % n) for i in range(n)])  27 us
    pallas_call x2, Pallas kernels, attend_back(): pl.pallas_call(functools.partial(attend_back_kernel, n, seq), grid_spec=p...  26 us
    ppermute x6, waiting for transfers between devices, later(): lax.ppermute(values, 'ctx', [(i + shift, i) for i in range(n - shift)])  23.9 us
  transfers between devices with their start and end apart: 70, of which 22 were waited for; matrix products, arithmetic and copies ran while one was open for 7% of the time, Pallas kernels for 29%

profile of v3, /device:TPU:0, one launch (start us, length us, event | category | flops | bytes accessed | tf_op | source)
XLA Modules:
  0.0 560.2 jit_solution(12038462750501131849)
XLA Ops:
  32.7 7.2 %attend.2 = (bf16[512,448]{1,0:T(8,128)(2,1)}, f32[8,512]{1,0:T(8,128)}) custom-call(s32[5]{0:T(128)} %pad_add_fusion.1.info_ref, bf16[2,448,512]{2,1,0:T(8,128)(2,1)} %get-tuple-element.77.q_ref, s32[2,1,512]{2,1,0:T(1,128)} %broadcast_in_dim.24.first_ref, bf16[2,512,128]{2,1,0:T(8,128)(2,1)} %get-tuple-element.78.refs_0_, bf16[2,512,128]{2,1,0:T(8,128)(2,1)} %copy-done.41, ...), custom_call_target="tpu_custom_call" | custom-call | flops 939524096 | bytes 3670016 | tf_op jit(solution)/shard_map/attend/pallas_call | solution.py:174
  44.8 15.8 %attend.3 = (bf16[512,448]{1,0:T(8,128)(2,1)}, f32[8,512]{1,0:T(8,128)}) custom-call(s32[5]{0:T(128)} %pad_add_fusion.1.info_ref, bf16[2,448,512]{2,1,0:T(8,128)(2,1)} %get-tuple-element.77.q_ref, s32[2,1,512]{2,1,0:T(1,128)} %broadcast_in_dim.24.first_ref, bf16[2,512,128]{2,1,0:T(8,128)(2,1)} %get-tuple-element.78.refs_0_, bf16[2,512,128]{2,1,0:T(8,128)(2,1)} %copy-done.41, ...), custom_call_target="tpu_custom_call" | custom-call | flops 939524096 | bytes 3670016 | tf_op jit(solution)/shard_map/attend/pallas_call | solution.py:174
  62.0 26.4 %mlp.2 = (f32[512,896]{1,0:T(8,128)}, bf16[896,512]{1,0:T(8,128)(2,1)}, bf16[512,2432]{1,0:T(8,128)(2,1)}, bf16[512,2432]{1,0:T(8,128)(2,1)}, bf16[512,2432]{1,0...) custom-call(bf16[2,512,896]{2,1,0:T(8,128)(2,1)} %x_ref.9, ...), custom_call_target="tpu_custom_call" | custom-call | flops 13388218368 | bytes 20545536 | tf_op jit(solution)/shard_map/mlp/pallas_call | solution.py:432
  92.3 26.5 %mlp.3 = (f32[512,896]{1,0:T(8,128)}, bf16[896,512]{1,0:T(8,128)(2,1)}, bf16[512,2432]{1,0:T(8,128)(2,1)}, bf16[512,2432]{1,0:T(8,128)(2,1)}, bf16[512,2432]{1,0...) custom-call(bf16[2,512,896]{2,1,0:T(8,128)(2,1)} %x_ref.9, ...), custom_call_target="tpu_custom_call" | custom-call | flops 13388218368 | bytes 20545536 | tf_op jit(solution)/shard_map/mlp/pallas_call | solution.py:432
  121.0 7.0 %collective-permute-done.15.refs_3_ = bf16[2,224,512]{2,1,0:T(8,128)(2,1)S(1)} collective-permute-done((bf16[2,224,512]{2,1,0:T(8,128)(2,1)S(1)}, bf16[2,224,512]{2,1,0:T(8,128)(2,1)S(1)}, u32[]{:S(2)}, u32[]{:S(2)}) %collective-permute-start.15) | collective-permute-done | bytes 458784 | tf_op jit(solution)/shard_map/ppermute | solution.py:579
  132.8 11.0 %weight_grad.8 = (f32[224,2432]{1,0:T(8,128)}, bf16[224,2432]{1,0:T(8,128)(2,1)}) custom-call(s32[4]{0:T(128)} %pad_add_fusion.2.places_ref, bf16[4,224,512]{2,1,0:T(8,128)(2,1)} %bitcast.82, bf16[4,224,512]{2,1,0:T(8,128)(2,1)} %bitcast.86, bf16[2,224,512]{2,1,0:T(8,128)(2,1)} %copy-done.39, bf16[2,224,512]{2,1,0:T(8,128)(2,1)} %copy-done.40, ...), custom_call_target="tpu_custom_call" | custom-call | flops 4462739456 | bytes 13230080 | tf_op jit(solution)/shard_map/weight_grad/pallas_call | solution.py:487
  145.4 10.7 %weight_grad.7 = (f32[224,2432]{1,0:T(8,128)}, bf16[224,2432]{1,0:T(8,128)(2,1)}) custom-call(s32[4]{0:T(128)} %pad_add_fusion.2.places_ref, bf16[4,224,512]{2,1,0:T(8,128)(2,1)} %bitcast.83, bf16[4,224,512]{2,1,0:T(8,128)(2,1)} %bitcast.87, bf16[2,224,512]{2,1,0:T(8,128)(2,1)} %copy-done.39, bf16[2,224,512]{2,1,0:T(8,128)(2,1)} %copy-done.40, ...), custom_call_target="tpu_custom_call" | custom-call | flops 4462739456 | bytes 13230080 | tf_op jit(solution)/shard_map/weight_grad/pallas_call | solution.py:487
  158.2 10.7 %weight_grad.6 = (f32[224,2432]{1,0:T(8,128)}, bf16[224,2432]{1,0:T(8,128)(2,1)}) custom-call(s32[4]{0:T(128)} %pad_add_fusion.2.places_ref, bf16[4,224,512]{2,1,0:T(8,128)(2,1)} %bitcast.80, bf16[4,224,512]{2,1,0:T(8,128)(2,1)} %bitcast.78, bf16[2,224,512]{2,1,0:T(8,128)(2,1)} %copy-done.38, bf16[2,224,512]{2,1,0:T(8,128)(2,1)} %collective-permute-done.11.refs_3_, ...), custom_call_target="tpu_custom_call" | custom-call | flops 4462739456 | bytes 13230080 | tf_op jit(solution)/shard_map/weight_grad/pallas_call | solution.py:487
  174.0 12.9 %attend_back.3 = (f32[512,896]{1,0:T(8,128)}, bf16[896,512]{1,0:T(8,128)(2,1)}, f32[1,896]{1,0:T(1,128)}, bf16[512,448]{1,0:T(8,128)(2,1)}, f32[1,448]{1,0:T(1,1...) custom-call(s32[5]{0:T(128)} %pad_add_fusion.1.info_ref, ...), custom_call_target="tpu_custom_call" | custom-call | flops 2818572288 | bytes 7340032 | tf_op jit(solution)/shard_map/attend_back/pallas_call | solution.py:303
  190.0 13.2 %attend_back.2 = (f32[512,896]{1,0:T(8,128)}, bf16[896,512]{1,0:T(8,128)(2,1)}, f32[1,896]{1,0:T(1,128)}, bf16[512,448]{1,0:T(8,128)(2,1)}, f32[1,448]{1,0:T(1,1...) custom-call(s32[5]{0:T(128)} %pad_add_fusion.1.info_ref, ...), custom_call_target="tpu_custom_call" | custom-call | flops 2818572288 | bytes 7340032 | tf_op jit(solution)/shard_map/attend_back/pallas_call | solution.py:303
  204.4 11.3 %collective-permute-done.5 = bf16[512,896]{1,0:T(8,128)(2,1)} collective-permute-done((bf16[512,896]{1,0:T(8,128)(2,1)}, bf16[512,896]{1,0:T(8,128)(2,1)}, u32[]{:S(2)}, u32[]{:S(2)}) %collective-permute-start.5) | collective-permute-done | bytes 917536 | tf_op jit(solution)/shard_map/ppermute | solution.py:575
  221.6 17.7 %collective-permute-done.29.refs_2_ = bf16[512,128]{1,0:T(8,128)(2,1)} collective-permute-done((bf16[512,128]{1,0:T(8,128)(2,1)}, bf16[512,128]{1,0:T(8,128)(2,1)}, u32[]{:S(2)}, u32[]{:S(2)}) %collective-permute-start.29) | collective-permute-done | bytes 131104 | tf_op jit(solution)/shard_map/ppermute | solution.py:595
  289.8 6.4 %input_back.3 = (f32[2,512,896]{2,1,0:T(8,128)}, f32[1,896]{1,0:T(1,128)}) custom-call(bf16[512,448]{1,0:T(8,128)(2,1)} %get-tuple-element.103.gq_ref.refs_5_, bf16[512,448]{1,0:T(8,128)(2,1)} %collective-permute-done.20.gqx_ref, bf16[512,128]{1,0:T(8,128)(2,1)} %get-tuple-element.108.gkv_ref.refs_5_, ...), custom_call_target="tpu_custom_call", output_to_operand_aliasing={{0}: (9, {})} | custom-call | flops 1056964608 | bytes 6422528 | tf_op jit(solution)/shard_map/input_back/pallas_call | solution.py:557
  323.0 39.9 %collective-permute-done.54 = bf16[224,448]{1,0:T(8,128)(2,1)S(1)} collective-permute-done((bf16[224,448]{1,0:T(8,128)(2,1)}, bf16[224,448]{1,0:T(8,128)(2,1)S(1)}, u32[]{:S(2)}, u32[]{:S(2)}) %collective-permute-start.54) | collective-permute-done | bytes 200736 | tf_op jit(solution)/shard_map/ppermute | solution.py:585
  369.0 13.4 %collective-permute-done.55 = bf16[224,448]{1,0:T(8,128)(2,1)S(1)} collective-permute-done((bf16[224,448]{1,0:T(8,128)(2,1)S(1)}, bf16[224,448]{1,0:T(8,128)(2,1)S(1)}, u32[]{:S(2)}, u32[]{:S(2)}) %collective-permute-start.55) | collective-permute-done | bytes 200736 | tf_op jit(solution)/shard_map/ppermute | solution.py:611
  382.4 7.1 %collective-permute-start.42 = (bf16[224,448]{1,0:T(8,128)(2,1)S(1)}, bf16[224,448]{1,0:T(8,128)(2,1)}, u32[]{:S(2)}, u32[]{:S(2)}) collective-permute-start(bf16[224,448]{1,0:T(8,128)(2,1)S(1)} %add_convert_fusion.9), channel_id=1, source_target_pairs={{0,2},{2,4},{4,6},{6,0},{1,3},{3,5},{5,7},{7,1},{8,10},{10,12},{12... | collective-permute-start | bytes 602120 | tf_op jit(solution)/shard_map/ppermute | solution.py:611
  390.6 10.7 %collective-permute-done.41 = bf16[224,448]{1,0:T(8,128)(2,1)S(1)} collective-permute-done((bf16[224,448]{1,0:T(8,128)(2,1)S(1)}, bf16[224,448]{1,0:T(8,128)(2,1)S(1)}, u32[]{:S(2)}, u32[]{:S(2)}) %collective-permute-start.41) | collective-permute-done | bytes 200736 | tf_op jit(solution)/shard_map/ppermute | solution.py:611
  413.2 13.2 %collective-permute-done.58 = bf16[224,2432]{1,0:T(8,128)(2,1)S(1)} collective-permute-done((bf16[224,2432]{1,0:T(8,128)(2,1)}, bf16[224,2432]{1,0:T(8,128)(2,1)S(1)}, u32[]{:S(2)}, u32[]{:S(2)}) %collective-permute-start.58) | collective-permute-done | bytes 1089568 | tf_op jit(solution)/shard_map/ppermute | solution.py:585
  428.1 7.9 %collective-permute-done.67 = bf16[224,2432]{1,0:T(8,128)(2,1)S(1)} collective-permute-done((bf16[224,2432]{1,0:T(8,128)(2,1)S(1)}, bf16[224,2432]{1,0:T(8,128)(2,1)S(1)}, u32[]{:S(2)}, u32[]{:S(2)}) %collective-permute-start.67) | collective-permute-done | bytes 1089568 | tf_op jit(solution)/shard_map/ppermute | solution.py:621
  437.1 22.2 %collective-permute-done.63 = bf16[224,2432]{1,0:T(8,128)(2,1)S(1)} collective-permute-done((bf16[224,2432]{1,0:T(8,128)(2,1)S(1)}, bf16[224,2432]{1,0:T(8,128)(2,1)S(1)}, u32[]{:S(2)}, u32[]{:S(2)}) %collective-permute-start.63) | collective-permute-done | bytes 1089568 | tf_op jit(solution)/shard_map/ppermute | solution.py:621
  460.5 20.7 %collective-permute-done.59 = bf16[224,2432]{1,0:T(8,128)(2,1)S(1)} collective-permute-done((bf16[224,2432]{1,0:T(8,128)(2,1)S(1)}, bf16[224,2432]{1,0:T(8,128)(2,1)S(1)}, u32[]{:S(2)}, u32[]{:S(2)}) %collective-permute-start.59) | collective-permute-done | bytes 1089568 | tf_op jit(solution)/shard_map/ppermute | solution.py:621
  487.1 26.4 %collective-permute-done.69 = bf16[224,2432]{1,0:T(8,128)(2,1)S(1)} collective-permute-done((bf16[224,2432]{1,0:T(8,128)(2,1)S(1)}, bf16[224,2432]{1,0:T(8,128)(2,1)S(1)}, u32[]{:S(2)}, u32[]{:S(2)}) %collective-permute-start.69) | collective-permute-done | bytes 1089568 | tf_op jit(solution)/shard_map/ppermute | solution.py:627
  515.1 21.9 %collective-permute-done.65 = bf16[224,2432]{1,0:T(8,128)(2,1)S(1)} collective-permute-done((bf16[224,2432]{1,0:T(8,128)(2,1)S(1)}, bf16[224,2432]{1,0:T(8,128)(2,1)S(1)}, u32[]{:S(2)}, u32[]{:S(2)}) %collective-permute-start.65) | collective-permute-done | bytes 1089568 | tf_op jit(solution)/shard_map/ppermute | solution.py:627
  538.4 20.0 %collective-permute-done.61 = bf16[224,2432]{1,0:T(8,128)(2,1)S(1)} collective-permute-done((bf16[224,2432]{1,0:T(8,128)(2,1)S(1)}, bf16[224,2432]{1,0:T(8,128)(2,1)S(1)}, u32[]{:S(2)}, u32[]{:S(2)}) %collective-permute-start.61) | collective-permute-done | bytes 1089568 | tf_op jit(solution)/shard_map/ppermute | solution.py:627
  (290 shorter events, 178.4 us)
Async XLA Ops:
  20.7 40.4 %collective-permute-start.4 = (bf16[448,896]{1,0:T(8,128)(2,1)S(1)}, bf16[448,896]{1,0:T(8,128)(2,1)S(1)}, u32[]{:S(2)}, u32[]{:S(2)}) collective-permute-start(bf16[448,896]{1,0:T(8,128)(2,1)S(1)} %bitcast.94), channel_id=1, source_target_pairs={{0,1},{1,0},{2,3},{3,2},{4,5},{5,4},{6,7},{7,6},{8,9},{9,8},{10,11... | collective-permute-start | bytes 2408456 | tf_op jit(solution)/shard_map/ppermute | solution.py:575
  60.6 31.7 %collective-permute-start.6 = (bf16[512,448]{1,0:T(8,128)(2,1)}, bf16[512,448]{1,0:T(8,128)(2,1)}, u32[]{:S(2)}, u32[]{:S(2)}) collective-permute-start(bf16[512,448]{1,0:T(8,128)(2,1)} %get-tuple-element.82.mine_ref.att_ref.refs_5_), channel_id=1, source_target_pairs={{0,1},{1,0},{2,3},{3,2},{4,5},{5,4},{6,7},{7,6},{8,9},{9,8},{10,11... | collective-permute-start | bytes 1376264 | tf_op jit(solution)/shard_map/ppermute | solution.py:575
  88.5 39.7 %collective-permute-start.18 = (bf16[512,2432]{1,0:T(8,128)(2,1)}, bf16[512,2432]{1,0:T(8,128)(2,1)}, u32[]{:S(2)}, u32[]{:S(2)}) collective-permute-start(bf16[512,2432]{1,0:T(8,128)(2,1)} %get-tuple-element.97.refs_4_), channel_id=1, source_target_pairs={{0,8},{8,0},{16,24},{24,16},{1,9},{9,1},{17,25},{25,17},{2,10},{10... | collective-permute-start | bytes 7471112 | tf_op jit(solution)/shard_map/ppermute | solution.py:579
  130.7 38.1 %collective-permute-start.8 = (bf16[512,896]{1,0:T(8,128)(2,1)}, bf16[512,896]{1,0:T(8,128)(2,1)}, u32[]{:S(2)}, u32[]{:S(2)}) collective-permute-start(bf16[512,896]{1,0:T(8,128)(2,1)} %get-tuple-element.86.mine_ref), channel_id=1, source_target_pairs={{0,1},{1,0},{2,3},{3,2},{4,5},{5,4},{6,7},{7,6},{8,9},{9,8},{10,11... | collective-permute-start | bytes 2752520 | tf_op jit(solution)/shard_map/ppermute | solution.py:575
  132.3 41.7 %collective-permute-start.9 = (bf16[512,896]{1,0:T(8,128)(2,1)}, bf16[512,896]{1,0:T(8,128)(2,1)}, u32[]{:S(2)}, u32[]{:S(2)}) collective-permute-start(bf16[512,896]{1,0:T(8,128)(2,1)} %get-tuple-element.85.mine_ref), channel_id=1, source_target_pairs={{0,1},{1,0},{2,3},{3,2},{4,5},{5,4},{6,7},{7,6},{8,9},{9,8},{10,11... | collective-permute-start | bytes 2752520 | tf_op jit(solution)/shard_map/ppermute | solution.py:575
  143.8 59.3 %collective-permute-start.25 = (bf16[896,576]{0,1:T(8,128)(2,1)S(1)}, bf16[896,576]{0,1:T(8,128)(2,1)}, u32[]{:S(2)}, u32[]{:S(2)}) collective-permute-start(bf16[896,576]{0,1:T(8,128)(2,1)S(1)} %bitcast.81), channel_id=1, source_target_pairs={{0,1},{1,0},{2,3},{3,2},{4,5},{5,4},{6,7},{7,6},{8,9},{9,8},{10,11... | collective-permute-start | bytes 3096584 | tf_op jit(solution)/shard_map/ppermute | solution.py:575
  156.1 59.7 %collective-permute-start.5 = (bf16[512,896]{1,0:T(8,128)(2,1)}, bf16[512,896]{1,0:T(8,128)(2,1)}, u32[]{:S(2)}, u32[]{:S(2)}) collective-permute-start(bf16[512,896]{1,0:T(8,128)(2,1)} %get-tuple-element.81), channel_id=1, source_target_pairs={{0,1},{1,0},{2,3},{3,2},{4,5},{5,4},{6,7},{7,6},{8,9},{9,8},{10,11... | collective-permute-start | bytes 2752520 | tf_op jit(solution)/shard_map/ppermute | solution.py:575
  156.7 101.4 %collective-permute-start.7 = (bf16[512,896]{1,0:T(8,128)(2,1)}, bf16[512,896]{1,0:T(8,128)(2,1)}, u32[]{:S(2)}, u32[]{:S(2)}) collective-permute-start(bf16[512,896]{1,0:T(8,128)(2,1)} %get-tuple-element.84), channel_id=1, source_target_pairs={{0,1},{1,0},{2,3},{3,2},{4,5},{5,4},{6,7},{7,6},{8,9},{9,8},{10,11... | collective-permute-start | bytes 2752520 | tf_op jit(solution)/shard_map/ppermute | solution.py:575
  186.9 34.2 %collective-permute-start.27 = (bf16[512,128]{1,0:T(8,128)(2,1)}, bf16[512,128]{1,0:T(8,128)(2,1)S(1)}, u32[]{:S(2)}, u32[]{:S(2)}) collective-permute-start(bf16[512,128]{1,0:T(8,128)(2,1)} %get-tuple-element.114), channel_id=1, source_target_pairs={{2,0},{4,2},{6,4},{3,1},{5,3},{7,5},{10,8},{12,10},{14,12},{11,9},... | collective-permute-start | bytes 393224 | tf_op jit(solution)/shard_map/ppermute | solution.py:595
  188.2 32.9 %collective-permute-start.28 = (bf16[512,128]{1,0:T(8,128)(2,1)}, bf16[512,128]{1,0:T(8,128)(2,1)}, u32[]{:S(2)}, u32[]{:S(2)}) collective-permute-start(bf16[512,128]{1,0:T(8,128)(2,1)} %get-tuple-element.115), channel_id=1, source_target_pairs={{4,0},{6,2},{5,1},{7,3},{12,8},{14,10},{13,9},{15,11},{20,16},{22,... | collective-permute-start | bytes 393224 | tf_op jit(solution)/shard_map/ppermute | solution.py:595
  203.1 36.1 %collective-permute-start.29 = (bf16[512,128]{1,0:T(8,128)(2,1)}, bf16[512,128]{1,0:T(8,128)(2,1)}, u32[]{:S(2)}, u32[]{:S(2)}) collective-permute-start(bf16[512,128]{1,0:T(8,128)(2,1)} %get-tuple-element.116), channel_id=1, source_target_pairs={{6,0},{7,1},{14,8},{15,9},{22,16},{23,17},{30,24},{31,25}} | collective-permute-start | bytes 393224 | tf_op jit(solution)/shard_map/ppermute | solution.py:595
  221.1 40.0 %collective-permute-start.36 = (bf16[2,224,512]{2,1,0:T(8,128)(2,1)}, bf16[2,224,512]{2,1,0:T(8,128)(2,1)S(1)}, u32[]{:S(2)}, u32[]{:S(2)}) collective-permute-start(bf16[2,224,512]{2,1,0:T(8,128)(2,1)} %dynamic-slice_bitcast_fusion.3), channel_id=1, source_target_pairs={{0,8},{8,0},{16,24},{24,16},{1,9},{9,1},{17,25},{25,17},{2,10},{10... | collective-permute-start | bytes 1376264 | tf_op jit(solution)/shard_map/ppermute | solution.py:579
  221.1 40.2 %collective-permute-start.37 = (bf16[2,224,512]{2,1,0:T(8,128)(2,1)}, bf16[2,224,512]{2,1,0:T(8,128)(2,1)S(1)}, u32[]{:S(2)}, u32[]{:S(2)}) collective-permute-start(bf16[2,224,512]{2,1,0:T(8,128)(2,1)} %dynamic-slice_bitcast_fusion.2), channel_id=1, source_target_pairs={{0,8},{8,0},{16,24},{24,16},{1,9},{9,1},{17,25},{25,17},{2,10},{10... | collective-permute-start | bytes 1376264 | tf_op jit(solution)/shard_map/ppermute | solution.py:579
  247.2 31.7 %collective-permute-start.26 = (bf16[512,448]{1,0:T(8,128)(2,1)S(1)}, bf16[512,448]{1,0:T(8,128)(2,1)}, u32[]{:S(2)}, u32[]{:S(2)}) collective-permute-start(bf16[512,448]{1,0:T(8,128)(2,1)S(1)} %copy-done.5), channel_id=1, source_target_pairs={{0,1},{1,0},{2,3},{3,2},{4,5},{5,4},{6,7},{7,6},{8,9},{9,8},{10,11... | collective-permute-start | bytes 1376264 | tf_op jit(solution)/shard_map/ppermute | solution.py:575
  261.2 38.4 %collective-permute-start.38 = (bf16[512,448]{1,0:T(8,128)(2,1)S(1)}, bf16[512,448]{1,0:T(8,128)(2,1)}, u32[]{:S(2)}, u32[]{:S(2)}) collective-permute-start(bf16[512,448]{1,0:T(8,128)(2,1)S(1)} %copy-done.5), channel_id=1, source_target_pairs={{0,8},{8,0},{16,24},{24,16},{1,9},{9,1},{17,25},{25,17},{2,10},{10... | collective-permute-start | bytes 1376264 | tf_op jit(solution)/shard_map/ppermute | solution.py:579
  307.5 100.8 %collective-permute-start.66 = (bf16[224,2432]{1,0:T(8,128)(2,1)}, bf16[224,2432]{1,0:T(8,128)(2,1)S(1)}, u32[]{:S(2)}, u32[]{:S(2)}) collective-permute-start(bf16[224,2432]{1,0:T(8,128)(2,1)} %get-tuple-element.143), channel_id=1, source_target_pairs={{0,16},{8,24},{16,0},{24,8},{1,17},{9,25},{17,1},{25,9},{2,18},{10... | collective-permute-start | bytes 3268616 | tf_op jit(solution)/shard_map/ppermute | solution.py:585
  309.4 102.3 %collective-permute-start.62 = (bf16[224,2432]{1,0:T(8,128)(2,1)}, bf16[224,2432]{1,0:T(8,128)(2,1)S(1)}, u32[]{:S(2)}, u32[]{:S(2)}) collective-permute-start(bf16[224,2432]{1,0:T(8,128)(2,1)} %get-tuple-element.141), channel_id=1, source_target_pairs={{0,16},{8,24},{16,0},{24,8},{1,17},{9,25},{17,1},{25,9},{2,18},{10... | collective-permute-start | bytes 3268616 | tf_op jit(solution)/shard_map/ppermute | solution.py:585
  319.0 43.9 %collective-permute-start.54 = (bf16[224,448]{1,0:T(8,128)(2,1)}, bf16[224,448]{1,0:T(8,128)(2,1)S(1)}, u32[]{:S(2)}, u32[]{:S(2)}) collective-permute-start(bf16[224,448]{1,0:T(8,128)(2,1)} %get-tuple-element.137), channel_id=1, source_target_pairs={{0,16},{8,24},{16,0},{24,8},{1,17},{9,25},{17,1},{25,9},{2,18},{10... | collective-permute-start | bytes 602120 | tf_op jit(solution)/shard_map/ppermute | solution.py:585
  320.8 46.3 %collective-permute-start.40 = (bf16[224,448]{1,0:T(8,128)(2,1)}, bf16[224,448]{1,0:T(8,128)(2,1)S(1)}, u32[]{:S(2)}, u32[]{:S(2)}) collective-permute-start(bf16[224,448]{1,0:T(8,128)(2,1)} %get-tuple-element.131), channel_id=1, source_target_pairs={{0,16},{8,24},{16,0},{24,8},{1,17},{9,25},{17,1},{25,9},{2,18},{10... | collective-permute-start | bytes 602120 | tf_op jit(solution)/shard_map/ppermute | solution.py:585
  411.9 47.4 %collective-permute-start.63 = (bf16[224,2432]{1,0:T(8,128)(2,1)S(1)}, bf16[224,2432]{1,0:T(8,128)(2,1)S(1)}, u32[]{:S(2)}, u32[]{:S(2)}) collective-permute-start(bf16[224,2432]{1,0:T(8,128)(2,1)S(1)} %fusion.1), channel_id=1, source_target_pairs={{0,2},{6,4},{1,3},{7,5},{8,10},{14,12},{9,11},{15,13},{16,18},{22,... | collective-permute-start | bytes 3268616 | tf_op jit(solution)/shard_map/ppermute | solution.py:621
  426.7 54.5 %collective-permute-start.59 = (bf16[224,2432]{1,0:T(8,128)(2,1)S(1)}, bf16[224,2432]{1,0:T(8,128)(2,1)S(1)}, u32[]{:S(2)}, u32[]{:S(2)}) collective-permute-start(bf16[224,2432]{1,0:T(8,128)(2,1)S(1)} %fusion), channel_id=1, source_target_pairs={{0,2},{6,4},{1,3},{7,5},{8,10},{14,12},{9,11},{15,13},{16,18},{22,... | collective-permute-start | bytes 3268616 | tf_op jit(solution)/shard_map/ppermute | solution.py:621
  436.4 46.0 %collective-permute-start.68 = (bf16[224,2432]{1,0:T(8,128)(2,1)S(1)}, bf16[224,2432]{1,0:T(8,128)(2,1)S(1)}, u32[]{:S(2)}, u32[]{:S(2)}) collective-permute-start(bf16[224,2432]{1,0:T(8,128)(2,1)S(1)} %add_convert_fusion.1), channel_id=1, source_target_pairs={{2,4},{4,2},{3,5},{5,3},{10,12},{12,10},{11,13},{13,11},{18,20},{2... | collective-permute-start | bytes 3268616 | tf_op jit(solution)/shard_map/ppermute | solution.py:623
  484.3 52.7 %collective-permute-start.65 = (bf16[224,2432]{1,0:T(8,128)(2,1)S(1)}, bf16[224,2432]{1,0:T(8,128)(2,1)S(1)}, u32[]{:S(2)}, u32[]{:S(2)}) collective-permute-start(bf16[224,2432]{1,0:T(8,128)(2,1)S(1)} %add_convert_fusion.2), channel_id=1, source_target_pairs={{2,0},{4,6},{3,1},{5,7},{10,8},{12,14},{11,9},{13,15},{18,16},{20,... | collective-permute-start | bytes 3268616 | tf_op jit(solution)/shard_map/ppermute | solution.py:627
  485.8 72.6 %collective-permute-start.61 = (bf16[224,2432]{1,0:T(8,128)(2,1)S(1)}, bf16[224,2432]{1,0:T(8,128)(2,1)S(1)}, u32[]{:S(2)}, u32[]{:S(2)}) collective-permute-start(bf16[224,2432]{1,0:T(8,128)(2,1)S(1)} %add_convert_fusion.4), channel_id=1, source_target_pairs={{2,0},{4,6},{3,1},{5,7},{10,8},{12,14},{11,9},{13,15},{18,16},{20,... | collective-permute-start | bytes 3268616 | tf_op jit(solution)/shard_map/ppermute | solution.py:627
  (93 other events, 1314.0 us)

commit v4 on v3

--- a/solution.py
+++ b/solution.py
@@ -6,6 +6,7 @@
 from jax.experimental import pallas as pl
 from jax.experimental.pallas import tpu as pltpu
 from jax.sharding import PartitionSpec as P
+
 
 EPS = 1e-06
 THETA = 1000000.0
@@ -145,11 +146,9 @@
             )
             acc_ref[rows, :] = acc_ref[rows, :] * factor + dot(values, weights.astype(BF))
 
-    block(0, True)
-
-    @pl.loop(1, count)
+    @pl.loop(0, count)
     def _(back):
-        masked = last_first > place - back * tokens
+        masked = (back == 0) | (last_first > place - back * tokens)
 
         @pl.when(masked)
         def _():
@@ -264,26 +263,25 @@
             gacc_ref[rows, :] = gacc_ref[rows, :] + dot(keys_t, grad_scores)
         return jnp.concatenate([grad_key, grad_value], axis=1)
 
-    own_ref[...] = block(0, True)
-
-    @pl.loop(1, n)
+    @pl.loop(0, n)
     def _(back):
-        masked = last_first > place - back * tokens
+        masked = (back == 0) | (last_first > place - back * tokens)
 
         @pl.when(back >= count)
         def _():
-            sent_ref[back - 1] = jnp.zeros((tokens, 2 * HD), BF)
+            sent_ref[back] = jnp.zeros((tokens, 2 * HD), F32)
 
         @pl.when((back < count) & masked)
         def _():
-            sent_ref[back - 1] = block(back, True).astype(BF)
+            sent_ref[back] = block(back, True)
 
         @pl.when((back < count) & jnp.logical_not(masked))
         def _():
-            sent_ref[back - 1] = block(back, False).astype(BF)
-
+            sent_ref[back] = block(back, False)
+
+    own_ref[...] = sent_ref[0]
     for s in range(n - 1):
-        sent_refs[s][...] = sent_ref[s]
+        sent_refs[s][...] = sent_ref[s + 1].astype(BF)
     cosine, sine = cos_ref[0], sin_ref[0]
     for h in range(heads):
         rows = slice(h * HD, (h + 1) * HD)
@@ -331,7 +329,7 @@
             + [full(*pair)] * (n - 1),
             scratch_shapes=[
                 pltpu.VMEM((n,) + pair, BF),
-                pltpu.VMEM((n - 1,) + pair, BF),
+                pltpu.VMEM((n,) + pair, F32),
                 pltpu.VMEM((width, tokens), BF),
                 pltpu.VMEM((heads, tokens, HD), BF),
                 pltpu.VMEM((heads, tokens, HD), BF),
@@ -360,6 +358,7 @@
 
 def mlp_kernel(
     total,
+    places_ref,
     x_ref,
     mine_ref,
     other_ref,
@@ -371,12 +370,12 @@
     up_ref,
     down_ref,
     middle_ref,
-    hid_t_ref,
-    act_ref,
-    gg_ref,
-    gu_ref,
+    near_ref,
+    far_ref,
+    acts_ref,
     part_ref,
     back_ref,
+    turned_ref,
     hidden_ref,
     acc_ref,
     bacc_ref,
@@ -391,7 +390,16 @@
         middle_ref[...] = middle
         hidden = middle * inverse_rms(middle) * gain_ref[...]
         hidden_ref[...] = hidden.astype(BF)
-        hid_t_ref[...] = hidden.T.astype(BF)
+        turned_ref[0] = hidden.T.astype(BF)
+        turned_ref[1] = cot_ref[0].astype(F32).T.astype(BF)
+        shares = near_ref.shape[1]
+        size = near_ref.shape[2]
+        for k in range(2):
+            for i in range(shares):
+                near = pl.multiple_of(places_ref[i] * size, 16)
+                far = pl.multiple_of(places_ref[shares + i] * size, 16)
+                near_ref[k, i] = turned_ref[k, pl.ds(near, size), :]
+                far_ref[k, i] = turned_ref[k, pl.ds(far, size), :]
         acc_ref[...] = jnp.zeros_like(acc_ref)
         bacc_ref[...] = jnp.zeros_like(bacc_ref)
 
@@ -412,9 +420,9 @@
     act = (silu * up).astype(BF)
     gg = (grad_act * up * sigma * (1.0 + gate * (1.0 - sigma))).astype(BF)
     gu = (grad_act * silu).astype(BF)
-    act_ref[...] = act
-    gg_ref[...] = gg
-    gu_ref[...] = gu
+    acts_ref[0] = act
+    acts_ref[1] = gg
+    acts_ref[2] = gu
     acc_ref[...] += dot(act, wd)
     bacc_ref[...] += dot_nt(gg, wg) + dot_nt(gu, wu)
 
@@ -424,15 +432,18 @@
         back_ref[...] = bacc_ref[...].astype(BF)
 
 
-def mlp(seq, x, mine, other, wo, wx, gain, cot, wg, wu, wd, tile=512):
+def mlp(seq, places, shares, x, mine, other, wo, wx, gain, cot, wg, wu, wd, tile=512):
+    n_row = places.shape[0] // 2
     _, tokens, model = x.shape
     ff = wg.shape[1]
-    cols = pl.BlockSpec((tokens, tile), lambda j: (0, j))
-    columns = pl.BlockSpec((model, tile), lambda j: (0, j))
+    columns = pl.BlockSpec((model, tile), lambda j, p: (0, j))
+    lefts = (2, n_row, shares, tokens)
     return pl.pallas_call(
         functools.partial(mlp_kernel, ff),
-        grid=(pl.cdiv(ff, tile),),
-        in_specs=[
+        grid_spec=pltpu.PrefetchScalarGridSpec(
+            num_scalar_prefetch=1,
+            grid=(pl.cdiv(ff, tile),),
+            in_specs=[
             row_of(x, seq),
             whole(mine),
             whole(other),
@@ -442,18 +453,30 @@
             row_of(cot, seq),
             columns,
             columns,
-            pl.BlockSpec((tile, model), lambda j: (j, 0)),
+            pl.BlockSpec((tile, model), lambda j, p: (j, 0)),
         ],
-        out_specs=[full(tokens, model), full(model, tokens)]
-        + [cols] * 3
-        + [full(tokens, model)] * 2,
-        out_shape=[shape_of((tokens, model), F32), shape_of((model, tokens), BF)]
-        + [shape_of((tokens, ff), BF)] * 3
-        + [shape_of((tokens, model), BF)] * 2,
+        out_specs=[
+            full(tokens, model),
+            full(*lefts),
+            full(*lefts),
+            pl.BlockSpec((3, tokens, tile), lambda j, p: (0, 0, j)),
+            full(tokens, model),
+            full(tokens, model),
+        ],
         scratch_shapes=[
+            pltpu.VMEM((2, model, tokens), BF),
             pltpu.VMEM((tokens, model), BF),
             pltpu.VMEM((tokens, model), F32),
             pltpu.VMEM((tokens, model), F32),
+        ],
+        ),
+        out_shape=[
+            shape_of((tokens, model), F32),
+            shape_of(lefts, BF),
+            shape_of(lefts, BF),
+            shape_of((3, tokens, ff), BF),
+            shape_of((tokens, model), BF),
+            shape_of((tokens, model), BF),
         ],
         cost_estimate=pl.CostEstimate(
             flops=12 * tokens * model * ff,
@@ -462,45 +485,93 @@
         ),
         compiler_params=params(),
         name="mlp",
-    )(x, mine, other, wo, wx, gain, cot, wg, wu, wd)
-
-
-def weight_kernel(count, shares, places_ref, *refs):
-    lefts, rights, outs = refs[: 2 * count], refs[2 * count : 4 * count], refs[4 * count :]
+    )(places, x, mine, other, wo, wx, gain, cot, wg, wu, wd)
+
+
+def weight_kernel(count, shares, pieces, *refs):
+    lefts, rights, outs = refs[:count], refs[count : 2 * count], refs[2 * count :]
     for share in range(shares):
         total = None
-        for k in range(2 * count):
-            place = places_ref[share if k < count else shares + share]
-            part = dot(lefts[k][place], rights[k][...])
+        for k in range(count):
+            part = dot(lefts[k][0, share], rights[k][0])
             total = part if total is None else total + part
-        outs[share][...] = total.astype(outs[share].dtype)
-
-
-def weight_grad(places, lefts, rights, tile):
-    count = len(lefts) // 2
+        size = total.shape[0] // pieces
+        for piece in range(pieces):
+            out = outs[share * pieces + piece]
+            out[...] = total[piece * size : (piece + 1) * size].astype(out.dtype)
+
+
+def weight_grad(lefts, kind, rights, which, pieces, tile=512):
+    count = len(lefts)
+    _, shares, rows, tokens = lefts[0].shape
+    ff = rights[0].shape[2]
+    tile = min(tile, ff)
+    left = pl.BlockSpec((1, shares, rows, tokens), lambda j: (kind, 0, 0, 0))
+    cols = pl.BlockSpec((1, tokens, tile), lambda j: (which, 0, j))
+    out = pl.BlockSpec((rows // pieces, tile), lambda j: (0, j))
+    shape = (rows // pieces, ff)
+    outs = pl.pallas_call(
+        functools.partial(weight_kernel, count, shares, pieces),
+        grid=(pl.cdiv(ff, tile),),
+        in_specs=[left] * count + [cols] * count,
+        out_specs=[out] * (shares * pieces),
+        out_shape=[shape_of(shape, F32)] * pieces + [shape_of(shape, BF)] * ((shares - 1) * pieces),
+        cost_estimate=pl.CostEstimate(
+            flops=2 * count * shares * rows * tokens * ff,
+            transcendentals=0,
+            bytes_accessed=2 * count * tokens * ff + 6 * rows * ff,
+        ),
+        compiler_params=params(),
+        name="weight_grad",
+    )(*lefts, *rights)
+    return [outs[k * pieces : (k + 1) * pieces] for k in range(shares)]
+
+
+def share_kernel(kinds, places_ref, *refs):
+    near_ref, far_ref = refs[-2:]
+    shares, size = near_ref.shape[1], near_ref.shape[2]
+    for kind, count in enumerate(kinds):
+        start = 2 * sum(kinds[:kind])
+        lefts, rights = refs[start : start + count], refs[start + count : start + 2 * count]
+        for out_ref, base in ((near_ref, 0), (far_ref, shares)):
+            for i in range(shares):
+                total = None
+                for left, right in zip(lefts, rights):
+                    place = pl.multiple_of(places_ref[base + i] * size, 16)
+                    part = dot(left[0, pl.ds(place, size), :], right[...])
+                    total = part if total is None else total + part
+                out_ref[kind, i] = total
+
+
+def share_grads(places, share, groups):
     shares = places.shape[0] // 2
-    _, rows, tokens = lefts[0].shape
-    ff = rights[0].shape[1]
-    tile = min(tile, ff)
-    cols = pl.BlockSpec((tokens, tile), lambda j, p: (0, j))
-    out = pl.BlockSpec((rows, tile), lambda j, p: (0, j))
+    operands, specs = [], []
+    for group in groups:
+        for left, index, _ in group:
+            operands.append(left)
+            specs.append(row_of(left, index))
+        for _, _, right in group:
+            operands.append(right)
+            specs.append(whole(right))
+    width = groups[0][0][2].shape[1]
+    shape = (len(groups), shares, share, width)
     return pl.pallas_call(
-        functools.partial(weight_kernel, count, shares),
+        functools.partial(share_kernel, [len(g) for g in groups]),
         grid_spec=pltpu.PrefetchScalarGridSpec(
             num_scalar_prefetch=1,
-            grid=(pl.cdiv(ff, tile),),
-            in_specs=[whole(a) for a in lefts] + [cols] * len(rights),
-            out_specs=[out] * shares,
-        ),
-        out_shape=[shape_of((rows, ff), F32)] + [shape_of((rows, ff), BF)] * (shares - 1),
+            grid=(1,),
+            in_specs=specs,
+            out_specs=[full(*shape), full(*shape)],
+        ),
+        out_shape=[shape_of(shape, F32), shape_of(shape, F32)],
         cost_estimate=pl.CostEstimate(
-            flops=4 * count * shares * rows * tokens * ff,
+            flops=4 * len(operands) * shares * share * width * operands[0].shape[-1],
             transcendentals=0,
-            bytes_accessed=4 * count * tokens * ff + 6 * rows * ff,
+            bytes_accessed=sum(o.size * 2 for o in operands),
         ),
         compiler_params=params(),
-        name="weight_grad",
-    )(places, *lefts, *rights)
+        name="share_grads",
+    )(places, *operands)
 
 
 def pair_back_kernel(own_ref, cos_ref, sin_ref, *refs):
@@ -545,7 +616,7 @@
 
 
 def input_back(seq, gq, gqx, gkv, gkvx, w, wx, x, gain, gmid, so_far):
-    seqs, tokens, model = x.shape
+    _, tokens, model = x.shape
     operands = [gq, gqx, gkv, gkvx, w, wx, x, gain, gmid]
     specs = [whole(a) for a in operands]
     specs[6] = row_of(x, seq)
@@ -595,21 +666,15 @@
     return lax.ppermute(values, "ctx", [(i + shift, i) for i in range(n - shift)])
 
 
-def tree_sum(terms):
-    if len(terms) == 1:
-        return terms[0]
-    if len(terms) % 2:
-        return terms[0] + tree_sum(terms[1:])
-    return tree_sum(terms[0::2]) + tree_sum(terms[1::2])
-
-
-def ring_sum(part):
-    n = lax.axis_size("ctx")
-    mine = part.astype(BF)
-    terms = [mine]
-    for shift in range(1, n):
-        terms.append(lax.ppermute(mine, "ctx", [(i, (i + shift) % n) for i in range(n)]))
-    return tree_sum([t.astype(F32) for t in terms])
+def doubling_sum(part, axis, size, stride, dtype):
+    n = lax.axis_size(axis)
+    bit = 1
+    while bit < size:
+        mine = part.astype(dtype)
+        pairs = [(i, (i // stride ^ bit) * stride + i % stride) for i in range(n)]
+        part = mine.astype(F32) + lax.ppermute(mine, axis, pairs).astype(F32)
+        bit *= 2
+    return part
 
 
 def line_sum(part):
@@ -618,7 +683,8 @@
     me = lax.axis_index("ctx")
     for step in range(half - 1):
         pairs = [(step, step + 1), (n - 1 - step, n - 2 - step)]
-        part = part + lax.ppermute(part.astype(BF), "ctx", pairs).astype(F32)
+        moved = lax.ppermute(part.astype(BF), "ctx", pairs)
+        part = part + moved.astype(F32)
     mine = part.astype(BF)
     moved = lax.ppermute(mine, "ctx", [(half - 1, half), (half, half - 1)])
     total = (mine.astype(F32) + moved.astype(F32)).astype(BF)
@@ -629,7 +695,7 @@
     return total.astype(F32)
 
 
-def shards(
+def layer(
     block_input,
     positions,
     gain_attn,
@@ -667,121 +733,116 @@
     ).astype(jnp.int32)
     query_first = query_first[:, None, :]
     rows_from = (row + jnp.arange(n_row, dtype=jnp.int32)) % n_row
-    places = jnp.concatenate([rows_from * 2 + core, rows_from]).astype(jnp.int32)
-
-    def for_other_core(turned):
-        split = turned.reshape(n_row, 2, share, turned.shape[1])
-        return core_other(lax.dynamic_index_in_dim(split, 1 - core, 1, keepdims=False))
-
-    def blocks(turned):
-        return turned.reshape(n_dp, share, turned.shape[1])
-
-    def gradient(lefts, lefts_other, rights, rights_other, tile=512):
-        own, *sent = weight_grad(places, lefts + lefts_other, rights + rights_other, tile)
-        return own, sent
-
-    def over_rows(own, sent):
-        for shift in range(1, n_row):
-            own = own + row_back(sent[shift - 1], shift).astype(F32)
-        return own
+    places = jnp.concatenate([rows_from * 2 + core, rows_from * 2 + 1 - core]).astype(jnp.int32)
 
     hidden_t, queries, key_value = project(
         block_input, gain_one, proj_qkv, b_qkv, cosine, sine, heads_width
     )
     pairs = [key_value] + [earlier(key_value, shift) for shift in range(1, n_ctx)]
-    cot_t = jnp.swapaxes(cotangent, 1, 2)
-    cot_other = [for_other_core(cot_t[i]) for i in every]
-    hidden_other = [for_other_core(hidden_t[i]) for i in every]
-
-    attended, lse = zip(*[attend(i, info, queries, pairs, query_first) for i in every])
-    att_moved = [tp_other(a) for a in attended]
-    middle, hid_t, acts, gates, ups, part, back = zip(
-        *[
-            mlp(
-                i,
-                block_input,
-                attended[i],
-                att_moved[i],
-                proj_out,
-                other_out,
-                gain_two,
-                cotangent,
-                w_gate,
-                w_up,
-                w_down,
-            )
-            for i in every
-        ]
-    )
-    back_moved = [tp_other(b) for b in back]
-    part_moved = [tp_other(p) for p in part]
+    attended, lse, att_moved = [], [], []
+    for i in every:
+        out, log = attend(i, info, queries, pairs, query_first)
+        attended.append(out)
+        lse.append(log)
+        att_moved.append(tp_other(out))
+    middle, near, far, acts, part, back = [], [], [], [], [], []
+    for i in every:
+        outs = mlp(
+            i,
+            places,
+            share,
+            block_input,
+            attended[i],
+            att_moved[i],
+            proj_out,
+            other_out,
+            gain_two,
+            cotangent,
+            w_gate,
+            w_up,
+            w_down,
+        )
+        for group, out in zip((middle, near, far, acts, part, back), outs):
+            group.append(out)
+    back_moved, part_moved, lefts, rights = [], [], list(near), list(acts)
+    for i in every:
+        back_moved.append(tp_other(back[i]))
+        part_moved.append(tp_other(part[i]))
+        lefts.append(core_other(far[i]))
+        rights.append(core_other(acts[i]))
     output = jnp.stack(
         [
             (middle[i] + (part[i].astype(F32) + part_moved[i].astype(F32))).astype(BF)
             for i in every
         ]
     )
-    hid_other = [for_other_core(h) for h in hid_t]
-    hid_blocks = [blocks(h) for h in hid_t]
-    acts_other, gates_other, ups_other = (
-        [core_other(a) for a in group] for group in (acts, gates, ups)
-    )
-    down = gradient([blocks(cot_t[i]) for i in every], cot_other, list(acts), acts_other)
-    gate = gradient(hid_blocks, hid_other, list(gates), gates_other)
-    up = gradient(hid_blocks, hid_other, list(ups), ups_other)
-    back_moved, down, gate, up = lax.optimization_barrier((back_moved, down, gate, up))
-    down, gate, up = over_rows(*down), over_rows(*gate), over_rows(*up)
-    grad_down, grad_gate, grad_up = line_sum(down).T, line_sum(gate), line_sum(up)
-
-    results = [
-        attend_back(
-            i,
-            info,
-            back[i],
-            back_moved[i],
-            middle[i],
-            cotangent,
-            gain_two,
-            proj_out,
-            attended[i],
-            queries,
-            lse[i],
-            query_first,
-            cosine,
-            sine,
-            pairs,
+    pieces = 2 if share % 32 == 0 else 1
+    totals = []
+    for kind, which in ((1, 0), (0, 1), (0, 2)):
+        owns, *sents = weight_grad(lefts, kind, rights, which, pieces)
+        total = []
+        for piece, own in enumerate(owns):
+            for shift in range(1, n_row):
+                moved = row_back(sents[shift - 1][piece], shift)
+                own = own + moved.astype(F32)
+            total.append(line_sum(own))
+        totals.append(jnp.concatenate(total, axis=0))
+    grad_down, grad_gate, grad_up = totals[0].T, totals[1], totals[2]
+
+    results = []
+    for i in every:
+        results.append(
+            attend_back(
+                i,
+                info,
+                back[i],
+                back_moved[i],
+                middle[i],
+                cotangent,
+                gain_two,
+                proj_out,
+                attended[i],
+                queries,
+                lse[i],
+                query_first,
+                cosine,
+                sine,
+                pairs,
+            )
         )
-        for i in every
-    ]
     grad_mid, grad_mid_t, gain_mlp_parts, grad_q, bias_q, grad_own = zip(*[r[:6] for r in results])
     grad_q_moved = [tp_other(g) for g in grad_q]
-    pair_results = [
-        pair_back(
-            i,
-            grad_own[i],
-            [later(results[i][5 + shift], shift) for shift in range(1, n_ctx)],
-            cosine,
-            sine,
-        )
-        for i in every
-    ]
-    grad_kv, bias_kv = zip(*pair_results)
+    grad_kv, bias_kv = zip(
+        *[
+            pair_back(
+                i,
+                grad_own[i],
+                [later(results[i][5 + shift], shift) for shift in range(1, n_ctx)],
+                cosine,
+                sine,
+            )
+            for i in every
+        ]
+    )
     grad_kv_moved = [tp_other(g) for g in grad_kv]
 
-    mid_blocks = [blocks(g) for g in grad_mid_t]
-    mid_other = [for_other_core(g) for g in grad_mid_t]
-    hidden_blocks = [blocks(hidden_t[i]) for i in every]
-    grad_out = over_rows(
-        *gradient(mid_blocks, mid_other, list(attended), [core_other(a) for a in attended])
+    def summed(groups):
+        mine, theirs = share_grads(places, share, groups)
+        total = mine + core_other(theirs)
+        own = total[:, 0]
+        for shift in range(1, n_row):
+            own = own + row_back(total[:, shift].astype(BF), shift).astype(F32)
+        return doubling_sum(own, "ctx", n_ctx, 1, BF)
+
+    grad_out, qkv_q = summed(
+        [
+            [(grad_mid_t[i][None], 0, attended[i]) for i in every],
+            [(hidden_t, i, grad_q[i]) for i in every],
+        ],
     )
-    grad_out = ring_sum(grad_out).T[None]
-    qkv_q = over_rows(
-        *gradient(hidden_blocks, hidden_other, list(grad_q), [core_other(g) for g in grad_q])
-    )
-    qkv_kv = over_rows(
-        *gradient(hidden_blocks, hidden_other, list(grad_kv), [core_other(g) for g in grad_kv])
-    )
-    grad_qkv = jnp.concatenate([ring_sum(qkv_q), ring_sum(qkv_kv)], axis=1)[:, None, :]
+    grad_out = grad_out.T[None]
+    (qkv_kv,) = summed([[(hidden_t, i, grad_kv[i]) for i in every]])
+    grad_qkv = jnp.concatenate([qkv_q, qkv_kv], axis=1)[:, None, :]
 
     grad_input, gain_attn_parts = None, []
     for i in every:
@@ -800,20 +861,12 @@
         )
         gain_attn_parts.append(gain_part)
 
-    def small_sum(values):
-        values = values + core_other(values)
-        values = tree_sum([values] + [row_back(values, shift) for shift in range(1, n_row)])
-        ring = [
-            lax.ppermute(values, "ctx", [(i, (i + shift) % n_ctx) for i in range(n_ctx)])
-            for shift in range(1, n_ctx)
-        ]
-        return tree_sum([values] + ring)[0]
-
-    small = small_sum(
-        jnp.concatenate(
-            [sum(gain_attn_parts), sum(gain_mlp_parts), sum(bias_q), sum(bias_kv)], axis=1
-        )
+    small = jnp.concatenate(
+        [sum(gain_attn_parts), sum(gain_mlp_parts), sum(bias_q), sum(bias_kv)], axis=1
     )
+    small = small + core_other(small)
+    small = doubling_sum(small, "dp", n_row, 2, F32)
+    small = doubling_sum(small, "ctx", n_ctx, 1, F32)[0]
 
     def my_part(values):
         size = values.shape[0] // n_dp
@@ -859,4 +912,4 @@
         P("dp", "tp"),
         P("tp", "dp"),
     )
-    return jax.shard_map(shards, mesh=mesh, in_specs=in_specs, out_specs=out_specs, check_vma=False)
+    return jax.shard_map(layer, mesh=mesh, in_specs=in_specs, out_specs=out_specs, check_vma=False)

time: 569 us -> 558 us (0.981)
  starting transfers between devices: 78.7 us -> 91.9 us
  Pallas kernels: 170 us -> 161 us
  local copies, waits for them, and re-layouts: 27.2 us -> 18.2 us
    ppermute x12, waiting for transfers between devices: 22.1 us -> 58.7 us  [tp_other(): return lax.ppermute(values, 'tp', [(0, 1), (1, 0)])]
    ppermute x15 -> x13, waiting for transfers between devices: 77.8 us -> 58 us  [the longest x7 40.2 us: doubling_sum(): part = mine.astype(F32) + lax.ppermute(mine, axis, pairs).astype(F32)]
    ppermute x7 -> x8, waiting for transfers between devices: 54.6 us -> 40.9 us  [row_back(): return lax.ppermute(values, 'dp', pairs)]
    ppermute x15 -> x13, starting transfers between devices: 25.3 us -> 37.5 us  [the longest x7 29.4 us: doubling_sum(): part = mine.astype(F32) + lax.ppermute(mine, axis, pairs).astype(F32)]
    squeeze x8 -> x0, local copies, waits for them, and re-layouts: 7.83 us -> none  [for_other_core(): lax.dynamic_index_in_dim(split, 1 - core, 1, keepdims=False)]
    ppermute x21 -> x7, waiting for transfers between devices: 7.04 us -> 0.02 us  [core_other(): lax.ppermute(values, 'dp', [(i, i ^ 1) for i in range(lax.axis_size('dp'))])]
    ppermute x21 -> x7, starting transfers between devices: 7.48 us -> 0.78 us  [core_other(): lax.ppermute(values, 'dp', [(i, i ^ 1) for i in range(lax.axis_size('dp'))])]
    pallas_call x8 -> x7, Pallas kernels: 98.9 us -> 95 us  [the longest x2 55.5 us: mlp(): pl.pallas_call(functools.partial(mlp_kernel, ff), grid_spec=pltpu.Prefetc...]
  transfers between devices with their start and end apart: 70 -> 61, of which waited for: 22 -> 30; matrix products, arithmetic and copies ran while one was open for 7% -> 4% of each run, Pallas kernels for 29% -> 27%
where the time goes in v4:
time: 558 us; the launch traced here: 550 us
  waiting for transfers between devices  259 us (46%)
  Pallas kernels  161 us (29%)
  starting transfers between devices  91.9 us (16%)
  local copies, waits for them, and re-layouts  18.2 us (3%)
  other arithmetic  17.8 us (3%)
    ppermute x6, waiting for transfers between devices, line_sum(): moved = lax.ppermute(total, 'ctx', pairs)  65.4 us
    ppermute x12, waiting for transfers between devices, tp_other(): return lax.ppermute(values, 'tp', [(0, 1), (1, 0)])  58.7 us
    pallas_call x2, Pallas kernels, mlp(): pl.pallas_call(functools.partial(mlp_kernel, ff), grid_spec=pltpu.Prefetc...  55.5 us
    ppermute x8, waiting for transfers between devices, row_back(): return lax.ppermute(values, 'dp', pairs)  40.9 us
    ppermute x7, waiting for transfers between devices, doubling_sum(): part = mine.astype(F32) + lax.ppermute(mine, axis, pairs).astype(F32)  40.2 us
    ppermute x7, starting transfers between devices, doubling_sum(): part = mine.astype(F32) + lax.ppermute(mine, axis, pairs).astype(F32)  29.4 us
    pallas_call x3, Pallas kernels, weight_grad(): pl.pallas_call(functools.partial(weight_kernel, count, shares, pieces), g...  29.2 us
    ppermute x6, waiting for transfers between devices, later(): lax.ppermute(values, 'ctx', [(i + shift, i) for i in range(n - shift)])  28 us
  transfers between devices with their start and end apart: 61, of which 30 were waited for; matrix products, arithmetic and copies ran while one was open for 4% of the time, Pallas kernels for 27%

profile of v4, /device:TPU:0, one launch (start us, length us, event | category | flops | bytes accessed | tf_op | source)
XLA Modules:
  0.0 550.4 jit_solution(3384263760497848088)
XLA Ops:
  43.2 11.2 %attend.3 = (bf16[512,448]{1,0:T(8,128)(2,1)}, f32[8,512]{1,0:T(8,128)}) custom-call(s32[5]{0:T(128)} %pad_add_fusion.2.info_ref, bf16[2,448,512]{2,1,0:T(8,128)(2,1)} %get-tuple-element.71.q_ref, s32[2,1,512]{2,1,0:T(1,128)} %broadcast_in_dim.30.first_ref, bf16[2,512,128]{2,1,0:T(8,128)(2,1)} %get-tuple-element.72.refs_0_, bf16[2,512,128]{2,1,0:T(8,128)(2,1)} %copy-done.40, ...), custom_call_target="tpu_custom_call" | custom-call | flops 939524096 | bytes 3670016 | tf_op jit(solution)/shard_map/attend/pallas_call | solution.py:173
  56.6 27.5 %mlp.2 = (f32[512,896]{1,0:T(8,128)}, bf16[2,2,224,512]{3,2,1,0:T(8,128)(2,1)}, bf16[2,2,224,512]{3,2,1,0:T(8,128)(2,1)}, bf16[3,512,2432]{2,1,0:T(8,128)(2,1)},...) custom-call(s32[4]{0:T(128)} %pad_add_fusion.1.places_ref, bf16[2,512,896]{2,1,0:T(8,128)(2,1)} %x_ref.9, ...), custom_call_target="tpu_custom_call" | custom-call | flops 13388218368 | bytes 20545536 | tf_op jit(solution)/shard_map/mlp/pallas_call | solution.py:441
  84.3 28.0 %mlp.3 = (f32[512,896]{1,0:T(8,128)}, bf16[2,2,224,512]{3,2,1,0:T(8,128)(2,1)}, bf16[2,2,224,512]{3,2,1,0:T(8,128)(2,1)}, bf16[3,512,2432]{2,1,0:T(8,128)(2,1)},...) custom-call(s32[4]{0:T(128)} %pad_add_fusion.1.places_ref, bf16[2,512,896]{2,1,0:T(8,128)(2,1)} %x_ref.9, ...), custom_call_target="tpu_custom_call" | custom-call | flops 13388218368 | bytes 20545536 | tf_op jit(solution)/shard_map/mlp/pallas_call | solution.py:441
  116.2 19.9 %collective-permute-done.8.other_ref = bf16[512,896]{1,0:T(8,128)(2,1)S(1)} collective-permute-done((bf16[512,896]{1,0:T(8,128)(2,1)}, bf16[512,896]{1,0:T(8,128)(2,1)S(1)}, u32[]{:S(2)}, u32[]{:S(2)}) %collective-permute-start.8) | collective-permute-done | bytes 917536 | tf_op jit(solution)/shard_map/ppermute | solution.py:646
  137.1 12.9 %attend_back.2 = (f32[512,896]{1,0:T(8,128)}, bf16[896,512]{1,0:T(8,128)(2,1)}, f32[1,896]{1,0:T(1,128)}, bf16[512,448]{1,0:T(8,128)(2,1)}, f32[1,448]{1,0:T(1,1...) custom-call(s32[5]{0:T(128)} %pad_add_fusion.2.info_ref, ...), custom_call_target="tpu_custom_call" | custom-call | flops 2818572288 | bytes 7340032 | tf_op jit(solution)/shard_map/attend_back/pallas_call | solution.py:301
  159.5 17.7 %collective-permute-done.15.other_ref = bf16[512,896]{1,0:T(8,128)(2,1)} collective-permute-done((bf16[512,896]{1,0:T(8,128)(2,1)S(1)}, bf16[512,896]{1,0:T(8,128)(2,1)}, u32[]{:S(2)}, u32[]{:S(2)}) %collective-permute-start.15) | collective-permute-done | bytes 917536 | tf_op jit(solution)/shard_map/ppermute | solution.py:646
  178.7 13.0 %attend_back.3 = (f32[512,896]{1,0:T(8,128)}, bf16[896,512]{1,0:T(8,128)(2,1)}, f32[1,896]{1,0:T(1,128)}, bf16[512,448]{1,0:T(8,128)(2,1)}, f32[1,448]{1,0:T(1,1...) custom-call(s32[5]{0:T(128)} %pad_add_fusion.2.info_ref, ...), custom_call_target="tpu_custom_call" | custom-call | flops 2818572288 | bytes 7340032 | tf_op jit(solution)/shard_map/attend_back/pallas_call | solution.py:301
  220.8 13.3 %collective-permute-done.19.refs_2_ = bf16[512,128]{1,0:T(8,128)(2,1)} collective-permute-done((bf16[512,128]{1,0:T(8,128)(2,1)}, bf16[512,128]{1,0:T(8,128)(2,1)}, u32[]{:S(2)}, u32[]{:S(2)}) %collective-permute-start.19) | collective-permute-done | bytes 131104 | tf_op jit(solution)/shard_map/ppermute | solution.py:666
  286.4 10.7 %collective-permute-done.22 = f32[1,2368]{1,0:T(1,128)S(1)} collective-permute-done((f32[1,2368]{1,0:T(1,128)S(1)}, f32[1,2368]{1,0:T(1,128)S(1)}, u32[]{:S(2)}, u32[]{:S(2)}) %collective-permute-start.22) | collective-permute-done | bytes 9504 | tf_op jit(solution)/shard_map/ppermute | solution.py:675
  309.0 15.2 %collective-permute-start.24 = (f32[1,2368]{1,0:T(1,128)S(1)}, f32[1,2368]{1,0:T(1,128)S(1)}, u32[]{:S(2)}, u32[]{:S(2)}) collective-permute-start(f32[1,2368]{1,0:T(1,128)S(1)} %add.183), channel_id=1, source_target_pairs={{0,4},{2,6},{4,0},{6,2},{1,5},{3,7},{5,1},{7,3},{8,12},{10,14},{12... | collective-permute-start | bytes 28424 | tf_op jit(solution)/shard_map/ppermute | solution.py:675
  339.3 19.0 %collective-permute-done.28 = bf16[2,224,448]{2,1,0:T(8,128)(2,1)S(1)} collective-permute-done((bf16[2,224,448]{2,1,0:T(8,128)(2,1)S(1)}, bf16[2,224,448]{2,1,0:T(8,128)(2,1)S(1)}, u32[]{:S(2)}, u32[]{:S(2)}) %collective-permute-start.28) | collective-permute-done | bytes 401440 | tf_op jit(solution)/shard_map/ppermute | solution.py:675
  362.2 9.7 %weight_grad.3 = (f32[112,2432]{1,0:T(8,128)}, f32[112,2432]{1,0:T(8,128)}, bf16[112,2432]{1,0:T(8,128)(2,1)}, bf16[112,2432]{1,0:T(8,128)(2,1)}) custom-call(bf16[2,2,224,512]{3,2,1,0:T(8,128)(2,1)} %get-tuple-element.114.refs_0_, bf16[2,2,224,512]{3,2,1,0:T(8,128)(2,1)} %get-tuple-element.115.refs_1_, bf16[2,2,224,512]{3,2,1,0:T(8,128)(2,1)} %copy-done, ...), custom_call_target="tpu_custom_call" | custom-call | flops 4462739456 | bytes 13230080 | tf_op jit(solution)/shard_map/weight_grad/pallas_call | solution.py:513
  374.0 9.7 %weight_grad.4 = (f32[112,2432]{1,0:T(8,128)}, f32[112,2432]{1,0:T(8,128)}, bf16[112,2432]{1,0:T(8,128)(2,1)}, bf16[112,2432]{1,0:T(8,128)(2,1)}) custom-call(bf16[2,2,224,512]{3,2,1,0:T(8,128)(2,1)} %get-tuple-element.114.refs_0_, bf16[2,2,224,512]{3,2,1,0:T(8,128)(2,1)} %get-tuple-element.115.refs_1_, bf16[2,2,224,512]{3,2,1,0:T(8,128)(2,1)} %copy-done, ...), custom_call_target="tpu_custom_call" | custom-call | flops 4462739456 | bytes 13230080 | tf_op jit(solution)/shard_map/weight_grad/pallas_call | solution.py:513
  385.8 9.8 %weight_grad.5 = (f32[112,2432]{1,0:T(8,128)}, f32[112,2432]{1,0:T(8,128)}, bf16[112,2432]{1,0:T(8,128)(2,1)}, bf16[112,2432]{1,0:T(8,128)(2,1)}) custom-call(bf16[2,2,224,512]{3,2,1,0:T(8,128)(2,1)} %get-tuple-element.114.refs_0_, bf16[2,2,224,512]{3,2,1,0:T(8,128)(2,1)} %get-tuple-element.115.refs_1_, bf16[2,2,224,512]{3,2,1,0:T(8,128)(2,1)} %copy-done, ...), custom_call_target="tpu_custom_call" | custom-call | flops 4462739456 | bytes 13230080 | tf_op jit(solution)/shard_map/weight_grad/pallas_call | solution.py:513
  400.5 10.2 %collective-permute-done.49 = bf16[112,2432]{1,0:T(8,128)(2,1)S(1)} collective-permute-done((bf16[112,2432]{1,0:T(8,128)(2,1)}, bf16[112,2432]{1,0:T(8,128)(2,1)S(1)}, u32[]{:S(2)}, u32[]{:S(2)}) %collective-permute-start.49) | collective-permute-done | bytes 544800 | tf_op jit(solution)/shard_map/ppermute | solution.py:656
  412.2 10.2 %collective-permute-done.45 = bf16[112,2432]{1,0:T(8,128)(2,1)S(1)} collective-permute-done((bf16[112,2432]{1,0:T(8,128)(2,1)}, bf16[112,2432]{1,0:T(8,128)(2,1)S(1)}, u32[]{:S(2)}, u32[]{:S(2)}) %collective-permute-start.45) | collective-permute-done | bytes 544800 | tf_op jit(solution)/shard_map/ppermute | solution.py:656
  423.9 10.2 %collective-permute-done.57 = bf16[112,2432]{1,0:T(8,128)(2,1)S(1)} collective-permute-done((bf16[112,2432]{1,0:T(8,128)(2,1)}, bf16[112,2432]{1,0:T(8,128)(2,1)S(1)}, u32[]{:S(2)}, u32[]{:S(2)}) %collective-permute-start.57) | collective-permute-done | bytes 544800 | tf_op jit(solution)/shard_map/ppermute | solution.py:656
  435.8 9.0 %collective-permute-done.53 = bf16[112,2432]{1,0:T(8,128)(2,1)S(1)} collective-permute-done((bf16[112,2432]{1,0:T(8,128)(2,1)}, bf16[112,2432]{1,0:T(8,128)(2,1)S(1)}, u32[]{:S(2)}, u32[]{:S(2)}) %collective-permute-start.53) | collective-permute-done | bytes 544800 | tf_op jit(solution)/shard_map/ppermute | solution.py:656
  459.7 9.5 %collective-permute-done.54 = bf16[112,2432]{1,0:T(8,128)(2,1)S(1)} collective-permute-done((bf16[112,2432]{1,0:T(8,128)(2,1)S(1)}, bf16[112,2432]{1,0:T(8,128)(2,1)S(1)}, u32[]{:S(2)}, u32[]{:S(2)}) %collective-permute-start.54) | collective-permute-done | bytes 544800 | tf_op jit(solution)/shard_map/ppermute | solution.py:686
  478.3 14.1 %collective-permute-done.44 = bf16[112,2432]{1,0:T(8,128)(2,1)S(1)} collective-permute-done((bf16[112,2432]{1,0:T(8,128)(2,1)S(1)}, bf16[112,2432]{1,0:T(8,128)(2,1)S(1)}, u32[]{:S(2)}, u32[]{:S(2)}) %collective-permute-start.44) | collective-permute-done | bytes 544800 | tf_op jit(solution)/shard_map/ppermute | solution.py:693
  493.8 10.3 %collective-permute-done.40 = bf16[112,2432]{1,0:T(8,128)(2,1)S(1)} collective-permute-done((bf16[112,2432]{1,0:T(8,128)(2,1)S(1)}, bf16[112,2432]{1,0:T(8,128)(2,1)S(1)}, u32[]{:S(2)}, u32[]{:S(2)}) %collective-permute-start.40) | collective-permute-done | bytes 544800 | tf_op jit(solution)/shard_map/ppermute | solution.py:693
  504.2 11.6 %collective-permute-done.52 = bf16[112,2432]{1,0:T(8,128)(2,1)S(1)} collective-permute-done((bf16[112,2432]{1,0:T(8,128)(2,1)S(1)}, bf16[112,2432]{1,0:T(8,128)(2,1)S(1)}, u32[]{:S(2)}, u32[]{:S(2)}) %collective-permute-start.52) | collective-permute-done | bytes 544800 | tf_op jit(solution)/shard_map/ppermute | solution.py:693
  515.8 11.6 %collective-permute-done.48 = bf16[112,2432]{1,0:T(8,128)(2,1)S(1)} collective-permute-done((bf16[112,2432]{1,0:T(8,128)(2,1)S(1)}, bf16[112,2432]{1,0:T(8,128)(2,1)S(1)}, u32[]{:S(2)}, u32[]{:S(2)}) %collective-permute-start.48) | collective-permute-done | bytes 544800 | tf_op jit(solution)/shard_map/ppermute | solution.py:693
  527.5 11.6 %collective-permute-done.60 = bf16[112,2432]{1,0:T(8,128)(2,1)S(1)} collective-permute-done((bf16[112,2432]{1,0:T(8,128)(2,1)S(1)}, bf16[112,2432]{1,0:T(8,128)(2,1)S(1)}, u32[]{:S(2)}, u32[]{:S(2)}) %collective-permute-start.60) | collective-permute-done | bytes 544800 | tf_op jit(solution)/shard_map/ppermute | solution.py:693
  (277 shorter events, 222.3 us)
Async XLA Ops:
  21.4 33.6 %collective-permute-start.4 = (bf16[448,896]{1,0:T(8,128)(2,1)S(1)}, bf16[448,896]{1,0:T(8,128)(2,1)S(1)}, u32[]{:S(2)}, u32[]{:S(2)}) collective-permute-start(bf16[448,896]{1,0:T(8,128)(2,1)S(1)} %bitcast.54), channel_id=1, source_target_pairs={{0,1},{1,0},{2,3},{3,2},{4,5},{5,4},{6,7},{7,6},{8,9},{9,8},{10,11... | collective-permute-start | bytes 2408456 | tf_op jit(solution)/shard_map/ppermute | solution.py:646
  54.4 29.9 %collective-permute-start.6 = (bf16[512,448]{1,0:T(8,128)(2,1)}, bf16[512,448]{1,0:T(8,128)(2,1)}, u32[]{:S(2)}, u32[]{:S(2)}) collective-permute-start(bf16[512,448]{1,0:T(8,128)(2,1)} %get-tuple-element.76.mine_ref.att_ref.refs_3_), channel_id=1, source_target_pairs={{0,1},{1,0},{2,3},{3,2},{4,5},{5,4},{6,7},{7,6},{8,9},{9,8},{10,11... | collective-permute-start | bytes 1376264 | tf_op jit(solution)/shard_map/ppermute | solution.py:646
  84.2 276.8 %collective-permute-start.35 = (bf16[3,512,2432]{2,1,0:T(8,128)(2,1)}, bf16[3,512,2432]{2,1,0:T(8,128)(2,1)}, u32[]{:S(2)}, u32[]{:S(2)}) collective-permute-start(bf16[3,512,2432]{2,1,0:T(8,128)(2,1)} %get-tuple-element.118.refs_4_), channel_id=1, source_target_pairs={{0,8},{8,0},{16,24},{24,16},{1,9},{9,1},{17,25},{25,17},{2,10},{10... | collective-permute-start | bytes 22413320 | tf_op jit(solution)/shard_map/ppermute | solution.py:650
  112.3 248.7 %collective-permute-start.36 = (bf16[3,512,2432]{2,1,0:T(8,128)(2,1)}, bf16[3,512,2432]{2,1,0:T(8,128)(2,1)}, u32[]{:S(2)}, u32[]{:S(2)}) collective-permute-start(bf16[3,512,2432]{2,1,0:T(8,128)(2,1)} %get-tuple-element.119.refs_5_), channel_id=1, source_target_pairs={{0,8},{8,0},{16,24},{24,16},{1,9},{9,1},{17,25},{25,17},{2,10},{10... | collective-permute-start | bytes 22413320 | tf_op jit(solution)/shard_map/ppermute | solution.py:650
  114.2 44.1 %collective-permute-start.14 = (bf16[896,576]{0,1:T(8,128)(2,1)S(1)}, bf16[896,576]{0,1:T(8,128)(2,1)S(1)}, u32[]{:S(2)}, u32[]{:S(2)}) collective-permute-start(bf16[896,576]{0,1:T(8,128)(2,1)S(1)} %bitcast.47), channel_id=1, source_target_pairs={{0,1},{1,0},{2,3},{3,2},{4,5},{5,4},{6,7},{7,6},{8,9},{9,8},{10,11... | collective-permute-start | bytes 3096584 | tf_op jit(solution)/shard_map/ppermute | solution.py:646
  114.7 62.5 %collective-permute-start.15 = (bf16[512,896]{1,0:T(8,128)(2,1)S(1)}, bf16[512,896]{1,0:T(8,128)(2,1)}, u32[]{:S(2)}, u32[]{:S(2)}) collective-permute-start(bf16[512,896]{1,0:T(8,128)(2,1)S(1)} %copy-done.35), channel_id=1, source_target_pairs={{0,1},{1,0},{2,3},{3,2},{4,5},{5,4},{6,7},{7,6},{8,9},{9,8},{10,11... | collective-permute-start | bytes 2752520 | tf_op jit(solution)/shard_map/ppermute | solution.py:646
  149.9 41.8 %collective-permute-start.10 = (bf16[512,128]{1,0:T(8,128)(2,1)}, bf16[512,128]{1,0:T(8,128)(2,1)S(1)}, u32[]{:S(2)}, u32[]{:S(2)}) collective-permute-start(bf16[512,128]{1,0:T(8,128)(2,1)} %get-tuple-element.83), channel_id=1, source_target_pairs={{2,0},{4,2},{6,4},{3,1},{5,3},{7,5},{10,8},{12,10},{14,12},{11,9},... | collective-permute-start | bytes 393224 | tf_op jit(solution)/shard_map/ppermute | solution.py:666
  158.2 34.8 %collective-permute-start.11 = (bf16[512,128]{1,0:T(8,128)(2,1)}, bf16[512,128]{1,0:T(8,128)(2,1)S(1)}, u32[]{:S(2)}, u32[]{:S(2)}) collective-permute-start(bf16[512,128]{1,0:T(8,128)(2,1)} %get-tuple-element.84), channel_id=1, source_target_pairs={{4,0},{6,2},{5,1},{7,3},{12,8},{14,10},{13,9},{15,11},{20,16},{22,... | collective-permute-start | bytes 393224 | tf_op jit(solution)/shard_map/ppermute | solution.py:666
  193.1 45.1 %collective-permute-start.7 = (bf16[512,896]{1,0:T(8,128)(2,1)S(1)}, bf16[512,896]{1,0:T(8,128)(2,1)S(1)}, u32[]{:S(2)}, u32[]{:S(2)}) collective-permute-start(bf16[512,896]{1,0:T(8,128)(2,1)S(1)} %copy-done.14), channel_id=1, source_target_pairs={{0,1},{1,0},{2,3},{3,2},{4,5},{5,4},{6,7},{7,6},{8,9},{9,8},{10,11... | collective-permute-start | bytes 2752520 | tf_op jit(solution)/shard_map/ppermute | solution.py:646
  206.4 36.6 %collective-permute-start.5 = (bf16[512,896]{1,0:T(8,128)(2,1)S(1)}, bf16[512,896]{1,0:T(8,128)(2,1)S(1)}, u32[]{:S(2)}, u32[]{:S(2)}) collective-permute-start(bf16[512,896]{1,0:T(8,128)(2,1)S(1)} %copy-done.12), channel_id=1, source_target_pairs={{0,1},{1,0},{2,3},{3,2},{4,5},{5,4},{6,7},{7,6},{8,9},{9,8},{10,11... | collective-permute-start | bytes 2752520 | tf_op jit(solution)/shard_map/ppermute | solution.py:646
  234.1 46.1 %collective-permute-start.25 = (f32[2,2,224,448]{3,2,1,0:T(8,128)}, f32[2,2,224,448]{3,2,1,0:T(8,128)}, u32[]{:S(2)}, u32[]{:S(2)}) collective-permute-start(f32[2,2,224,448]{3,2,1,0:T(8,128)} %get-tuple-element.111), channel_id=1, source_target_pairs={{0,8},{8,0},{16,24},{24,16},{1,9},{9,1},{17,25},{25,17},{2,10},{10... | collective-permute-start | bytes 4816904 | tf_op jit(solution)/shard_map/ppermute | solution.py:650
  297.1 63.8 %collective-permute-start.33 = (bf16[2,2,224,512]{3,2,1,0:T(8,128)(2,1)S(1)}, bf16[2,2,224,512]{3,2,1,0:T(8,128)(2,1)S(1)}, u32[]{:S(2)}, u32[]{:S(2)}) collective-permute-start(bf16[2,2,224,512]{3,2,1,0:T(8,128)(2,1)S(1)} %copy-done.34), channel_id=1, source_target_pairs={{0,8},{8,0},{16,24},{24,16},{1,9},{9,1},{17,25},{25,17},{2,10},{10... | collective-permute-start | bytes 2752520 | tf_op jit(solution)/shard_map/ppermute | solution.py:650
  372.2 26.8 %collective-permute-start.37 = (bf16[112,2432]{1,0:T(8,128)(2,1)}, bf16[112,2432]{1,0:T(8,128)(2,1)S(1)}, u32[]{:S(2)}, u32[]{:S(2)}) collective-permute-start(bf16[112,2432]{1,0:T(8,128)(2,1)} %get-tuple-element.121), channel_id=1, source_target_pairs={{0,16},{8,24},{16,0},{24,8},{1,17},{9,25},{17,1},{25,9},{2,18},{10... | collective-permute-start | bytes 1634312 | tf_op jit(solution)/shard_map/ppermute | solution.py:656
  383.7 27.1 %collective-permute-start.49 = (bf16[112,2432]{1,0:T(8,128)(2,1)}, bf16[112,2432]{1,0:T(8,128)(2,1)S(1)}, u32[]{:S(2)}, u32[]{:S(2)}) collective-permute-start(bf16[112,2432]{1,0:T(8,128)(2,1)} %get-tuple-element.127), channel_id=1, source_target_pairs={{0,16},{8,24},{16,0},{24,8},{1,17},{9,25},{17,1},{25,9},{2,18},{10... | collective-permute-start | bytes 1634312 | tf_op jit(solution)/shard_map/ppermute | solution.py:656
  384.0 38.4 %collective-permute-start.45 = (bf16[112,2432]{1,0:T(8,128)(2,1)}, bf16[112,2432]{1,0:T(8,128)(2,1)S(1)}, u32[]{:S(2)}, u32[]{:S(2)}) collective-permute-start(bf16[112,2432]{1,0:T(8,128)(2,1)} %get-tuple-element.125), channel_id=1, source_target_pairs={{0,16},{8,24},{16,0},{24,8},{1,17},{9,25},{17,1},{25,9},{2,18},{10... | collective-permute-start | bytes 1634312 | tf_op jit(solution)/shard_map/ppermute | solution.py:656
  395.6 38.5 %collective-permute-start.57 = (bf16[112,2432]{1,0:T(8,128)(2,1)}, bf16[112,2432]{1,0:T(8,128)(2,1)S(1)}, u32[]{:S(2)}, u32[]{:S(2)}) collective-permute-start(bf16[112,2432]{1,0:T(8,128)(2,1)} %get-tuple-element.131), channel_id=1, source_target_pairs={{0,16},{8,24},{16,0},{24,8},{1,17},{9,25},{17,1},{25,9},{2,18},{10... | collective-permute-start | bytes 1634312 | tf_op jit(solution)/shard_map/ppermute | solution.py:656
  395.9 48.9 %collective-permute-start.53 = (bf16[112,2432]{1,0:T(8,128)(2,1)}, bf16[112,2432]{1,0:T(8,128)(2,1)S(1)}, u32[]{:S(2)}, u32[]{:S(2)}) collective-permute-start(bf16[112,2432]{1,0:T(8,128)(2,1)} %get-tuple-element.129), channel_id=1, source_target_pairs={{0,16},{8,24},{16,0},{24,8},{1,17},{9,25},{17,1},{25,9},{2,18},{10... | collective-permute-start | bytes 1634312 | tf_op jit(solution)/shard_map/ppermute | solution.py:656
  399.1 47.2 %collective-permute-start.42 = (bf16[112,2432]{1,0:T(8,128)(2,1)S(1)}, bf16[112,2432]{1,0:T(8,128)(2,1)S(1)}, u32[]{:S(2)}, u32[]{:S(2)}) collective-permute-start(bf16[112,2432]{1,0:T(8,128)(2,1)S(1)} %fusion.5), channel_id=1, source_target_pairs={{0,2},{6,4},{1,3},{7,5},{8,10},{14,12},{9,11},{15,13},{16,18},{22,... | collective-permute-start | bytes 1634312 | tf_op jit(solution)/shard_map/ppermute | solution.py:686
  410.7 37.1 %collective-permute-start.38 = (bf16[112,2432]{1,0:T(8,128)(2,1)S(1)}, bf16[112,2432]{1,0:T(8,128)(2,1)S(1)}, u32[]{:S(2)}, u32[]{:S(2)}) collective-permute-start(bf16[112,2432]{1,0:T(8,128)(2,1)S(1)} %fusion.4), channel_id=1, source_target_pairs={{0,2},{6,4},{1,3},{7,5},{8,10},{14,12},{9,11},{15,13},{16,18},{22,... | collective-permute-start | bytes 1634312 | tf_op jit(solution)/shard_map/ppermute | solution.py:686
  472.5 31.6 %collective-permute-start.40 = (bf16[112,2432]{1,0:T(8,128)(2,1)S(1)}, bf16[112,2432]{1,0:T(8,128)(2,1)S(1)}, u32[]{:S(2)}, u32[]{:S(2)}) collective-permute-start(bf16[112,2432]{1,0:T(8,128)(2,1)S(1)} %add_convert_fusion.12), channel_id=1, source_target_pairs={{2,0},{4,6},{3,1},{5,7},{10,8},{12,14},{11,9},{13,15},{18,16},{20,... | collective-permute-start | bytes 1634312 | tf_op jit(solution)/shard_map/ppermute | solution.py:693
  473.9 41.8 %collective-permute-start.52 = (bf16[112,2432]{1,0:T(8,128)(2,1)S(1)}, bf16[112,2432]{1,0:T(8,128)(2,1)S(1)}, u32[]{:S(2)}, u32[]{:S(2)}) collective-permute-start(bf16[112,2432]{1,0:T(8,128)(2,1)S(1)} %add_convert_fusion.6), channel_id=1, source_target_pairs={{2,0},{4,6},{3,1},{5,7},{10,8},{12,14},{11,9},{13,15},{18,16},{20,... | collective-permute-start | bytes 1634312 | tf_op jit(solution)/shard_map/ppermute | solution.py:693
  475.4 52.1 %collective-permute-start.48 = (bf16[112,2432]{1,0:T(8,128)(2,1)S(1)}, bf16[112,2432]{1,0:T(8,128)(2,1)S(1)}, u32[]{:S(2)}, u32[]{:S(2)}) collective-permute-start(bf16[112,2432]{1,0:T(8,128)(2,1)S(1)} %add_convert_fusion.8), channel_id=1, source_target_pairs={{2,0},{4,6},{3,1},{5,7},{10,8},{12,14},{11,9},{13,15},{18,16},{20,... | collective-permute-start | bytes 1634312 | tf_op jit(solution)/shard_map/ppermute | solution.py:693
  476.8 62.3 %collective-permute-start.60 = (bf16[112,2432]{1,0:T(8,128)(2,1)S(1)}, bf16[112,2432]{1,0:T(8,128)(2,1)S(1)}, u32[]{:S(2)}, u32[]{:S(2)}) collective-permute-start(bf16[112,2432]{1,0:T(8,128)(2,1)S(1)} %add_convert_fusion.2), channel_id=1, source_target_pairs={{2,0},{4,6},{3,1},{5,7},{10,8},{12,14},{11,9},{13,15},{18,16},{20,... | collective-permute-start | bytes 1634312 | tf_op jit(solution)/shard_map/ppermute | solution.py:693
  492.4 56.0 %collective-permute-start.56 = (bf16[112,2432]{1,0:T(8,128)(2,1)S(1)}, bf16[112,2432]{1,0:T(8,128)(2,1)S(1)}, u32[]{:S(2)}, u32[]{:S(2)}) collective-permute-start(bf16[112,2432]{1,0:T(8,128)(2,1)S(1)} %add_convert_fusion.4), channel_id=1, source_target_pairs={{2,0},{4,6},{3,1},{5,7},{10,8},{12,14},{11,9},{13,15},{18,16},{20,... | collective-permute-start | bytes 1634312 | tf_op jit(solution)/shard_map/ppermute | solution.py:693
  (82 other events, 1054.7 us)
